TPU v7x, 16 devices: a whole 2x2x2 slice. The times are simulated.
16 devices in a mesh: dp: 2 (over z), tp: 8 (over y, x, core).
Axes of the slice: x: 2, y: 2, z: 2, core: 2. Of those that a mesh axis runs over, the one named last changes fastest.
Arguments:
- x_in: bfloat16 [3, 2, 8, 512, 2048], P(None, None, 'dp')
- u_pre: bfloat16 [3, 2, 8, 512, 8192], P(None, None, 'dp', None, 'tp')
- w_up: bfloat16 [3, 2048, 8192], P(None, None, 'tp')
- w_down: bfloat16 [3, 8192, 2048], P(None, 'tp')
- d_out: bfloat16 [2, 8, 512, 2048], P(None, 'dp')
- noise_up: float32 [3, 2048, 8192], P(None, 'dp', 'tp')
- noise_down: float32 [3, 8192, 2048], P(None, 'tp', 'dp')
- clip_norm: float32 [1], replicated
- noise_mult: float32 [1], replicated
Outputs:
- output 1: float32 [3, 2048, 8192], P(None, 'dp', 'tp')
- output 2: float32 [3, 8192, 2048], P(None, 'tp', 'dp')
- output 3: bfloat16 [2, 8, 512, 2048], P(None, 'dp')
All inputs are finite; a program needn't handle non-finite values.
Results may differ from a plain program's by a relative error of at most 0.0169904.
Values are sent between devices in bfloat16 or wider.
A program may use at most 1 GiB of HBM per device.

v0:
```python
import functools
import math

import jax
import jax.numpy as jnp
from jax import lax
from jax.experimental import pallas as pl
from jax.experimental.pallas import tpu as pltpu
from jax.sharding import PartitionSpec as P


PIECE = 256
HALF = 1024
PER_CHUNK = 2
TANH_SCALE = math.sqrt(2.0 / math.pi)
TANH_CUBE = 0.044715

NT = (((1,), (1,)), ((), ()))
TN = (((0,), (0,)), ((), ()))


def dot(lhs, rhs, dims):
    return lax.dot_general(lhs, rhs, dims, preferred_element_type=jnp.float32)


def piece_of(me, r1, r2, rc, x_first):
    bits = (r2 * 4 + r1 * 2 + rc) if x_first else (r1 * 4 + r2 * 2 + rc)
    return me ^ bits


def backward_kernel(layer, micro, first_ex, x_first, from_slots, me_ref, *refs):
    *refs, w1, w2, x_buf, w1_sem, w2_sem, x_sem = refs
    if from_slots:
        own, first, core_own, core_first, norm_in, u_ref, w1_hbm, w2_hbm, x_hbm = refs[:9]
        h_ref, dh_ref, keep_ref, send_ref, norm_ref, dz_ref = refs[9:]
    else:
        dz_in, u_ref, w1_hbm, w2_hbm, x_hbm, h_ref, dh_ref, keep_ref, send_ref, norm_ref, piece_ref = refs
    me = me_ref[0]
    step = pl.program_id(0)
    slots = [(rc, r1, r2) for rc in (1, 0) for r1 in range(2) for r2 in range(2)]
    hid = u_ref.shape[-1]

    def rows_of(rc, r1, r2):
        return pl.ds(pl.multiple_of(piece_of(me, r1, r2, rc, x_first) * PIECE, PIECE), PIECE)

    def w2_copy(i):
        rows = pl.ds(i * (hid // 2), hid // 2)
        return pltpu.make_async_copy(w2_hbm.at[layer, rows, :], w2.at[rows, :], w2_sem.at[i])

    def w1_copy(i):
        return pltpu.make_async_copy(w1_hbm.at[layer, rows_of(*slots[i]), :], w1.at[i], w1_sem.at[i])

    def x_copy():
        return pltpu.make_async_copy(x_hbm.at[layer, micro, first_ex + step], x_buf, x_sem)

    @pl.when(step == 0)
    def _():
        for i in range(2):
            w2_copy(i).start()
        for i in range(8):
            w1_copy(i).start()

    x_copy().start()
    if from_slots:
        for rc, r1, slot in ((0, 0, own), (0, 1, first), (1, 0, core_own), (1, 1, core_first)):
            for r2 in range(2):
                dz_ref[:, rows_of(rc, r1, r2)] = slot[r2]
        cot = dz_ref
    else:
        cot = dz_in
        piece_ref[...] = dz_in[:, pl.ds(pl.multiple_of(me * PIECE, PIECE), PIECE)]
    width = 256
    for j in range(hid // width):
        if j % 2 == 0:

            @pl.when(step == 0)
            def _(j=j):
                w2_copy(j // 2).wait()

        cols = slice(j * width, (j + 1) * width)
        d_act = dot(cot[...], w2[cols, :], NT)
        u = u_ref[:, cols].astype(jnp.float32)
        u_sq = u * u
        t = jnp.tanh(TANH_SCALE * (u + TANH_CUBE * (u_sq * u)))
        cdf = 0.5 * (1.0 + t)
        slope = cdf + (0.5 * TANH_SCALE) * (1.0 - t * t) * (u * (1.0 + (3.0 * TANH_CUBE) * u_sq))
        h_ref[:, cols] = (u * cdf).astype(jnp.bfloat16)
        dh_ref[:, cols] = (slope * d_act).astype(jnp.bfloat16)

    @pl.when(step == 0)
    def _():
        for i in range(8):
            w1_copy(i).wait()

    for i, (rc, r1, r2) in enumerate(slots):
        out = send_ref if rc else keep_ref
        out[r1, r2] = dot(dh_ref[...], w1[i], NT).astype(jnp.bfloat16)

    def gram_product(left, right):
        prod = dot(left[...], left[:256, :], NT) * dot(right[...], right[:256, :], NT)
        corner = dot(left[256:, :], left[256:, :], NT) * dot(right[256:, :], right[256:, :], NT)
        total = prod[:256] + 2.0 * prod[256:] + corner
        return jnp.sum(total.reshape(32, 8, 256), axis=0)

    norm = gram_product(h_ref, cot)
    x_copy().wait()
    norm += gram_product(dh_ref, x_buf)
    norm_ref[...] = norm_in[...] + norm if from_slots else norm


def backward_chunk(layer, micro, first_ex, x_first, me, dz_inputs, norm_in, x_in, u_pre, w_up, w_down):
    rows = PER_CHUNK * 512
    hid, model = u_pre.shape[-1], w_up.shape[1]
    from_slots = isinstance(dz_inputs, tuple)
    norm_spec = pl.BlockSpec((None, 8, 256), lambda e, m: (e, 0, 0))
    piece_spec = pl.BlockSpec((512, PIECE), lambda e, m: (e, 0))
    if from_slots:
        in_specs = [pl.BlockSpec((2, 512, PIECE), lambda e, m: (0, e, 0))] * 4 + [norm_spec]
        operands = (*dz_inputs, norm_in)
    else:
        in_specs = [pl.BlockSpec((None, None, 512, model), lambda e, m: (micro, first_ex + e, 0, 0))]
        operands = (dz_inputs,)
    part_spec = pl.BlockSpec((2, 2, 512, PIECE), lambda e, m: (0, 0, e, 0))
    part_shape = jax.ShapeDtypeStruct((2, 2, rows, PIECE), jnp.bfloat16)
    act_spec = pl.BlockSpec((512, hid), lambda e, m: (e, 0))
    act_shape = jax.ShapeDtypeStruct((rows, hid), jnp.bfloat16)
    last_cols = model if from_slots else PIECE
    any_spec = pl.BlockSpec(memory_space=pl.ANY)
    return pl.pallas_call(
        functools.partial(backward_kernel, layer, micro, first_ex, x_first, from_slots),
        grid_spec=pltpu.PrefetchScalarGridSpec(
            num_scalar_prefetch=1,
            grid=(PER_CHUNK,),
            in_specs=in_specs
            + [pl.BlockSpec((None, None, None, 512, hid), lambda e, m: (layer, micro, first_ex + e, 0, 0))]
            + [any_spec] * 3,
            out_specs=[act_spec, act_spec, part_spec, part_spec, norm_spec]
            + [pl.BlockSpec((512, last_cols), lambda e, m: (e, 0))],
            scratch_shapes=[
                pltpu.VMEM((8, PIECE, hid), jnp.bfloat16),
                pltpu.VMEM((hid, model), jnp.bfloat16),
                pltpu.VMEM((512, model), jnp.bfloat16),
                pltpu.SemaphoreType.DMA((8,)),
                pltpu.SemaphoreType.DMA((2,)),
                pltpu.SemaphoreType.DMA,
            ],
        ),
        out_shape=[act_shape, act_shape, part_shape, part_shape]
        + [jax.ShapeDtypeStruct((PER_CHUNK, 8, 256), jnp.float32), jax.ShapeDtypeStruct((rows, last_cols), jnp.bfloat16)],
        compiler_params=pltpu.CompilerParams(dimension_semantics=("arbitrary",)),
        cost_estimate=pl.CostEstimate(flops=6 * rows * hid * model, bytes_accessed=24 << 20, transcendentals=rows * hid),
    )(me, *operands, u_pre, w_up, w_down, x_in)


def grad_kernel(up, n_chunks, with_noise, half_ref, clip_ref, *refs):
    if with_noise:
        scale_ref, refs = refs[0], refs[1:]
    lhs, rhs = refs[:-1][: (1 if up else n_chunks)], refs[:-1][(1 if up else n_chunks) :]
    if with_noise:
        noise_ref, rhs = rhs[-1], rhs[:-1]
    out_ref = refs[-1]
    step = pl.program_id(0)

    @pl.when(step == 0)
    def _():
        out_ref[...] = scale_ref[0] * noise_ref[...] if with_noise else jnp.zeros_like(out_ref)

    clip = clip_ref[step]
    for k in range(n_chunks):

        @pl.when(step // PER_CHUNK == k)
        def _(k=k):
            a = lhs[min(k, len(lhs) - 1)]
            b = rhs[min(k, len(rhs) - 1)]
            scaled = (b[...].astype(jnp.float32) * clip).astype(jnp.bfloat16)
            for j in range(2):
                cols = slice(j * 512, (j + 1) * 512)
                out_ref[:, cols] += dot(a[...], scaled[:, cols], TN)


def weight_grad(up, layer, half, clip, lhs, rhs, noise=None, noise_scale=None):
    n_chunks = len(lhs) if not up else len(rhs)
    n_ex = n_chunks * PER_CHUNK

    def chunk_row(k):
        return lambda s, h: (jnp.clip(s - PER_CHUNK * k, 0, PER_CHUNK - 1), 0)

    def chunk_half(k):
        return lambda s, h: (jnp.clip(s - PER_CHUNK * k, 0, PER_CHUNK - 1), h[0])

    if up:
        lhs_specs = [pl.BlockSpec((None, None, None, 512, HALF), lambda s, h: (layer, s // 4, s % 4, 0, h[0]))]
        rhs_specs = [pl.BlockSpec((512, 1024), chunk_row(k)) for k in range(n_chunks)]
        lhs = (lhs,)
    else:
        lhs_specs = [pl.BlockSpec((512, 1024), chunk_row(k)) for k in range(n_chunks)]
        if isinstance(rhs, tuple):
            rhs_specs = [pl.BlockSpec((512, HALF), chunk_half(k)) for k in range(n_chunks)]
        else:
            rhs_specs = [pl.BlockSpec((None, None, 512, HALF), lambda s, h: (s // 4, s % 4, 0, h[0]))]
            rhs = (rhs,)
    extra, extra_specs, lead, lead_specs = (), [], (), []
    if noise is not None:
        extra = (noise,)
        extra_specs = [pl.BlockSpec((None, 1024, 1024), lambda s, h: (layer, 0, 0))]
        lead = (noise_scale,)
        lead_specs = [pl.BlockSpec(memory_space=pltpu.SMEM)]
    return pl.pallas_call(
        functools.partial(grad_kernel, up, n_chunks, noise is not None),
        grid_spec=pltpu.PrefetchScalarGridSpec(
            num_scalar_prefetch=1,
            grid=(n_ex,),
            in_specs=[pl.BlockSpec(memory_space=pltpu.SMEM)] + lead_specs + lhs_specs + rhs_specs + extra_specs,
            out_specs=pl.BlockSpec((1024, 1024), lambda s, h: (0, 0)),
        ),
        out_shape=jax.ShapeDtypeStruct((1024, 1024), jnp.float32),
        compiler_params=pltpu.CompilerParams(dimension_semantics=("arbitrary",)),
        cost_estimate=pl.CostEstimate(flops=2 * n_ex * 512 * 1024 * 1024, bytes_accessed=24 << 20, transcendentals=0),
    )(half, clip, *lead, *lhs, *rhs, *extra)


def finish_kernel(inv, own_ref, got_ref, *refs):
    refs[-1][...] = (own_ref[...] + got_ref[...]) * inv


def finish_grad(layer, n_layers, examples, own, got, buffer):
    spec = pl.BlockSpec((256, 1024), lambda i: (i, 0))
    operands, in_specs, aliases = (own, got), [spec, spec], {}
    if buffer is not None:
        operands, in_specs, aliases = (own, got, buffer), [spec, spec, pl.BlockSpec(memory_space=pl.ANY)], {2: 0}
    return pl.pallas_call(
        functools.partial(finish_kernel, 1.0 / examples),
        grid=(4,),
        in_specs=in_specs,
        out_specs=pl.BlockSpec((None, 256, 1024), lambda i: (layer, i, 0)),
        out_shape=jax.ShapeDtypeStruct((n_layers, 1024, 1024), jnp.float32),
        input_output_aliases=aliases,
        compiler_params=pltpu.CompilerParams(dimension_semantics=("arbitrary",)),
        cost_estimate=pl.CostEstimate(flops=12 << 20, bytes_accessed=12 << 20, transcendentals=0),
    )(*operands)


def join_kernel(orders, me_ref, *refs):
    out_ref = refs[-1]
    step = pl.program_id(0)
    for k, x_first in enumerate(orders):

        @pl.when(step // PER_CHUNK == k)
        def _(k=k, x_first=x_first):
            own, first, core_own, core_first = refs[4 * k : 4 * k + 4]
            for rc, r1, slots in ((0, 0, own), (0, 1, first), (1, 0, core_own), (1, 1, core_first)):
                for r2 in range(2):
                    start = pl.multiple_of(piece_of(me_ref[0], r1, r2, rc, x_first) * PIECE, PIECE)
                    out_ref[:, pl.ds(start, PIECE)] = slots[r2]


def join_slots(me, orders, chunks, shape):
    def spec(k):
        return pl.BlockSpec((2, 512, PIECE), lambda s, m: (0, jnp.clip(s - PER_CHUNK * k, 0, PER_CHUNK - 1), 0))

    return pl.pallas_call(
        functools.partial(join_kernel, orders),
        grid_spec=pltpu.PrefetchScalarGridSpec(
            num_scalar_prefetch=1,
            grid=(len(orders) * PER_CHUNK,),
            in_specs=[spec(k) for k in range(len(orders)) for _ in range(4)],
            out_specs=pl.BlockSpec((None, None, 512, shape[-1]), lambda s, m: (s // 4, s % 4, 0, 0)),
        ),
        out_shape=jax.ShapeDtypeStruct(shape, jnp.bfloat16),
        compiler_params=pltpu.CompilerParams(dimension_semantics=("arbitrary",)),
        cost_estimate=pl.CostEstimate(flops=32 << 20, bytes_accessed=32 << 20, transcendentals=0),
        name="join_d_in",
    )(me, *[s for chunk in chunks for s in chunk])


def solution(mesh):
    dp_size, tp_size = mesh.shape["dp"], mesh.shape["tp"]
    CORE, X, Y = 1, 2, 4

    def swap(value, mask):
        return lax.ppermute(value, "tp", [(i, i ^ mask) for i in range(tp_size)])

    def add(a, b):
        return (a.astype(jnp.float32) + b.astype(jnp.float32)).astype(jnp.bfloat16)

    def sum_over_tp(keep, send, cot_piece, x_first):
        one, two = (X, Y) if x_first else (Y, X)
        got = swap(send, CORE)
        away, kept = add(keep[1], got[1]), add(keep[0], got[0])
        got = swap(away, one)
        away = add(kept[1], got[1])
        last = swap(away, two)
        mine = add(kept[0], got[0]).astype(jnp.float32) + last.astype(jnp.float32)
        piece = (cot_piece.astype(jnp.float32) + mine).astype(jnp.bfloat16)
        other = swap(piece, two)
        own = jnp.stack([piece, other])
        first = swap(own, one)
        core_own = swap(own, CORE)
        core_first = swap(first, CORE)
        return piece, (own, first, core_own, core_first)

    def local_pass(x_in, u_pre, w_up, w_down, d_out, noise_up, noise_down, clip_norm, noise_mult):
        n_layers = x_in.shape[0]
        micro, per_micro = d_out.shape[:2]
        examples = micro * per_micro * dp_size
        me = lax.axis_index("tp").astype(jnp.int32)
        my_dp = lax.axis_index("dp").astype(jnp.int32)
        me_arr = me.reshape(1)
        chunks = [(m, e) for m in range(micro) for e in range(0, per_micro, PER_CHUNK)]
        orders = [k % 2 == 0 for k in range(len(chunks))]
        cots = [d_out] * len(chunks)
        pieces = [None] * len(chunks)
        norms = [None] * len(chunks)
        saved = [None] * n_layers
        for layer in reversed(range(n_layers)):
            top = layer == n_layers - 1
            hids, dhids, full = [], [], []
            for k, (m, e) in enumerate(chunks):
                hidden, d_hid, keep, send, norms[k], cot = backward_chunk(
                    layer, m, e, orders[k], me_arr, cots[k], norms[k], x_in, u_pre, w_up, w_down
                )
                pieces[k], cots[k] = sum_over_tp(keep, send, cot if top else pieces[k], orders[k])
                hids.append(hidden)
                dhids.append(d_hid)
                full.append(cot)
            saved[layer] = (tuple(hids), tuple(dhids), d_out if top else tuple(full))
        d_in = join_slots(me_arr, orders, cots, d_out.shape)
        norm_vec = lax.psum(jnp.sum(jnp.concatenate(norms), axis=(1, 2)), "tp")
        clip = jnp.minimum(1.0, clip_norm[0] / jnp.sqrt(norm_vec))
        noise_scale = (noise_mult[0] * clip_norm[0]).reshape(1)
        own_half, other_half = my_dp.reshape(1), (1 - my_dp).reshape(1)
        swap_dp = [(i, 1 - i) for i in range(dp_size)]
        grads = [(up, layer) for layer in reversed(range(n_layers)) for up in (True, False)]

        def grad(up, layer, *rest):
            hids, dhids, full = saved[layer]
            lhs, rhs = (x_in, dhids) if up else (hids, full)
            return weight_grad(up, layer, rest[0], clip, lhs, rhs, *rest[1:])

        got = []
        for up, layer in grads:
            part = grad(up, layer, other_half)
            got.append(lax.ppermute(part, "dp", swap_dp))
        result = [None, None]
        for i, (up, layer) in enumerate(grads):
            own = grad(up, layer, own_half, noise_up if up else noise_down, noise_scale)
            if i == len(grads) - 1:
                own, d_in = lax.optimization_barrier((own, d_in))
            result[up] = finish_grad(layer, n_layers, examples, own, got[i], result[up])
        return result[1], result[0], d_in

    in_specs = (P(None, None, "dp", None, None), P(None, None, "dp", None, "tp"), P(None, None, "tp"), P(None, "tp", None), P(None, "dp", None, None), P(None, "dp", "tp"), P(None, "tp", "dp"), P(), P())
    out_specs = (P(None, "dp", "tp"), P(None, "tp", "dp"), P(None, "dp", None, None))
    return jax.shard_map(local_pass, mesh=mesh, in_specs=in_specs, out_specs=out_specs, check_vma=False)
```

profile of v0, /device:TPU:0, one launch (start us, length us, event | category | flops | bytes accessed | tf_op | source)
XLA Modules:
  0.0 1205.6 jit_solution(7691221031610658403)
XLA Ops:
  0.6 23.8 %shard_map.112 = (bf16[1024,1024]{1,0:T(8,128)(2,1)}, bf16[1024,1024]{1,0:T(8,128)(2,1)}, bf16[2,2,1024,256]{3,2,1,0:T(8,128)(2,1)}, bf16[2,2,1024,256]{3,2,1,0:...) custom-call(s32[1]{0:T(128)} %bitcast.2.me_ref, bf16[2,4,512,2048]{3,2,1,0:T(8,128)(2,1)} %refs_4_.9, ...), custom_call_target="tpu_custom_call" | custom-call | flops 12884901888 | bytes 25165824 | tf_op jit(solution)/shard_map/pallas_call | solution.py:129
  25.2 24.1 %shard_map.115 = (bf16[1024,1024]{1,0:T(8,128)(2,1)}, bf16[1024,1024]{1,0:T(8,128)(2,1)}, bf16[2,2,1024,256]{3,2,1,0:T(8,128)(2,1)}, bf16[2,2,1024,256]{3,2,1,0:...) custom-call(s32[1]{0:T(128)} %bitcast.2.me_ref, bf16[2,4,512,2048]{3,2,1,0:T(8,128)(2,1)} %refs_4_.9, ...), custom_call_target="tpu_custom_call" | custom-call | flops 12884901888 | bytes 25165824 | tf_op jit(solution)/shard_map/pallas_call | solution.py:129
  49.4 24.4 %shard_map.118 = (bf16[1024,1024]{1,0:T(8,128)(2,1)}, bf16[1024,1024]{1,0:T(8,128)(2,1)}, bf16[2,2,1024,256]{3,2,1,0:T(8,128)(2,1)}, bf16[2,2,1024,256]{3,2,1,0:...) custom-call(s32[1]{0:T(128)} %bitcast.2.me_ref, bf16[2,4,512,2048]{3,2,1,0:T(8,128)(2,1)} %refs_4_.9, ...), custom_call_target="tpu_custom_call" | custom-call | flops 12884901888 | bytes 25165824 | tf_op jit(solution)/shard_map/pallas_call | solution.py:129
  81.8 24.0 %shard_map.121 = (bf16[1024,1024]{1,0:T(8,128)(2,1)}, bf16[1024,1024]{1,0:T(8,128)(2,1)}, bf16[2,2,1024,256]{3,2,1,0:T(8,128)(2,1)}, bf16[2,2,1024,256]{3,2,1,0:...) custom-call(s32[1]{0:T(128)} %bitcast.2.me_ref, bf16[2,4,512,2048]{3,2,1,0:T(8,128)(2,1)} %refs_4_.9, ...), custom_call_target="tpu_custom_call" | custom-call | flops 12884901888 | bytes 25165824 | tf_op jit(solution)/shard_map/pallas_call | solution.py:129
  113.6 21.3 %collective-permute-done.15 = bf16[2,1024,256]{2,1,0:T(8,128)(2,1)S(1)} collective-permute-done((bf16[2,1024,256]{2,1,0:T(8,128)(2,1)S(1)}, bf16[2,1024,256]{2,1,0:T(8,128)(2,1)S(1)}, u32[]{:S(2)}, u32[]{:S(2)}) %collective-permute-start.15) | collective-permute-done | bytes 1048608 | tf_op jit(solution)/shard_map/ppermute | solution.py:281
  164.8 18.3 %collective-permute-done.43 = bf16[2,1024,256]{2,1,0:T(8,128)(2,1)S(1)} collective-permute-done((bf16[2,1024,256]{2,1,0:T(8,128)(2,1)S(1)}, bf16[2,1024,256]{2,1,0:T(8,128)(2,1)S(1)}, u32[]{:S(2)}, u32[]{:S(2)}) %collective-permute-start.43) | collective-permute-done | bytes 1048608 | tf_op jit(solution)/shard_map/ppermute | solution.py:281
  206.8 21.3 %collective-permute-done.31 = bf16[1024,256]{1,0:T(8,128)(2,1)S(1)} collective-permute-done((bf16[1024,256]{1,0:T(8,128)(2,1)S(1)}, bf16[1024,256]{1,0:T(8,128)(2,1)S(1)}, u32[]{:S(2)}, u32[]{:S(2)}) %collective-permute-start.31) | collective-permute-done | bytes 524320 | tf_op jit(solution)/shard_map/ppermute | solution.py:281
  233.5 25.0 %shard_map.113 = (bf16[1024,1024]{1,0:T(8,128)(2,1)}, bf16[1024,1024]{1,0:T(8,128)(2,1)}, bf16[2,2,1024,256]{3,2,1,0:T(8,128)(2,1)}, bf16[2,2,1024,256]{3,2,1,0:...) custom-call(s32[1]{0:T(128)} %bitcast.2.me_ref, bf16[2,1024,256]{2,1,0:T(8,128)(2,1)} %copy-done.9, ...), custom_call_target="tpu_custom_call" | custom-call | flops 12884901888 | bytes 25165824 | tf_op jit(solution)/shard_map/pallas_call | solution.py:129
  260.2 25.0 %shard_map.116 = (bf16[1024,1024]{1,0:T(8,128)(2,1)}, bf16[1024,1024]{1,0:T(8,128)(2,1)}, bf16[2,2,1024,256]{3,2,1,0:T(8,128)(2,1)}, bf16[2,2,1024,256]{3,2,1,0:...) custom-call(s32[1]{0:T(128)} %bitcast.2.me_ref, bf16[2,1024,256]{2,1,0:T(8,128)(2,1)} %pad_maximum_fusion.2.refs_0_, ...), custom_call_target="tpu_custom_call" | custom-call | flops 12884901888 | bytes 25165824 | tf_op jit(solution)/shard_map/pallas_call | solution.py:129
  285.6 25.2 %shard_map.119 = (bf16[1024,1024]{1,0:T(8,128)(2,1)}, bf16[1024,1024]{1,0:T(8,128)(2,1)}, bf16[2,2,1024,256]{3,2,1,0:T(8,128)(2,1)}, bf16[2,2,1024,256]{3,2,1,0:...) custom-call(s32[1]{0:T(128)} %bitcast.2.me_ref, bf16[2,1024,256]{2,1,0:T(8,128)(2,1)} %pad_maximum_fusion.4.refs_0_, ...), custom_call_target="tpu_custom_call" | custom-call | flops 12884901888 | bytes 25165824 | tf_op jit(solution)/shard_map/pallas_call | solution.py:129
  316.0 25.0 %shard_map.122 = (bf16[1024,1024]{1,0:T(8,128)(2,1)}, bf16[1024,1024]{1,0:T(8,128)(2,1)}, bf16[2,2,1024,256]{3,2,1,0:T(8,128)(2,1)}, bf16[2,2,1024,256]{3,2,1,0:...) custom-call(s32[1]{0:T(128)} %bitcast.2.me_ref, bf16[2,1024,256]{2,1,0:T(8,128)(2,1)} %pad_maximum_fusion.6.refs_0_, ...), custom_call_target="tpu_custom_call" | custom-call | flops 12884901888 | bytes 25165824 | tf_op jit(solution)/shard_map/pallas_call | solution.py:129
  350.0 20.1 %collective-permute-done.22 = bf16[2,1024,256]{2,1,0:T(8,128)(2,1)S(1)} collective-permute-done((bf16[2,1024,256]{2,1,0:T(8,128)(2,1)S(1)}, bf16[2,1024,256]{2,1,0:T(8,128)(2,1)S(1)}, u32[]{:S(2)}, u32[]{:S(2)}) %collective-permute-start.22) | collective-permute-done | bytes 1048608 | tf_op jit(solution)/shard_map/ppermute | solution.py:281
  400.5 18.8 %collective-permute-done.50 = bf16[2,1024,256]{2,1,0:T(8,128)(2,1)S(1)} collective-permute-done((bf16[2,1024,256]{2,1,0:T(8,128)(2,1)S(1)}, bf16[2,1024,256]{2,1,0:T(8,128)(2,1)S(1)}, u32[]{:S(2)}, u32[]{:S(2)}) %collective-permute-start.50) | collective-permute-done | bytes 1048608 | tf_op jit(solution)/shard_map/ppermute | solution.py:281
  444.1 20.3 %collective-permute-done.38 = bf16[1024,256]{1,0:T(8,128)(2,1)} collective-permute-done((bf16[1024,256]{1,0:T(8,128)(2,1)S(1)}, bf16[1024,256]{1,0:T(8,128)(2,1)}, u32[]{:S(2)}, u32[]{:S(2)}) %collective-permute-start.38) | collective-permute-done | bytes 524320 | tf_op jit(solution)/shard_map/ppermute | solution.py:281
  469.0 25.0 %shard_map.114 = (bf16[1024,1024]{1,0:T(8,128)(2,1)}, bf16[1024,1024]{1,0:T(8,128)(2,1)}, bf16[2,2,1024,256]{3,2,1,0:T(8,128)(2,1)}, bf16[2,2,1024,256]{3,2,1,0:...) custom-call(s32[1]{0:T(128)} %bitcast.2.me_ref, bf16[2,1024,256]{2,1,0:T(8,128)(2,1)} %copy-done.8, ...), custom_call_target="tpu_custom_call" | custom-call | flops 12884901888 | bytes 25165824 | tf_op jit(solution)/shard_map/pallas_call | solution.py:129
  495.1 24.9 %shard_map.117 = (bf16[1024,1024]{1,0:T(8,128)(2,1)}, bf16[1024,1024]{1,0:T(8,128)(2,1)}, bf16[2,2,1024,256]{3,2,1,0:T(8,128)(2,1)}, bf16[2,2,1024,256]{3,2,1,0:...) custom-call(s32[1]{0:T(128)} %bitcast.2.me_ref, bf16[2,1024,256]{2,1,0:T(8,128)(2,1)} %pad_maximum_fusion.3.refs_0_, ...), custom_call_target="tpu_custom_call" | custom-call | flops 12884901888 | bytes 25165824 | tf_op jit(solution)/shard_map/pallas_call | solution.py:129
  521.0 25.2 %shard_map.120 = (bf16[1024,1024]{1,0:T(8,128)(2,1)}, bf16[1024,1024]{1,0:T(8,128)(2,1)}, bf16[2,2,1024,256]{3,2,1,0:T(8,128)(2,1)}, bf16[2,2,1024,256]{3,2,1,0:...) custom-call(s32[1]{0:T(128)} %bitcast.2.me_ref, bf16[2,1024,256]{2,1,0:T(8,128)(2,1)} %pad_maximum_fusion.5.refs_0_, ...), custom_call_target="tpu_custom_call" | custom-call | flops 12884901888 | bytes 25165824 | tf_op jit(solution)/shard_map/pallas_call | solution.py:129
  546.3 24.9 %shard_map.123 = (bf16[1024,1024]{1,0:T(8,128)(2,1)}, bf16[1024,1024]{1,0:T(8,128)(2,1)}, bf16[2,2,1024,256]{3,2,1,0:T(8,128)(2,1)}, bf16[2,2,1024,256]{3,2,1,0:...) custom-call(s32[1]{0:T(128)} %bitcast.2.me_ref, bf16[2,1024,256]{2,1,0:T(8,128)(2,1)} %copy-done.10, ...), custom_call_target="tpu_custom_call" | custom-call | flops 12884901888 | bytes 25165824 | tf_op jit(solution)/shard_map/pallas_call | solution.py:129
  620.7 16.8 %shard_map.127 = f32[1024,1024]{1,0:T(8,128)} custom-call(s32[1]{0:T(128)} %bitcast.61.half_ref, f32[8]{0:T(128)} %multiply_minimum_fusion.clip_ref, bf16[3,2,4,512,2048]{4,3,2,1,0:T(8,128)(2,1)} %refs_0_.13, bf16[1024,1024]{1,0:T(8,128)(2,1)} %get-tuple-element.113.refs_2_.refs_1_, bf16[1024,1024]{1,0:T(8,128)(2,1)} %get-tuple-element.114.refs_3_.refs_2_, ...), custom_call_target="tpu_custom_call" | custom-call | flops 8589934592 | bytes 25165824 | tf_op jit(solution)/shard_map/pallas_call | solution.py:208
  654.8 17.5 %shard_map.136 = f32[1024,1024]{1,0:T(8,128)} custom-call(s32[1]{0:T(128)} %bitcast.61.half_ref, f32[8]{0:T(128)} %multiply_minimum_fusion.clip_ref, bf16[1024,1024]{1,0:T(8,128)(2,1)} %get-tuple-element.138.refs_1_.refs_0_, bf16[1024,1024]{1,0:T(8,128)(2,1)} %get-tuple-element.139.refs_2_.refs_1_, bf16[1024,1024]{1,0:T(8,128)(2,1)} %get-tuple-element.140.refs_3_.refs_2_, ...), custom_call_target="tpu_custom_call" | custom-call | flops 8589934592 | bytes 25165824 | tf_op jit(solution)/shard_map/pallas_call | solution.py:208
  706.1 16.3 %shard_map.125 = f32[1024,1024]{1,0:T(8,128)} custom-call(s32[1]{0:T(128)} %bitcast.61.half_ref, f32[8]{0:T(128)} %multiply_minimum_fusion.clip_ref, bf16[3,2,4,512,2048]{4,3,2,1,0:T(8,128)(2,1)} %refs_0_.13, bf16[1024,1024]{1,0:T(8,128)(2,1)} %get-tuple-element.109.refs_2_.refs_1_, bf16[1024,1024]{1,0:T(8,128)(2,1)} %get-tuple-element.110.refs_3_.refs_2_, ...), custom_call_target="tpu_custom_call" | custom-call | flops 8589934592 | bytes 25165824 | tf_op jit(solution)/shard_map/pallas_call | solution.py:208
  725.6 17.9 %shard_map.137.own_ref = f32[1024,1024]{1,0:T(8,128)} custom-call(s32[1]{0:T(128)} %bitcast.half_ref, f32[8]{0:T(128)} %multiply_minimum_fusion.clip_ref, f32[1]{0:T(128)} %bitcast.60.refs_0_, bf16[1024,1024]{1,0:T(8,128)(2,1)} %get-tuple-element.146.refs_1_.refs_0_, bf16[1024,1024]{1,0:T(8,128)(2,1)} %get-tuple-element.147.refs_2_.refs_1_, ...), custom_call_target="tpu_custom_call" | custom-call | flops 8589934592 | bytes 25165824 | tf_op jit(solution)/shard_map/pallas_call | solution.py:208
  746.9 39.1 %collective-permute-done.88.got_ref = f32[1024,1024]{1,0:T(8,128)} collective-permute-done((f32[1024,1024]{1,0:T(8,128)}, f32[1024,1024]{1,0:T(8,128)}, u32[]{:S(2)}, u32[]{:S(2)}) %collective-permute-start.88) | collective-permute-done | bytes 4194336 | tf_op jit(solution)/shard_map/ppermute | solution.py:343
  799.8 17.7 %shard_map.134 = f32[1024,1024]{1,0:T(8,128)} custom-call(s32[1]{0:T(128)} %bitcast.61.half_ref, f32[8]{0:T(128)} %multiply_minimum_fusion.clip_ref, bf16[1024,1024]{1,0:T(8,128)(2,1)} %get-tuple-element.121.refs_1_.refs_0_, bf16[1024,1024]{1,0:T(8,128)(2,1)} %get-tuple-element.122.refs_2_.refs_1_, bf16[1024,1024]{1,0:T(8,128)(2,1)} %get-tuple-element.123.refs_3_.refs_2_, ...), custom_call_target="tpu_custom_call" | custom-call | flops 8589934592 | bytes 25165824 | tf_op jit(solution)/shard_map/pallas_call | solution.py:208
  821.6 54.3 %collective-permute-done.58.got_ref = f32[1024,1024]{1,0:T(8,128)} collective-permute-done((f32[1024,1024]{1,0:T(8,128)}, f32[1024,1024]{1,0:T(8,128)}, u32[]{:S(2)}, u32[]{:S(2)}) %collective-permute-start.58) | collective-permute-done | bytes 4194336 | tf_op jit(solution)/shard_map/ppermute | solution.py:343
  875.9 89.9 %collective-permute-done.57.got_ref = f32[1024,1024]{1,0:T(8,128)} collective-permute-done((f32[1024,1024]{1,0:T(8,128)}, f32[1024,1024]{1,0:T(8,128)}, u32[]{:S(2)}, u32[]{:S(2)}) %collective-permute-start.57) | collective-permute-done | bytes 4194336 | tf_op jit(solution)/shard_map/ppermute | solution.py:343
  965.8 89.9 %collective-permute-done.56.got_ref = f32[1024,1024]{1,0:T(8,128)} collective-permute-done((f32[1024,1024]{1,0:T(8,128)}, f32[1024,1024]{1,0:T(8,128)}, u32[]{:S(2)}, u32[]{:S(2)}) %collective-permute-start.56) | collective-permute-done | bytes 4194336 | tf_op jit(solution)/shard_map/ppermute | solution.py:343
  1055.7 18.6 %shard_map.135.own_ref = f32[1024,1024]{1,0:T(8,128)} custom-call(s32[1]{0:T(128)} %bitcast.half_ref, f32[8]{0:T(128)} %multiply_minimum_fusion.clip_ref, f32[1]{0:T(128)} %bitcast.60.refs_0_, bf16[1024,1024]{1,0:T(8,128)(2,1)} %get-tuple-element.138.refs_1_.refs_0_, bf16[1024,1024]{1,0:T(8,128)(2,1)} %get-tuple-element.139.refs_2_.refs_1_, ...), custom_call_target="tpu_custom_call" | custom-call | flops 8589934592 | bytes 25165824 | tf_op jit(solution)/shard_map/pallas_call | solution.py:208
  1080.4 18.6 %shard_map.133.own_ref = f32[1024,1024]{1,0:T(8,128)} custom-call(s32[1]{0:T(128)} %bitcast.half_ref, f32[8]{0:T(128)} %multiply_minimum_fusion.clip_ref, f32[1]{0:T(128)} %bitcast.60.refs_0_, bf16[1024,1024]{1,0:T(8,128)(2,1)} %get-tuple-element.121.refs_1_.refs_0_, bf16[1024,1024]{1,0:T(8,128)(2,1)} %get-tuple-element.122.refs_2_.refs_1_, ...), custom_call_target="tpu_custom_call" | custom-call | flops 8589934592 | bytes 25165824 | tf_op jit(solution)/shard_map/pallas_call | solution.py:208
  1098.9 18.1 %shard_map.128.own_ref = f32[1024,1024]{1,0:T(8,128)} custom-call(s32[1]{0:T(128)} %bitcast.half_ref, f32[8]{0:T(128)} %multiply_minimum_fusion.clip_ref, f32[1]{0:T(128)} %bitcast.60.refs_0_, bf16[3,2,4,512,2048]{4,3,2,1,0:T(8,128)(2,1)} %refs_0_.13, bf16[1024,1024]{1,0:T(8,128)(2,1)} %get-tuple-element.117.refs_2_.refs_1_, ...), custom_call_target="tpu_custom_call" | custom-call | flops 8589934592 | bytes 25165824 | tf_op jit(solution)/shard_map/pallas_call | solution.py:208
  1118.1 18.0 %shard_map.126.own_ref = f32[1024,1024]{1,0:T(8,128)} custom-call(s32[1]{0:T(128)} %bitcast.half_ref, f32[8]{0:T(128)} %multiply_minimum_fusion.clip_ref, f32[1]{0:T(128)} %bitcast.60.refs_0_, bf16[3,2,4,512,2048]{4,3,2,1,0:T(8,128)(2,1)} %refs_0_.13, bf16[1024,1024]{1,0:T(8,128)(2,1)} %get-tuple-element.113.refs_2_.refs_1_, ...), custom_call_target="tpu_custom_call" | custom-call | flops 8589934592 | bytes 25165824 | tf_op jit(solution)/shard_map/pallas_call | solution.py:208
  1136.1 18.2 %shard_map.124.own_ref = f32[1024,1024]{1,0:T(8,128)} custom-call(s32[1]{0:T(128)} %bitcast.half_ref, f32[8]{0:T(128)} %multiply_minimum_fusion.clip_ref, f32[1]{0:T(128)} %bitcast.60.refs_0_, bf16[3,2,4,512,2048]{4,3,2,1,0:T(8,128)(2,1)} %refs_0_.13, bf16[1024,1024]{1,0:T(8,128)(2,1)} %get-tuple-element.109.refs_2_.refs_1_, ...), custom_call_target="tpu_custom_call" | custom-call | flops 8589934592 | bytes 25165824 | tf_op jit(solution)/shard_map/pallas_call | solution.py:208
  (342 shorter events, 335.3 us)
Async XLA Ops:
  24.5 49.8 %collective-permute-start = (bf16[2,2,1024,256]{3,2,1,0:T(8,128)(2,1)}, bf16[2,2,1024,256]{3,2,1,0:T(8,128)(2,1)S(1)}, u32[]{:S(2)}, u32[]{:S(2)}) collective-permute-start(bf16[2,2,1024,256]{3,2,1,0:T(8,128)(2,1)} %get-tuple-element.79), channel_id=1, source_target_pairs={{0,1},{1,0},{2,3},{3,2},{4,5},{5,4},{6,7},{7,6},{8,9},{9,8},{10,11... | collective-permute-start | bytes 6291464 | tf_op jit(solution)/shard_map/ppermute | solution.py:281
  49.4 56.6 %collective-permute-start.14 = (bf16[2,2,1024,256]{3,2,1,0:T(8,128)(2,1)}, bf16[2,2,1024,256]{3,2,1,0:T(8,128)(2,1)}, u32[]{:S(2)}, u32[]{:S(2)}) collective-permute-start(bf16[2,2,1024,256]{3,2,1,0:T(8,128)(2,1)} %get-tuple-element.87), channel_id=1, source_target_pairs={{0,1},{1,0},{2,3},{3,2},{4,5},{5,4},{6,7},{7,6},{8,9},{9,8},{10,11... | collective-permute-start | bytes 6291464 | tf_op jit(solution)/shard_map/ppermute | solution.py:281
  113.2 49.9 %collective-permute-start.29 = (bf16[2,1024,256]{2,1,0:T(8,128)(2,1)S(1)}, bf16[2,1024,256]{2,1,0:T(8,128)(2,1)S(1)}, u32[]{:S(2)}, u32[]{:S(2)}) collective-permute-start(bf16[2,1024,256]{2,1,0:T(8,128)(2,1)S(1)} %get-tuple-element.170), channel_id=1, source_target_pairs={{0,2},{1,3},{2,0},{3,1},{4,6},{5,7},{6,4},{7,5},{8,10},{9,11},{10,... | collective-permute-start | bytes 3145736 | tf_op jit(solution)/shard_map/ppermute | solution.py:281
  183.6 47.1 %collective-permute-start.5 = (bf16[2,1024,256]{2,1,0:T(8,128)(2,1)S(1)}, bf16[2,1024,256]{2,1,0:T(8,128)(2,1)S(1)}, u32[]{:S(2)}, u32[]{:S(2)}) collective-permute-start(bf16[2,1024,256]{2,1,0:T(8,128)(2,1)S(1)} %pad_maximum_fusion.refs_0_), channel_id=1, source_target_pairs={{0,1},{1,0},{2,3},{3,2},{4,5},{5,4},{6,7},{7,6},{8,9},{9,8},{10,11... | collective-permute-start | bytes 3145736 | tf_op jit(solution)/shard_map/ppermute | solution.py:281
  230.6 54.5 %collective-permute-start.33 = (bf16[2,1024,256]{2,1,0:T(8,128)(2,1)}, bf16[2,1024,256]{2,1,0:T(8,128)(2,1)}, u32[]{:S(2)}, u32[]{:S(2)}) collective-permute-start(bf16[2,1024,256]{2,1,0:T(8,128)(2,1)} %pad_maximum_fusion.4.refs_0_), channel_id=1, source_target_pairs={{0,1},{1,0},{2,3},{3,2},{4,5},{5,4},{6,7},{7,6},{8,9},{9,8},{10,11... | collective-permute-start | bytes 3145736 | tf_op jit(solution)/shard_map/ppermute | solution.py:281
  258.5 57.5 %collective-permute-start.47 = (bf16[2,1024,256]{2,1,0:T(8,128)(2,1)}, bf16[2,1024,256]{2,1,0:T(8,128)(2,1)}, u32[]{:S(2)}, u32[]{:S(2)}) collective-permute-start(bf16[2,1024,256]{2,1,0:T(8,128)(2,1)} %pad_maximum_fusion.6.refs_0_), channel_id=1, source_target_pairs={{0,1},{1,0},{2,3},{3,2},{4,5},{5,4},{6,7},{7,6},{8,9},{9,8},{10,11... | collective-permute-start | bytes 3145736 | tf_op jit(solution)/shard_map/ppermute | solution.py:281
  259.1 56.9 %collective-permute-start.48 = (bf16[2,1024,256]{2,1,0:T(8,128)(2,1)}, bf16[2,1024,256]{2,1,0:T(8,128)(2,1)}, u32[]{:S(2)}, u32[]{:S(2)}) collective-permute-start(bf16[2,1024,256]{2,1,0:T(8,128)(2,1)} %collective-permute-done.46.refs_1_), channel_id=1, source_target_pairs={{0,1},{1,0},{2,3},{3,2},{4,5},{5,4},{6,7},{7,6},{8,9},{9,8},{10,11... | collective-permute-start | bytes 3145736 | tf_op jit(solution)/shard_map/ppermute | solution.py:281
  259.2 51.8 %collective-permute-start.7 = (bf16[2,2,1024,256]{3,2,1,0:T(8,128)(2,1)}, bf16[2,2,1024,256]{3,2,1,0:T(8,128)(2,1)}, u32[]{:S(2)}, u32[]{:S(2)}) collective-permute-start(bf16[2,2,1024,256]{3,2,1,0:T(8,128)(2,1)} %get-tuple-element.82), channel_id=1, source_target_pairs={{0,1},{1,0},{2,3},{3,2},{4,5},{5,4},{6,7},{7,6},{8,9},{9,8},{10,11... | collective-permute-start | bytes 6291464 | tf_op jit(solution)/shard_map/ppermute | solution.py:281
  285.1 56.2 %collective-permute-start.21 = (bf16[2,2,1024,256]{3,2,1,0:T(8,128)(2,1)}, bf16[2,2,1024,256]{3,2,1,0:T(8,128)(2,1)}, u32[]{:S(2)}, u32[]{:S(2)}) collective-permute-start(bf16[2,2,1024,256]{3,2,1,0:T(8,128)(2,1)} %get-tuple-element.90), channel_id=1, source_target_pairs={{0,1},{1,0},{2,3},{3,2},{4,5},{5,4},{6,7},{7,6},{8,9},{9,8},{10,11... | collective-permute-start | bytes 6291464 | tf_op jit(solution)/shard_map/ppermute | solution.py:281
  341.1 42.0 %collective-permute-start.49 = (bf16[2,2,1024,256]{3,2,1,0:T(8,128)(2,1)}, bf16[2,2,1024,256]{3,2,1,0:T(8,128)(2,1)S(1)}, u32[]{:S(2)}, u32[]{:S(2)}) collective-permute-start(bf16[2,2,1024,256]{3,2,1,0:T(8,128)(2,1)} %get-tuple-element.106), channel_id=1, source_target_pairs={{0,1},{1,0},{2,3},{3,2},{4,5},{5,4},{6,7},{7,6},{8,9},{9,8},{10,11... | collective-permute-start | bytes 6291464 | tf_op jit(solution)/shard_map/ppermute | solution.py:281
  349.5 49.9 %collective-permute-start.36 = (bf16[2,1024,256]{2,1,0:T(8,128)(2,1)S(1)}, bf16[2,1024,256]{2,1,0:T(8,128)(2,1)S(1)}, u32[]{:S(2)}, u32[]{:S(2)}) collective-permute-start(bf16[2,1024,256]{2,1,0:T(8,128)(2,1)S(1)} %get-tuple-element.168), channel_id=1, source_target_pairs={{0,2},{1,3},{2,0},{3,1},{4,6},{5,7},{6,4},{7,5},{8,10},{9,11},{10,... | collective-permute-start | bytes 3145736 | tf_op jit(solution)/shard_map/ppermute | solution.py:281
  420.1 47.3 %collective-permute-start.12 = (bf16[2,1024,256]{2,1,0:T(8,128)(2,1)S(1)}, bf16[2,1024,256]{2,1,0:T(8,128)(2,1)}, u32[]{:S(2)}, u32[]{:S(2)}) collective-permute-start(bf16[2,1024,256]{2,1,0:T(8,128)(2,1)S(1)} %pad_maximum_fusion.1.refs_0_), channel_id=1, source_target_pairs={{0,1},{1,0},{2,3},{3,2},{4,5},{5,4},{6,7},{7,6},{8,9},{9,8},{10,11... | collective-permute-start | bytes 3145736 | tf_op jit(solution)/shard_map/ppermute | solution.py:281
  467.5 52.6 %collective-permute-start.40 = (bf16[2,1024,256]{2,1,0:T(8,128)(2,1)}, bf16[2,1024,256]{2,1,0:T(8,128)(2,1)S(1)}, u32[]{:S(2)}, u32[]{:S(2)}) collective-permute-start(bf16[2,1024,256]{2,1,0:T(8,128)(2,1)} %pad_maximum_fusion.5.refs_0_), channel_id=1, source_target_pairs={{0,1},{1,0},{2,3},{3,2},{4,5},{5,4},{6,7},{7,6},{8,9},{9,8},{10,11... | collective-permute-start | bytes 3145736 | tf_op jit(solution)/shard_map/ppermute | solution.py:281
  494.0 52.3 %collective-permute-start.54 = (bf16[2,1024,256]{2,1,0:T(8,128)(2,1)S(1)}, bf16[2,1024,256]{2,1,0:T(8,128)(2,1)}, u32[]{:S(2)}, u32[]{:S(2)}) collective-permute-start(bf16[2,1024,256]{2,1,0:T(8,128)(2,1)S(1)} %pad_maximum_fusion.7.refs_0_), channel_id=1, source_target_pairs={{0,1},{1,0},{2,3},{3,2},{4,5},{5,4},{6,7},{7,6},{8,9},{9,8},{10,11... | collective-permute-start | bytes 3145736 | tf_op jit(solution)/shard_map/ppermute | solution.py:281
  494.6 51.7 %collective-permute-start.55 = (bf16[2,1024,256]{2,1,0:T(8,128)(2,1)S(1)}, bf16[2,1024,256]{2,1,0:T(8,128)(2,1)}, u32[]{:S(2)}, u32[]{:S(2)}) collective-permute-start(bf16[2,1024,256]{2,1,0:T(8,128)(2,1)S(1)} %collective-permute-done.53.refs_1_), channel_id=1, source_target_pairs={{0,1},{1,0},{2,3},{3,2},{4,5},{5,4},{6,7},{7,6},{8,9},{9,8},{10,11... | collective-permute-start | bytes 3145736 | tf_op jit(solution)/shard_map/ppermute | solution.py:281
  585.1 52.5 %collective-permute-start.80 = (bf16[2,2,1024,256]{3,2,1,0:T(8,128)(2,1)}, bf16[2,2,1024,256]{3,2,1,0:T(8,128)(2,1)}, u32[]{:S(2)}, u32[]{:S(2)}) collective-permute-start(bf16[2,2,1024,256]{3,2,1,0:T(8,128)(2,1)} %get-tuple-element.136), channel_id=1, source_target_pairs={{0,1},{1,0},{2,3},{3,2},{4,5},{5,4},{6,7},{7,6},{8,9},{9,8},{10,11... | collective-permute-start | bytes 6291464 | tf_op jit(solution)/shard_map/ppermute | solution.py:281
  585.1 57.3 %collective-permute-start.73 = (bf16[2,2,1024,256]{3,2,1,0:T(8,128)(2,1)}, bf16[2,2,1024,256]{3,2,1,0:T(8,128)(2,1)}, u32[]{:S(2)}, u32[]{:S(2)}) collective-permute-start(bf16[2,2,1024,256]{3,2,1,0:T(8,128)(2,1)} %get-tuple-element.134), channel_id=1, source_target_pairs={{0,1},{1,0},{2,3},{3,2},{4,5},{5,4},{6,7},{7,6},{8,9},{9,8},{10,11... | collective-permute-start | bytes 6291464 | tf_op jit(solution)/shard_map/ppermute | solution.py:281
  602.4 144.5 %collective-permute-start.89 = (f32[1024,1024]{1,0:T(8,128)}, f32[1024,1024]{1,0:T(8,128)}, u32[]{:S(2)}, u32[]{:S(2)}) collective-permute-start(f32[1024,1024]{1,0:T(8,128)} %shard_map.138), channel_id=1, source_target_pairs={{0,8},{8,0},{1,9},{9,1},{2,10},{10,2},{3,11},{11,3},{4,12},{12,4},... | collective-permute-start | bytes 12582920 | tf_op jit(solution)/shard_map/ppermute | solution.py:343
  603.9 45.7 %collective-permute-start.59 = (bf16[2,2,1024,256]{3,2,1,0:T(8,128)(2,1)}, bf16[2,2,1024,256]{3,2,1,0:T(8,128)(2,1)}, u32[]{:S(2)}, u32[]{:S(2)}) collective-permute-start(bf16[2,2,1024,256]{3,2,1,0:T(8,128)(2,1)} %get-tuple-element.130), channel_id=1, source_target_pairs={{0,1},{1,0},{2,3},{3,2},{4,5},{5,4},{6,7},{7,6},{8,9},{9,8},{10,11... | collective-permute-start | bytes 6291464 | tf_op jit(solution)/shard_map/ppermute | solution.py:281
  672.2 113.8 %collective-permute-start.88 = (f32[1024,1024]{1,0:T(8,128)}, f32[1024,1024]{1,0:T(8,128)}, u32[]{:S(2)}, u32[]{:S(2)}) collective-permute-start(f32[1024,1024]{1,0:T(8,128)} %shard_map.136), channel_id=1, source_target_pairs={{0,8},{8,0},{1,9},{9,1},{2,10},{10,2},{3,11},{11,3},{4,12},{12,4},... | collective-permute-start | bytes 12582920 | tf_op jit(solution)/shard_map/ppermute | solution.py:343
  722.4 153.5 %collective-permute-start.58 = (f32[1024,1024]{1,0:T(8,128)}, f32[1024,1024]{1,0:T(8,128)}, u32[]{:S(2)}, u32[]{:S(2)}) collective-permute-start(f32[1024,1024]{1,0:T(8,128)} %shard_map.129), channel_id=1, source_target_pairs={{0,8},{8,0},{1,9},{9,1},{2,10},{10,2},{3,11},{11,3},{4,12},{12,4},... | collective-permute-start | bytes 12582920 | tf_op jit(solution)/shard_map/ppermute | solution.py:343
  722.9 242.9 %collective-permute-start.57 = (f32[1024,1024]{1,0:T(8,128)}, f32[1024,1024]{1,0:T(8,128)}, u32[]{:S(2)}, u32[]{:S(2)}) collective-permute-start(f32[1024,1024]{1,0:T(8,128)} %shard_map.127), channel_id=1, source_target_pairs={{0,8},{8,0},{1,9},{9,1},{2,10},{10,2},{3,11},{11,3},{4,12},{12,4},... | collective-permute-start | bytes 12582920 | tf_op jit(solution)/shard_map/ppermute | solution.py:343
  724.4 331.2 %collective-permute-start.56 = (f32[1024,1024]{1,0:T(8,128)}, f32[1024,1024]{1,0:T(8,128)}, u32[]{:S(2)}, u32[]{:S(2)}) collective-permute-start(f32[1024,1024]{1,0:T(8,128)} %shard_map.125), channel_id=1, source_target_pairs={{0,8},{8,0},{1,9},{9,1},{2,10},{10,2},{3,11},{11,3},{4,12},{12,4},... | collective-permute-start | bytes 12582920 | tf_op jit(solution)/shard_map/ppermute | solution.py:343
  746.9 43.7 %collective-permute-start.83 = (bf16[1024,256]{1,0:T(8,128)(2,1)S(1)}, bf16[1024,256]{1,0:T(8,128)(2,1)S(1)}, u32[]{:S(2)}, u32[]{:S(2)}) collective-permute-start(bf16[1024,256]{1,0:T(8,128)(2,1)S(1)} %fusion.14), channel_id=1, source_target_pairs={{0,2},{1,3},{2,0},{3,1},{4,6},{5,7},{6,4},{7,5},{8,10},{9,11},{10,... | collective-permute-start | bytes 1572872 | tf_op jit(solution)/shard_map/ppermute | solution.py:281
  819.2 380.4 %collective-permute-start.87 = (f32[1024,1024]{1,0:T(8,128)}, f32[1024,1024]{1,0:T(8,128)}, u32[]{:S(2)}, u32[]{:S(2)}) collective-permute-start(f32[1024,1024]{1,0:T(8,128)} %shard_map.134), channel_id=1, source_target_pairs={{0,8},{8,0},{1,9},{9,1},{2,10},{10,2},{3,11},{11,3},{4,12},{12,4},... | collective-permute-start | bytes 12582920 | tf_op jit(solution)/shard_map/ppermute | solution.py:343
  820.8 257.4 %collective-permute-start.84 = (bf16[2,1024,256]{2,1,0:T(8,128)(2,1)S(1)}, bf16[2,1024,256]{2,1,0:T(8,128)(2,1)}, u32[]{:S(2)}, u32[]{:S(2)}) collective-permute-start(bf16[2,1024,256]{2,1,0:T(8,128)(2,1)S(1)} %pad_maximum_fusion.11.refs_12_), channel_id=1, source_target_pairs={{0,4},{1,5},{2,6},{3,7},{4,0},{5,1},{6,2},{7,3},{8,12},{9,13},{10,... | collective-permute-start | bytes 3145736 | tf_op jit(solution)/shard_map/ppermute | solution.py:281
  875.9 203.9 %collective-permute-start.85 = (bf16[2,1024,256]{2,1,0:T(8,128)(2,1)S(1)}, bf16[2,1024,256]{2,1,0:T(8,128)(2,1)}, u32[]{:S(2)}, u32[]{:S(2)}) collective-permute-start(bf16[2,1024,256]{2,1,0:T(8,128)(2,1)S(1)} %pad_maximum_fusion.11.refs_12_), channel_id=1, source_target_pairs={{0,1},{1,0},{2,3},{3,2},{4,5},{5,4},{6,7},{7,6},{8,9},{9,8},{10,11... | collective-permute-start | bytes 3145736 | tf_op jit(solution)/shard_map/ppermute | solution.py:281
  965.8 114.2 %collective-permute-start.77 = (bf16[2,1024,256]{2,1,0:T(8,128)(2,1)S(1)}, bf16[2,1024,256]{2,1,0:T(8,128)(2,1)}, u32[]{:S(2)}, u32[]{:S(2)}) collective-permute-start(bf16[2,1024,256]{2,1,0:T(8,128)(2,1)S(1)} %pad_maximum_fusion.10.refs_8_), channel_id=1, source_target_pairs={{0,2},{1,3},{2,0},{3,1},{4,6},{5,7},{6,4},{7,5},{8,10},{9,11},{10,... | collective-permute-start | bytes 3145736 | tf_op jit(solution)/shard_map/ppermute | solution.py:281
  1117.0 65.9 %collective-permute-start.86 = (bf16[2,1024,256]{2,1,0:T(8,128)(2,1)}, bf16[2,1024,256]{2,1,0:T(8,128)(2,1)}, u32[]{:S(2)}, u32[]{:S(2)}) collective-permute-start(bf16[2,1024,256]{2,1,0:T(8,128)(2,1)} %collective-permute-done.84.refs_13_), channel_id=1, source_target_pairs={{0,1},{1,0},{2,3},{3,2},{4,5},{5,4},{6,7},{7,6},{8,9},{9,8},{10,11... | collective-permute-start | bytes 3145736 | tf_op jit(solution)/shard_map/ppermute | solution.py:281
  1117.2 65.7 %collective-permute-start.79 = (bf16[2,1024,256]{2,1,0:T(8,128)(2,1)}, bf16[2,1024,256]{2,1,0:T(8,128)(2,1)S(1)}, u32[]{:S(2)}, u32[]{:S(2)}) collective-permute-start(bf16[2,1024,256]{2,1,0:T(8,128)(2,1)} %collective-permute-done.77.refs_9_), channel_id=1, source_target_pairs={{0,1},{1,0},{2,3},{3,2},{4,5},{5,4},{6,7},{7,6},{8,9},{9,8},{10,11... | collective-permute-start | bytes 3145736 | tf_op jit(solution)/shard_map/ppermute | solution.py:281
  1117.5 65.4 %collective-permute-start.72 = (bf16[2,1024,256]{2,1,0:T(8,128)(2,1)}, bf16[2,1024,256]{2,1,0:T(8,128)(2,1)}, u32[]{:S(2)}, u32[]{:S(2)}) collective-permute-start(bf16[2,1024,256]{2,1,0:T(8,128)(2,1)} %collective-permute-done.70.refs_5_), channel_id=1, source_target_pairs={{0,1},{1,0},{2,3},{3,2},{4,5},{5,4},{6,7},{7,6},{8,9},{9,8},{10,11... | collective-permute-start | bytes 3145736 | tf_op jit(solution)/shard_map/ppermute | solution.py:281
  1117.8 65.2 %collective-permute-start.65 = (bf16[2,1024,256]{2,1,0:T(8,128)(2,1)}, bf16[2,1024,256]{2,1,0:T(8,128)(2,1)}, u32[]{:S(2)}, u32[]{:S(2)}) collective-permute-start(bf16[2,1024,256]{2,1,0:T(8,128)(2,1)} %collective-permute-done.63.refs_1_), channel_id=1, source_target_pairs={{0,1},{1,0},{2,3},{3,2},{4,5},{5,4},{6,7},{7,6},{8,9},{9,8},{10,11... | collective-permute-start | bytes 3145736 | tf_op jit(solution)/shard_map/ppermute | solution.py:281
  (114 other events, 3232.3 us)
where the time goes:
time: 1210 us
  Pallas kernels  556 us (46%)
  waiting for transfers between devices  507 us (42%)
  other arithmetic  62.7 us (5%)
  starting transfers between devices  56.8 us (5%)
  blocking collectives  13 us (1%)
    pallas_call x12, Pallas kernels, backward_chunk(): pl.pallas_call(functools.partial(backward_kernel, layer, micro, first_ex,...  296 us
    ppermute x6, waiting for transfers between devices, local_pass(): got.append(lax.ppermute(part, 'dp', swap_dp))  273 us
    ppermute x84, waiting for transfers between devices, swap(): return lax.ppermute(value, 'tp', [(i, i ^ mask) for i in range(tp_size)])  234 us
    pallas_call x12, Pallas kernels, weight_grad(): pl.pallas_call(functools.partial(grad_kernel, up, n_chunks, noise is not...  210 us
    ppermute x84, starting transfers between devices, swap(): return lax.ppermute(value, 'tp', [(i, i ^ mask) for i in range(tp_size)])  50.7 us
    convert_element_type x24, other arithmetic, add(): return (a.astype(jnp.float32) + b.astype(jnp.float32)).astype(jnp.bfloat16)  41.1 us
    pallas_call x6, Pallas kernels, finish_grad(): pl.pallas_call(functools.partial(finish_kernel, 1.0 / examples), grid=(4,...  34.5 us
  transfers between devices with their start and end apart: 90, of which 22 were waited for; matrix products, arithmetic and copies ran while one was open for 5% of the time, Pallas kernels for 42%

commit v1 on v0

--- a/solution.py
+++ b/solution.py
@@ -26,6 +26,21 @@
 def piece_of(me, r1, r2, rc, x_first):
     bits = (r2 * 4 + r1 * 2 + rc) if x_first else (r1 * 4 + r2 * 2 + rc)
     return me ^ bits
+
+
+def hidden_of(u_ref, cot, w2, h_ref, dh_ref, before=lambda j: None):
+    width = 256
+    for j in range(u_ref.shape[-1] // width):
+        before(j)
+        cols = slice(j * width, (j + 1) * width)
+        d_act = dot(cot[...], w2[cols, :], NT)
+        u = u_ref[:, cols].astype(jnp.float32)
+        u_sq = u * u
+        t = jnp.tanh(TANH_SCALE * (u + TANH_CUBE * (u_sq * u)))
+        cdf = 0.5 * (1.0 + t)
+        slope = cdf + (0.5 * TANH_SCALE) * (1.0 - t * t) * (u * (1.0 + (3.0 * TANH_CUBE) * u_sq))
+        h_ref[:, cols] = (u * cdf).astype(jnp.bfloat16)
+        dh_ref[:, cols] = (slope * d_act).astype(jnp.bfloat16)
 
 
 def backward_kernel(layer, micro, first_ex, x_first, from_slots, me_ref, *refs):
@@ -69,23 +84,15 @@
     else:
         cot = dz_in
         piece_ref[...] = dz_in[:, pl.ds(pl.multiple_of(me * PIECE, PIECE), PIECE)]
-    width = 256
-    for j in range(hid // width):
+
+    def wait_weights(j):
         if j % 2 == 0:
 
             @pl.when(step == 0)
-            def _(j=j):
+            def _():
                 w2_copy(j // 2).wait()
 
-        cols = slice(j * width, (j + 1) * width)
-        d_act = dot(cot[...], w2[cols, :], NT)
-        u = u_ref[:, cols].astype(jnp.float32)
-        u_sq = u * u
-        t = jnp.tanh(TANH_SCALE * (u + TANH_CUBE * (u_sq * u)))
-        cdf = 0.5 * (1.0 + t)
-        slope = cdf + (0.5 * TANH_SCALE) * (1.0 - t * t) * (u * (1.0 + (3.0 * TANH_CUBE) * u_sq))
-        h_ref[:, cols] = (u * cdf).astype(jnp.bfloat16)
-        dh_ref[:, cols] = (slope * d_act).astype(jnp.bfloat16)
+    hidden_of(u_ref, cot, w2, h_ref, dh_ref, wait_weights)
 
     @pl.when(step == 0)
     def _():
@@ -152,84 +159,106 @@
     )(me, *operands, u_pre, w_up, w_down, x_in)
 
 
-def grad_kernel(up, n_chunks, with_noise, half_ref, clip_ref, *refs):
-    if with_noise:
-        scale_ref, refs = refs[0], refs[1:]
-    lhs, rhs = refs[:-1][: (1 if up else n_chunks)], refs[:-1][(1 if up else n_chunks) :]
-    if with_noise:
-        noise_ref, rhs = rhs[-1], rhs[:-1]
-    out_ref = refs[-1]
+def grad_kernel(sizes, half_ref, clip_ref, *refs):
+    n_lhs, n_rhs, per, has_init = sizes
+    if has_init:
+        scale_ref, init_ref, *refs = refs
+    lhs, rhs, out_ref = refs[:n_lhs], refs[n_lhs:-1], refs[-1]
     step = pl.program_id(0)
 
     @pl.when(step == 0)
     def _():
-        out_ref[...] = scale_ref[0] * noise_ref[...] if with_noise else jnp.zeros_like(out_ref)
+        out_ref[...] = scale_ref[0] * init_ref[...] if has_init else jnp.zeros_like(out_ref)
 
     clip = clip_ref[step]
-    for k in range(n_chunks):
-
-        @pl.when(step // PER_CHUNK == k)
+    for k in range(max(n_lhs, n_rhs)):
+
+        @pl.when(step // per == k)
         def _(k=k):
-            a = lhs[min(k, len(lhs) - 1)]
-            b = rhs[min(k, len(rhs) - 1)]
+            a = lhs[min(k, n_lhs - 1)]
+            b = rhs[min(k, n_rhs - 1)]
             scaled = (b[...].astype(jnp.float32) * clip).astype(jnp.bfloat16)
             for j in range(2):
                 cols = slice(j * 512, (j + 1) * 512)
                 out_ref[:, cols] += dot(a[...], scaled[:, cols], TN)
 
 
-def weight_grad(up, layer, half, clip, lhs, rhs, noise=None, noise_scale=None):
-    n_chunks = len(lhs) if not up else len(rhs)
-    n_ex = n_chunks * PER_CHUNK
-
-    def chunk_row(k):
-        return lambda s, h: (jnp.clip(s - PER_CHUNK * k, 0, PER_CHUNK - 1), 0)
-
-    def chunk_half(k):
-        return lambda s, h: (jnp.clip(s - PER_CHUNK * k, 0, PER_CHUNK - 1), h[0])
-
-    if up:
-        lhs_specs = [pl.BlockSpec((None, None, None, 512, HALF), lambda s, h: (layer, s // 4, s % 4, 0, h[0]))]
-        rhs_specs = [pl.BlockSpec((512, 1024), chunk_row(k)) for k in range(n_chunks)]
-        lhs = (lhs,)
-    else:
-        lhs_specs = [pl.BlockSpec((512, 1024), chunk_row(k)) for k in range(n_chunks)]
-        if isinstance(rhs, tuple):
-            rhs_specs = [pl.BlockSpec((512, HALF), chunk_half(k)) for k in range(n_chunks)]
-        else:
-            rhs_specs = [pl.BlockSpec((None, None, 512, HALF), lambda s, h: (s // 4, s % 4, 0, h[0]))]
-            rhs = (rhs,)
-    extra, extra_specs, lead, lead_specs = (), [], (), []
-    if noise is not None:
-        extra = (noise,)
-        extra_specs = [pl.BlockSpec((None, 1024, 1024), lambda s, h: (layer, 0, 0))]
-        lead = (noise_scale,)
-        lead_specs = [pl.BlockSpec(memory_space=pltpu.SMEM)]
+def grad_operand(value, layer, per, columns):
+    def col(h):
+        return 0 if columns is None else h[0]
+
+    if isinstance(value, tuple):
+        return value, [
+            pl.BlockSpec((512, 1024), lambda s, h, k=k: (jnp.clip(s - per * k, 0, per - 1), col(h))) for k in range(len(value))
+        ]
+    lead = {5: lambda s: (layer, s // 4, s % 4), 4: lambda s: (s // 4, s % 4), 3: lambda s: (s,)}[value.ndim]
+    return (value,), [pl.BlockSpec((None,) * (value.ndim - 2) + (512, 1024), lambda s, h: (*lead(s), 0, col(h)))]
+
+
+def weight_grad(layer, half, clip, lhs, rhs, lhs_half, rhs_half, init=None, init_layer=0, scale=None):
+    parts = max(len(v) if isinstance(v, tuple) else 1 for v in (lhs, rhs))
+    n_ex = clip.shape[0]
+    per = n_ex // parts
+    lhs, lhs_specs = grad_operand(lhs, layer, per, lhs_half)
+    rhs, rhs_specs = grad_operand(rhs, layer, per, rhs_half)
+    lead, lead_specs = (), []
+    if init is not None:
+        lead = (scale, init)
+        lead_specs = [pl.BlockSpec(memory_space=pltpu.SMEM), pl.BlockSpec((None, 1024, 1024), lambda s, h: (init_layer, 0, 0))]
     return pl.pallas_call(
-        functools.partial(grad_kernel, up, n_chunks, noise is not None),
+        functools.partial(grad_kernel, (len(lhs), len(rhs), per, init is not None)),
         grid_spec=pltpu.PrefetchScalarGridSpec(
             num_scalar_prefetch=1,
             grid=(n_ex,),
-            in_specs=[pl.BlockSpec(memory_space=pltpu.SMEM)] + lead_specs + lhs_specs + rhs_specs + extra_specs,
+            in_specs=[pl.BlockSpec(memory_space=pltpu.SMEM)] + lead_specs + lhs_specs + rhs_specs,
             out_specs=pl.BlockSpec((1024, 1024), lambda s, h: (0, 0)),
         ),
         out_shape=jax.ShapeDtypeStruct((1024, 1024), jnp.float32),
         compiler_params=pltpu.CompilerParams(dimension_semantics=("arbitrary",)),
         cost_estimate=pl.CostEstimate(flops=2 * n_ex * 512 * 1024 * 1024, bytes_accessed=24 << 20, transcendentals=0),
-    )(half, clip, *lead, *lhs, *rhs, *extra)
-
-
-def finish_kernel(inv, own_ref, got_ref, *refs):
-    refs[-1][...] = (own_ref[...] + got_ref[...]) * inv
+    )(half, clip, *lead, *lhs, *rhs)
+
+
+def hidden_kernel(u_ref, dz_ref, w2_ref, h_ref, dh_ref):
+    hidden_of(u_ref, dz_ref, w2_ref, h_ref, dh_ref)
+
+
+def hidden_again(layer, u_other, cot_other, w_down):
+    n_ex, _, model = cot_other.shape
+    hid = u_other.shape[-1]
+    act_spec = pl.BlockSpec((512, hid), lambda e: (e, 0))
+    act_shape = jax.ShapeDtypeStruct((n_ex * 512, hid), jnp.bfloat16)
+    return pl.pallas_call(
+        hidden_kernel,
+        grid=(n_ex,),
+        in_specs=[
+            pl.BlockSpec((None, 512, hid), lambda e: (e, 0, 0)),
+            pl.BlockSpec((None, 512, model), lambda e: (e, 0, 0)),
+            pl.BlockSpec((None, hid, model), lambda e: (layer, 0, 0)),
+        ],
+        out_specs=[act_spec, act_spec],
+        out_shape=[act_shape, act_shape],
+        compiler_params=pltpu.CompilerParams(dimension_semantics=("arbitrary",)),
+        cost_estimate=pl.CostEstimate(flops=2 * n_ex * 512 * hid * model, bytes_accessed=48 << 20, transcendentals=n_ex * 512 * hid),
+        name="hidden_again",
+    )(u_other, cot_other, w_down)
+
+
+def finish_kernel(inv, has_got, own_ref, *refs):
+    total = own_ref[...] + refs[0][...] if has_got else own_ref[...]
+    refs[-1][...] = total * inv
 
 
 def finish_grad(layer, n_layers, examples, own, got, buffer):
     spec = pl.BlockSpec((256, 1024), lambda i: (i, 0))
-    operands, in_specs, aliases = (own, got), [spec, spec], {}
+    operands = (own,) if got is None else (own, got)
+    in_specs, aliases = [spec] * len(operands), {}
     if buffer is not None:
-        operands, in_specs, aliases = (own, got, buffer), [spec, spec, pl.BlockSpec(memory_space=pl.ANY)], {2: 0}
+        aliases = {len(operands): 0}
+        operands += (buffer,)
+        in_specs.append(pl.BlockSpec(memory_space=pl.ANY))
     return pl.pallas_call(
-        functools.partial(finish_kernel, 1.0 / examples),
+        functools.partial(finish_kernel, 1.0 / examples, got is not None),
         grid=(4,),
         in_specs=in_specs,
         out_specs=pl.BlockSpec((None, 256, 1024), lambda i: (layer, i, 0)),
@@ -312,6 +341,16 @@
         pieces = [None] * len(chunks)
         norms = [None] * len(chunks)
         saved = [None] * n_layers
+        top = n_layers - 1
+        swap_dp = [(i, 1 - i) for i in range(dp_size)]
+        ex_all = micro * per_micro
+        cot_slice = lax.dynamic_index_in_dim(d_out.reshape(ex_all, *d_out.shape[2:]), me, 0)
+        x_slice = lax.dynamic_slice(
+            x_in[top].reshape(ex_all, *d_out.shape[2:]), (me, 0, (1 - my_dp) * HALF), (1, d_out.shape[2], HALF)
+        )
+        cot_other = lax.ppermute(cot_slice, "dp", swap_dp)
+        u_other = lax.ppermute(u_pre[top].reshape(ex_all, *u_pre.shape[3:]), "dp", swap_dp)
+        x_other = lax.ppermute(x_slice, "dp", swap_dp)
         for layer in reversed(range(n_layers)):
             top = layer == n_layers - 1
             hids, dhids, full = [], [], []
@@ -319,31 +358,43 @@
                 hidden, d_hid, keep, send, norms[k], cot = backward_chunk(
                     layer, m, e, orders[k], me_arr, cots[k], norms[k], x_in, u_pre, w_up, w_down
                 )
+                if (layer, k) == (0, 1):
+                    cot_other, x_other, norms[k] = lax.optimization_barrier((cot_other, x_other, norms[k]))
                 pieces[k], cots[k] = sum_over_tp(keep, send, cot if top else pieces[k], orders[k])
                 hids.append(hidden)
                 dhids.append(d_hid)
                 full.append(cot)
             saved[layer] = (tuple(hids), tuple(dhids), d_out if top else tuple(full))
+        cot_other = lax.all_gather(cot_other, "tp", axis=0, tiled=True)
+        x_other = lax.all_gather(x_other, "tp", axis=0, tiled=True)
+        hid_other, dhid_other = hidden_again(n_layers - 1, u_other, cot_other, w_down)
         d_in = join_slots(me_arr, orders, cots, d_out.shape)
         norm_vec = lax.psum(jnp.sum(jnp.concatenate(norms), axis=(1, 2)), "tp")
         clip = jnp.minimum(1.0, clip_norm[0] / jnp.sqrt(norm_vec))
         noise_scale = (noise_mult[0] * clip_norm[0]).reshape(1)
         own_half, other_half = my_dp.reshape(1), (1 - my_dp).reshape(1)
-        swap_dp = [(i, 1 - i) for i in range(dp_size)]
-        grads = [(up, layer) for layer in reversed(range(n_layers)) for up in (True, False)]
-
-        def grad(up, layer, *rest):
+        top = n_layers - 1
+        grads = [(up, layer) for layer in reversed(range(top)) for up in (True, False)]
+
+        def grad(up, layer, half, *init):
             hids, dhids, full = saved[layer]
             lhs, rhs = (x_in, dhids) if up else (hids, full)
-            return weight_grad(up, layer, rest[0], clip, lhs, rhs, *rest[1:])
+            return weight_grad(layer, half, clip, lhs, rhs, True if up else None, None if up else True, *init)
 
         got = []
         for up, layer in grads:
             part = grad(up, layer, other_half)
             got.append(lax.ppermute(part, "dp", swap_dp))
         result = [None, None]
+        clip_other = lax.ppermute(clip, "dp", swap_dp)
+        one = jnp.ones((1,), jnp.float32)
+        for up in (True, False):
+            own = grad(up, top, own_half, noise_up if up else noise_down, top, noise_scale)[None]
+            lhs, rhs = (x_other, (dhid_other,)) if up else ((hid_other,), cot_other)
+            own = weight_grad(top, own_half, clip_other, lhs, rhs, None, None if up else True, own, 0, one)
+            result[up] = finish_grad(top, n_layers, examples, own, None, None)
         for i, (up, layer) in enumerate(grads):
-            own = grad(up, layer, own_half, noise_up if up else noise_down, noise_scale)
+            own = grad(up, layer, own_half, noise_up if up else noise_down, layer, noise_scale)
             if i == len(grads) - 1:
                 own, d_in = lax.optimization_barrier((own, d_in))
             result[up] = finish_grad(layer, n_layers, examples, own, got[i], result[up])

time: 1210 us -> 1490 us (1.23)
  waiting for transfers between devices: 507 us -> 704 us
  Pallas kernels: 556 us -> 586 us
  local copies, waits for them, and re-layouts: 6.44 us -> 34.6 us
    ppermute x0 -> x4, waiting for transfers between devices: none -> 302 us  [the longest x1 275 us: local_pass(): clip_other = lax.ppermute(clip, 'dp', swap_dp)]
    ppermute x6 -> x4, waiting for transfers between devices: 273 us -> 0.01 us  [local_pass(): got.append(lax.ppermute(part, 'dp', swap_dp))]
    ppermute x84, waiting for transfers between devices: 234 us -> 402 us  [swap(): return lax.ppermute(value, 'tp', [(i, i ^ mask) for i in range(tp_size)])]
    pallas_call x18 -> x19, Pallas kernels: 244 us -> 274 us  [the longest x12 210 us: weight_grad(): pl.pallas_call(functools.partial(grad_kernel, (len(lhs), len(rhs), per, i...]
    slice x0 -> x2, local copies, waits for them, and re-layouts: none -> 21.9 us  [the longest x1 14.2 us: local_pass(): x_in[top].reshape(ex_all, *d_out.shape[2:])]
  transfers between devices with their start and end apart: 90 -> 94, of which waited for: 22 -> 36; matrix products, arithmetic and copies ran while one was open for 5% -> 5% of each run, Pallas kernels for 42% -> 36%
where the time goes in v1:
time: 1490 us; the launch traced here: 1480 us
  waiting for transfers between devices  704 us (47%)
  Pallas kernels  586 us (39%)
  starting transfers between devices  69.6 us (5%)
  other arithmetic  54.7 us (4%)
  local copies, waits for them, and re-layouts  34.6 us (2%)
  between operations  16.6 us (1%)
    ppermute x84, waiting for transfers between devices, swap(): return lax.ppermute(value, 'tp', [(i, i ^ mask) for i in range(tp_size)])  402 us
    pallas_call x12, Pallas kernels, backward_chunk(): pl.pallas_call(functools.partial(backward_kernel, layer, micro, first_ex,...  296 us
    ppermute x1, waiting for transfers between devices, local_pass(): clip_other = lax.ppermute(clip, 'dp', swap_dp)  275 us
    pallas_call x12, Pallas kernels, weight_grad(): pl.pallas_call(functools.partial(grad_kernel, (len(lhs), len(rhs), per, i...  210 us
    ppermute x84, starting transfers between devices, swap(): return lax.ppermute(value, 'tp', [(i, i ^ mask) for i in range(tp_size)])  61.2 us
    convert_element_type x24, other arithmetic, add(): return (a.astype(jnp.float32) + b.astype(jnp.float32)).astype(jnp.bfloat16)  35.8 us
    pallas_call x6, Pallas kernels, finish_grad(): pl.pallas_call(functools.partial(finish_kernel, 1.0 / examples, got is no...  32.4 us
    pallas_call x1, Pallas kernels, hidden_again(): pl.pallas_call(hidden_kernel, grid=(n_ex,), in_specs=[pl.BlockSpec((None,...  31.6 us
  transfers between devices with their start and end apart: 94, of which 36 were waited for; matrix products, arithmetic and copies ran while one was open for 5% of the time, Pallas kernels for 36%

profile of v1, /device:TPU:0, one launch (start us, length us, event | category | flops | bytes accessed | tf_op | source)
XLA Modules:
  0.0 1479.8 jit_solution(17639671935327089479)
XLA Ops:
  7.2 23.8 %shard_map.115 = (bf16[1024,1024]{1,0:T(8,128)(2,1)}, bf16[1024,1024]{1,0:T(8,128)(2,1)}, bf16[2,2,1024,256]{3,2,1,0:T(8,128)(2,1)}, bf16[2,2,1024,256]{3,2,1,0:...) custom-call(s32[1]{0:T(128)} %bitcast.2.me_ref, bf16[2,4,512,2048]{3,2,1,0:T(8,128)(2,1)} %refs_6_.17, ...), custom_call_target="tpu_custom_call" | custom-call | flops 12884901888 | bytes 25165824 | tf_op jit(solution)/shard_map/pallas_call | solution.py:136
  40.9 23.5 %collective-permute-done.17 = bf16[2,1024,256]{2,1,0:T(8,128)(2,1)S(1)} collective-permute-done((bf16[2,1024,256]{2,1,0:T(8,128)(2,1)S(1)}, bf16[2,1024,256]{2,1,0:T(8,128)(2,1)S(1)}, u32[]{:S(2)}, u32[]{:S(2)}) %collective-permute-start.17) | collective-permute-done | bytes 1048608 | tf_op jit(solution)/shard_map/ppermute | solution.py:310
  92.1 21.7 %collective-permute-done.20.refs_1_ = bf16[2,1024,256]{2,1,0:T(8,128)(2,1)S(1)} collective-permute-done((bf16[2,1024,256]{2,1,0:T(8,128)(2,1)S(1)}, bf16[2,1024,256]{2,1,0:T(8,128)(2,1)S(1)}, u32[]{:S(2)}, u32[]{:S(2)}) %collective-permute-start.20) | collective-permute-done | bytes 1048608 | tf_op jit(solution)/shard_map/ppermute | solution.py:310
  117.5 24.9 %shard_map.116 = (bf16[1024,1024]{1,0:T(8,128)(2,1)}, bf16[1024,1024]{1,0:T(8,128)(2,1)}, bf16[2,2,1024,256]{3,2,1,0:T(8,128)(2,1)}, bf16[2,2,1024,256]{3,2,1,0:...) custom-call(s32[1]{0:T(128)} %bitcast.2.me_ref, bf16[2,1024,256]{2,1,0:T(8,128)(2,1)} %copy-done.6, ...), custom_call_target="tpu_custom_call" | custom-call | flops 12884901888 | bytes 25165824 | tf_op jit(solution)/shard_map/pallas_call | solution.py:136
  149.9 24.3 %collective-permute-done.24 = bf16[2,1024,256]{2,1,0:T(8,128)(2,1)S(1)} collective-permute-done((bf16[2,1024,256]{2,1,0:T(8,128)(2,1)S(1)}, bf16[2,1024,256]{2,1,0:T(8,128)(2,1)S(1)}, u32[]{:S(2)}, u32[]{:S(2)}) %collective-permute-start.24) | collective-permute-done | bytes 1048608 | tf_op jit(solution)/shard_map/ppermute | solution.py:310
  201.2 21.8 %collective-permute-done.27.refs_1_ = bf16[2,1024,256]{2,1,0:T(8,128)(2,1)} collective-permute-done((bf16[2,1024,256]{2,1,0:T(8,128)(2,1)S(1)}, bf16[2,1024,256]{2,1,0:T(8,128)(2,1)}, u32[]{:S(2)}, u32[]{:S(2)}) %collective-permute-start.27) | collective-permute-done | bytes 1048608 | tf_op jit(solution)/shard_map/ppermute | solution.py:310
  244.6 24.9 %shard_map.117 = (bf16[1024,1024]{1,0:T(8,128)(2,1)}, bf16[1024,1024]{1,0:T(8,128)(2,1)}, bf16[2,2,1024,256]{3,2,1,0:T(8,128)(2,1)}, bf16[2,2,1024,256]{3,2,1,0:...) custom-call(s32[1]{0:T(128)} %bitcast.2.me_ref, bf16[2,1024,256]{2,1,0:T(8,128)(2,1)} %copy-done.5, ...), custom_call_target="tpu_custom_call" | custom-call | flops 12884901888 | bytes 25165824 | tf_op jit(solution)/shard_map/pallas_call | solution.py:136
  269.5 27.5 %collective-permute-done.15 = bf16[1,512,1024]{2,1,0:T(8,128)(2,1)} collective-permute-done((bf16[1,512,1024]{2,1,0:T(8,128)(2,1)}, bf16[1,512,1024]{2,1,0:T(8,128)(2,1)}, u32[]{:S(2)}, u32[]{:S(2)}) %collective-permute-start.15) | collective-permute-done | bytes 1048608 | tf_op jit(solution)/shard_map/ppermute | solution.py:353
  298.4 24.3 %shard_map.118 = (bf16[1024,1024]{1,0:T(8,128)(2,1)}, bf16[1024,1024]{1,0:T(8,128)(2,1)}, bf16[2,2,1024,256]{3,2,1,0:T(8,128)(2,1)}, bf16[2,2,1024,256]{3,2,1,0:...) custom-call(s32[1]{0:T(128)} %bitcast.2.me_ref, bf16[2,4,512,2048]{3,2,1,0:T(8,128)(2,1)} %refs_6_.17, ...), custom_call_target="tpu_custom_call" | custom-call | flops 12884901888 | bytes 25165824 | tf_op jit(solution)/shard_map/pallas_call | solution.py:136
  322.8 24.0 %shard_map.112 = (bf16[1024,1024]{1,0:T(8,128)(2,1)}, bf16[1024,1024]{1,0:T(8,128)(2,1)}, bf16[2,2,1024,256]{3,2,1,0:T(8,128)(2,1)}, bf16[2,2,1024,256]{3,2,1,0:...) custom-call(s32[1]{0:T(128)} %bitcast.2.me_ref, bf16[2,4,512,2048]{3,2,1,0:T(8,128)(2,1)} %refs_6_.17, ...), custom_call_target="tpu_custom_call" | custom-call | flops 12884901888 | bytes 25165824 | tf_op jit(solution)/shard_map/pallas_call | solution.py:136
  347.3 24.3 %shard_map.121 = (bf16[1024,1024]{1,0:T(8,128)(2,1)}, bf16[1024,1024]{1,0:T(8,128)(2,1)}, bf16[2,2,1024,256]{3,2,1,0:T(8,128)(2,1)}, bf16[2,2,1024,256]{3,2,1,0:...) custom-call(s32[1]{0:T(128)} %bitcast.2.me_ref, bf16[2,4,512,2048]{3,2,1,0:T(8,128)(2,1)} %refs_6_.17, ...), custom_call_target="tpu_custom_call" | custom-call | flops 12884901888 | bytes 25165824 | tf_op jit(solution)/shard_map/pallas_call | solution.py:136
  378.7 26.6 %collective-permute-done.31 = bf16[2,1024,256]{2,1,0:T(8,128)(2,1)S(1)} collective-permute-done((bf16[2,1024,256]{2,1,0:T(8,128)(2,1)S(1)}, bf16[2,1024,256]{2,1,0:T(8,128)(2,1)S(1)}, u32[]{:S(2)}, u32[]{:S(2)}) %collective-permute-start.31) | collective-permute-done | bytes 1048608 | tf_op jit(solution)/shard_map/ppermute | solution.py:310
  511.9 25.2 %shard_map.119 = (bf16[1024,1024]{1,0:T(8,128)(2,1)}, bf16[1024,1024]{1,0:T(8,128)(2,1)}, bf16[2,2,1024,256]{3,2,1,0:T(8,128)(2,1)}, bf16[2,2,1024,256]{3,2,1,0:...) custom-call(s32[1]{0:T(128)} %bitcast.2.me_ref, bf16[2,1024,256]{2,1,0:T(8,128)(2,1)} %copy-done.3, ...), custom_call_target="tpu_custom_call" | custom-call | flops 12884901888 | bytes 25165824 | tf_op jit(solution)/shard_map/pallas_call | solution.py:136
  537.6 24.7 %shard_map.113 = (bf16[1024,1024]{1,0:T(8,128)(2,1)}, bf16[1024,1024]{1,0:T(8,128)(2,1)}, bf16[2,2,1024,256]{3,2,1,0:T(8,128)(2,1)}, bf16[2,2,1024,256]{3,2,1,0:...) custom-call(s32[1]{0:T(128)} %bitcast.2.me_ref, bf16[2,1024,256]{2,1,0:T(8,128)(2,1)} %pad_maximum_fusion.refs_0_, ...), custom_call_target="tpu_custom_call" | custom-call | flops 12884901888 | bytes 25165824 | tf_op jit(solution)/shard_map/pallas_call | solution.py:136
  563.4 24.9 %shard_map.122 = (bf16[1024,1024]{1,0:T(8,128)(2,1)}, bf16[1024,1024]{1,0:T(8,128)(2,1)}, bf16[2,2,1024,256]{3,2,1,0:T(8,128)(2,1)}, bf16[2,2,1024,256]{3,2,1,0:...) custom-call(s32[1]{0:T(128)} %bitcast.2.me_ref, bf16[2,1024,256]{2,1,0:T(8,128)(2,1)} %pad_maximum_fusion.6.refs_0_, ...), custom_call_target="tpu_custom_call" | custom-call | flops 12884901888 | bytes 25165824 | tf_op jit(solution)/shard_map/pallas_call | solution.py:136
  596.0 21.7 %collective-permute-done.38 = bf16[2,1024,256]{2,1,0:T(8,128)(2,1)S(1)} collective-permute-done((bf16[2,1024,256]{2,1,0:T(8,128)(2,1)S(1)}, bf16[2,1024,256]{2,1,0:T(8,128)(2,1)S(1)}, u32[]{:S(2)}, u32[]{:S(2)}) %collective-permute-start.38) | collective-permute-done | bytes 1048608 | tf_op jit(solution)/shard_map/ppermute | solution.py:310
  722.2 24.9 %shard_map.120 = (bf16[1024,1024]{1,0:T(8,128)(2,1)}, bf16[1024,1024]{1,0:T(8,128)(2,1)}, bf16[2,2,1024,256]{3,2,1,0:T(8,128)(2,1)}, bf16[2,2,1024,256]{3,2,1,0:...) custom-call(s32[1]{0:T(128)} %bitcast.2.me_ref, bf16[2,1024,256]{2,1,0:T(8,128)(2,1)} %copy-done.4, ...), custom_call_target="tpu_custom_call" | custom-call | flops 12884901888 | bytes 25165824 | tf_op jit(solution)/shard_map/pallas_call | solution.py:136
  747.7 25.0 %shard_map.114 = (bf16[1024,1024]{1,0:T(8,128)(2,1)}, bf16[1024,1024]{1,0:T(8,128)(2,1)}, bf16[2,2,1024,256]{3,2,1,0:T(8,128)(2,1)}, bf16[2,2,1024,256]{3,2,1,0:...) custom-call(s32[1]{0:T(128)} %bitcast.2.me_ref, bf16[2,1024,256]{2,1,0:T(8,128)(2,1)} %pad_maximum_fusion.1.refs_0_, ...), custom_call_target="tpu_custom_call" | custom-call | flops 12884901888 | bytes 25165824 | tf_op jit(solution)/shard_map/pallas_call | solution.py:136
  772.8 25.4 %shard_map.123 = (bf16[1024,1024]{1,0:T(8,128)(2,1)}, bf16[1024,1024]{1,0:T(8,128)(2,1)}, bf16[2,2,1024,256]{3,2,1,0:T(8,128)(2,1)}, bf16[2,2,1024,256]{3,2,1,0:...) custom-call(s32[1]{0:T(128)} %bitcast.2.me_ref, bf16[2,1024,256]{2,1,0:T(8,128)(2,1)} %copy-done.2, ...), custom_call_target="tpu_custom_call" | custom-call | flops 12884901888 | bytes 25165824 | tf_op jit(solution)/shard_map/pallas_call | solution.py:136
  824.1 17.3 %shard_map.136 = f32[1024,1024]{1,0:T(8,128)} custom-call(s32[1]{0:T(128)} %bitcast.63.half_ref, f32[8]{0:T(128)} %multiply_minimum_fusion.clip_ref, bf16[1024,1024]{1,0:T(8,128)(2,1)} %get-tuple-element.147.refs_2_.refs_0_, bf16[1024,1024]{1,0:T(8,128)(2,1)} %get-tuple-element.148.refs_3_.refs_1_, bf16[1024,1024]{1,0:T(8,128)(2,1)} %get-tuple-element.149.refs_4_.refs_2_, ...), custom_call_target="tpu_custom_call" | custom-call | flops 8589934592 | bytes 25165824 | tf_op jit(solution)/shard_map/pallas_call | solution.py:208
  859.9 18.7 %shard_map.135.own_ref = f32[1024,1024]{1,0:T(8,128)} custom-call(s32[1]{0:T(128)} %bitcast.half_ref, f32[8]{0:T(128)} %multiply_minimum_fusion.clip_ref, f32[1]{0:T(128)} %bitcast.62.refs_0_, f32[3,1024,1024]{2,1,0:T(8,128)} %refs_1_.19, bf16[1024,1024]{1,0:T(8,128)(2,1)} %get-tuple-element.147.refs_2_.refs_0_, ...), custom_call_target="tpu_custom_call" | custom-call | flops 8589934592 | bytes 25165824 | tf_op jit(solution)/shard_map/pallas_call | solution.py:208
  925.2 17.5 %shard_map.134 = f32[1024,1024]{1,0:T(8,128)} custom-call(s32[1]{0:T(128)} %bitcast.63.half_ref, f32[8]{0:T(128)} %multiply_minimum_fusion.clip_ref, bf16[1024,1024]{1,0:T(8,128)(2,1)} %get-tuple-element.130.refs_2_.refs_0_, bf16[1024,1024]{1,0:T(8,128)(2,1)} %get-tuple-element.131.refs_3_.refs_1_, bf16[1024,1024]{1,0:T(8,128)(2,1)} %get-tuple-element.132.refs_4_.refs_2_, ...), custom_call_target="tpu_custom_call" | custom-call | flops 8589934592 | bytes 25165824 | tf_op jit(solution)/shard_map/pallas_call | solution.py:208
  948.1 18.5 %shard_map.133.own_ref = f32[1024,1024]{1,0:T(8,128)} custom-call(s32[1]{0:T(128)} %bitcast.half_ref, f32[8]{0:T(128)} %multiply_minimum_fusion.clip_ref, f32[1]{0:T(128)} %bitcast.62.refs_0_, f32[3,1024,1024]{2,1,0:T(8,128)} %refs_1_.19, bf16[1024,1024]{1,0:T(8,128)(2,1)} %get-tuple-element.130.refs_2_.refs_0_, ...), custom_call_target="tpu_custom_call" | custom-call | flops 8589934592 | bytes 25165824 | tf_op jit(solution)/shard_map/pallas_call | solution.py:208
  973.6 16.7 %shard_map.127 = f32[1024,1024]{1,0:T(8,128)} custom-call(s32[1]{0:T(128)} %bitcast.63.half_ref, f32[8]{0:T(128)} %multiply_minimum_fusion.clip_ref, bf16[3,2,4,512,2048]{4,3,2,1,0:T(8,128)(2,1)} %refs_2_.13, bf16[1024,1024]{1,0:T(8,128)(2,1)} %get-tuple-element.119.refs_3_.refs_1_, bf16[1024,1024]{1,0:T(8,128)(2,1)} %get-tuple-element.120.refs_4_.refs_2_, ...), custom_call_target="tpu_custom_call" | custom-call | flops 8589934592 | bytes 25165824 | tf_op jit(solution)/shard_map/pallas_call | solution.py:208
  990.4 17.9 %shard_map.126.own_ref = f32[1024,1024]{1,0:T(8,128)} custom-call(s32[1]{0:T(128)} %bitcast.half_ref, f32[8]{0:T(128)} %multiply_minimum_fusion.clip_ref, f32[1]{0:T(128)} %bitcast.62.refs_0_, f32[3,1024,1024]{2,1,0:T(8,128)} %refs_1_.16, bf16[3,2,4,512,2048]{4,3,2,1,0:T(8,128)(2,1)} %refs_2_.13, bf16[1024,1024]{1,0:T(8,128)(2,1)} %get-tuple-element.119.refs_3_.refs_1_, ...), custom_call_target="tpu_custom_call" | custom-call | flops 8589934592 | bytes 25165824 | tf_op jit(solution)/shard_map/pallas_call | solution.py:208
  1009.3 18.2 %shard_map.124.own_ref = f32[1024,1024]{1,0:T(8,128)} custom-call(s32[1]{0:T(128)} %bitcast.half_ref, f32[8]{0:T(128)} %multiply_minimum_fusion.clip_ref, f32[1]{0:T(128)} %bitcast.62.refs_0_, f32[3,1024,1024]{2,1,0:T(8,128)} %refs_1_.16, bf16[3,2,4,512,2048]{4,3,2,1,0:T(8,128)(2,1)} %refs_2_.13, bf16[1024,1024]{1,0:T(8,128)(2,1)} %get-tuple-element.115.refs_3_.refs_1_, ...), custom_call_target="tpu_custom_call" | custom-call | flops 8589934592 | bytes 25165824 | tf_op jit(solution)/shard_map/pallas_call | solution.py:208
  1047.9 17.8 %shard_map.137 = f32[1024,1024]{1,0:T(8,128)} custom-call(s32[1]{0:T(128)} %bitcast.half_ref, f32[8]{0:T(128)} %multiply_minimum_fusion.clip_ref, f32[1]{0:T(128)} %bitcast.62.refs_0_, f32[3,1024,1024]{2,1,0:T(8,128)} %refs_1_.19, bf16[1024,1024]{1,0:T(8,128)(2,1)} %get-tuple-element.155.refs_2_, bf16[1024,1024]{1,0:T(8,128)(2,1)} %get-tuple-element.156.refs_3_, ...), custom_call_target="tpu_custom_call" | custom-call | flops 8589934592 | bytes 25165824 | tf_op jit(solution)/shard_map/pallas_call | solution.py:208
  1065.7 17.9 %shard_map.128 = f32[1024,1024]{1,0:T(8,128)} custom-call(s32[1]{0:T(128)} %bitcast.half_ref, f32[8]{0:T(128)} %multiply_minimum_fusion.clip_ref, f32[1]{0:T(128)} %bitcast.62.refs_0_, f32[3,1024,1024]{2,1,0:T(8,128)} %refs_1_.16, bf16[3,2,4,512,2048]{4,3,2,1,0:T(8,128)(2,1)} %refs_2_.13, bf16[1024,1024]{1,0:T(8,128)(2,1)} %get-tuple-element.123.refs_3_, ...), custom_call_target="tpu_custom_call" | custom-call | flops 8589934592 | bytes 25165824 | tf_op jit(solution)/shard_map/pallas_call | solution.py:208
  1100.1 31.6 %hidden_again.1 = (bf16[4096,1024]{1,0:T(8,128)(2,1)}, bf16[4096,1024]{1,0:T(8,128)(2,1)}) custom-call(bf16[8,512,1024]{2,1,0:T(8,128)(2,1)} %collective-permute-done.61.u_ref, bf16[8,512,2048]{2,1,0:T(8,128)(2,1)} %all-gather.5.cloned.1.call-done.dz_ref.refs_3_, bf16[3,1024,2048]{2,1,0:T(8,128)(2,1)} %w2_ref.1), custom_call_target="tpu_custom_call" | custom-call | flops 17179869184 | bytes 50331648 | tf_op jit(solution)/shard_map/hidden_again/pallas_call | solution.py:231
  1131.6 274.8 %collective-permute-done.60.clip_ref = f32[8]{0:T(128)S(1)} collective-permute-done((f32[8]{0:T(128)S(1)}, f32[8]{0:T(128)S(1)}, u32[]{:S(2)}, u32[]{:S(2)}) %collective-permute-start.60) | collective-permute-done | bytes 64 | tf_op jit(solution)/shard_map/ppermute | solution.py:389
  1406.9 16.6 %shard_map.129.own_ref = f32[1024,1024]{1,0:T(8,128)} custom-call(s32[1]{0:T(128)} %bitcast.half_ref, f32[8]{0:T(128)} %copy-done.50, f32[1]{0:T(128)} %constant.28.clone.1.refs_0_, f32[1,1024,1024]{2,1,0:T(8,128)} %bitcast.278, bf16[8,512,1024]{2,1,0:T(8,128)(2,1)} %all-gather.3.cloned.1.call-done.refs_2_, bf16[4096,1024]{1,0:T(8,128)(2,1)} %get-tuple-element.129.refs_3_), custom_call_target="tpu_custom_call" | custom-call | flops 8589934592 | bytes 25165824 | tf_op jit(solution)/shard_map/pallas_call | solution.py:208
  1428.2 16.5 %shard_map.138.own_ref = f32[1024,1024]{1,0:T(8,128)} custom-call(s32[1]{0:T(128)} %bitcast.half_ref, f32[8]{0:T(128)} %copy-done.50, f32[1]{0:T(128)} %constant.28.clone.1.refs_0_, f32[1,1024,1024]{2,1,0:T(8,128)} %bitcast.268, bf16[4096,1024]{1,0:T(8,128)(2,1)} %get-tuple-element.159.refs_2_, bf16[8,512,2048]{2,1,0:T(8,128)(2,1)} %all-gather.5.cloned.1.call-done.dz_ref.refs_3_), custom_call_target="tpu_custom_call" | custom-call | flops 8589934592 | bytes 25165824 | tf_op jit(solution)/shard_map/pallas_call | solution.py:208
  (347 shorter events, 499.8 us)
Async XLA Ops:
  7.2 1092.9 %all-gather.5.cloned.1.call-start = ((), (), s32[]{:S(2)}) async-start(), calls=%async_computation.1 | async-start | bytes 18874368 | tf_op jit(solution)/shard_map/all_gather | solution.py:368
  201.2 43.4 %collective-permute-start.28 = (bf16[2,1024,256]{2,1,0:T(8,128)(2,1)S(1)}, bf16[2,1024,256]{2,1,0:T(8,128)(2,1)}, u32[]{:S(2)}, u32[]{:S(2)}) collective-permute-start(bf16[2,1024,256]{2,1,0:T(8,128)(2,1)S(1)} %pad_maximum_fusion.3.refs_0_), channel_id=1, source_target_pairs={{0,1},{1,0},{2,3},{3,2},{4,5},{5,4},{6,7},{7,6},{8,9},{9,8},{10,11... | collective-permute-start | bytes 3145736 | tf_op jit(solution)/shard_map/ppermute | solution.py:310
  226.2 70.8 %collective-permute-start.14 = (bf16[1,512,2048]{2,1,0:T(8,128)(2,1)}, bf16[1,512,2048]{2,1,0:T(8,128)(2,1)S(1)}, u32[]{:S(2)}, u32[]{:S(2)}) collective-permute-start(bf16[1,512,2048]{2,1,0:T(8,128)(2,1)} %constant_dynamic-slice_fusion.1), channel_id=1, source_target_pairs={{0,8},{8,0},{1,9},{9,1},{2,10},{10,2},{3,11},{11,3},{4,12},{12,4},... | collective-permute-start | bytes 6291464 | tf_op jit(solution)/shard_map/ppermute | solution.py:351
  243.6 53.4 %collective-permute-start.15 = (bf16[1,512,1024]{2,1,0:T(8,128)(2,1)}, bf16[1,512,1024]{2,1,0:T(8,128)(2,1)}, u32[]{:S(2)}, u32[]{:S(2)}) collective-permute-start(bf16[1,512,1024]{2,1,0:T(8,128)(2,1)} %constant_dynamic-slice_fusion), channel_id=1, source_target_pairs={{0,8},{8,0},{1,9},{9,1},{2,10},{10,2},{3,11},{11,3},{4,12},{12,4},... | collective-permute-start | bytes 3145736 | tf_op jit(solution)/shard_map/ppermute | solution.py:353
  298.4 1108.0 %all-gather.3.cloned.1.call-start = ((), (), s32[]{:S(2)}) async-start(), calls=%async_computation | async-start | bytes 9437184 | tf_op jit(solution)/shard_map/all_gather | solution.py:369
  322.7 49.1 %collective-permute-start.30 = (bf16[2,2,1024,256]{3,2,1,0:T(8,128)(2,1)}, bf16[2,2,1024,256]{3,2,1,0:T(8,128)(2,1)}, u32[]{:S(2)}, u32[]{:S(2)}) collective-permute-start(bf16[2,2,1024,256]{3,2,1,0:T(8,128)(2,1)} %get-tuple-element.101), channel_id=1, source_target_pairs={{0,1},{1,0},{2,3},{3,2},{4,5},{5,4},{6,7},{7,6},{8,9},{9,8},{10,11... | collective-permute-start | bytes 6291464 | tf_op jit(solution)/shard_map/ppermute | solution.py:310
  377.4 50.1 %collective-permute-start.1 = (bf16[2,1024,256]{2,1,0:T(8,128)(2,1)S(1)}, bf16[2,1024,256]{2,1,0:T(8,128)(2,1)S(1)}, u32[]{:S(2)}, u32[]{:S(2)}) collective-permute-start(bf16[2,1024,256]{2,1,0:T(8,128)(2,1)S(1)} %get-tuple-element.172), channel_id=1, source_target_pairs={{0,2},{1,3},{2,0},{3,1},{4,6},{5,7},{6,4},{7,5},{8,10},{9,11},{10,... | collective-permute-start | bytes 3145736 | tf_op jit(solution)/shard_map/ppermute | solution.py:310
  454.0 39.8 %collective-permute-start.34 = (bf16[2,1024,256]{2,1,0:T(8,128)(2,1)S(1)}, bf16[2,1024,256]{2,1,0:T(8,128)(2,1)S(1)}, u32[]{:S(2)}, u32[]{:S(2)}) collective-permute-start(bf16[2,1024,256]{2,1,0:T(8,128)(2,1)S(1)} %pad_maximum_fusion.4.refs_0_), channel_id=1, source_target_pairs={{0,2},{1,3},{2,0},{3,1},{4,6},{5,7},{6,4},{7,5},{8,10},{9,11},{10,... | collective-permute-start | bytes 3145736 | tf_op jit(solution)/shard_map/ppermute | solution.py:310
  493.8 43.8 %collective-permute-start.5 = (bf16[2,1024,256]{2,1,0:T(8,128)(2,1)}, bf16[2,1024,256]{2,1,0:T(8,128)(2,1)}, u32[]{:S(2)}, u32[]{:S(2)}) collective-permute-start(bf16[2,1024,256]{2,1,0:T(8,128)(2,1)} %pad_maximum_fusion.refs_0_), channel_id=1, source_target_pairs={{0,1},{1,0},{2,3},{3,2},{4,5},{5,4},{6,7},{7,6},{8,9},{9,8},{10,11... | collective-permute-start | bytes 3145736 | tf_op jit(solution)/shard_map/ppermute | solution.py:310
  494.8 67.6 %collective-permute-start.49 = (bf16[2,1024,256]{2,1,0:T(8,128)(2,1)}, bf16[2,1024,256]{2,1,0:T(8,128)(2,1)S(1)}, u32[]{:S(2)}, u32[]{:S(2)}) collective-permute-start(bf16[2,1024,256]{2,1,0:T(8,128)(2,1)} %pad_maximum_fusion.6.refs_0_), channel_id=1, source_target_pairs={{0,1},{1,0},{2,3},{3,2},{4,5},{5,4},{6,7},{7,6},{8,9},{9,8},{10,11... | collective-permute-start | bytes 3145736 | tf_op jit(solution)/shard_map/ppermute | solution.py:310
  510.9 51.5 %collective-permute-start.50 = (bf16[2,1024,256]{2,1,0:T(8,128)(2,1)}, bf16[2,1024,256]{2,1,0:T(8,128)(2,1)}, u32[]{:S(2)}, u32[]{:S(2)}) collective-permute-start(bf16[2,1024,256]{2,1,0:T(8,128)(2,1)} %collective-permute-done.48.refs_1_), channel_id=1, source_target_pairs={{0,1},{1,0},{2,3},{3,2},{4,5},{5,4},{6,7},{7,6},{8,9},{9,8},{10,11... | collective-permute-start | bytes 3145736 | tf_op jit(solution)/shard_map/ppermute | solution.py:310
  537.1 51.7 %collective-permute-start.37 = (bf16[2,2,1024,256]{3,2,1,0:T(8,128)(2,1)}, bf16[2,2,1024,256]{3,2,1,0:T(8,128)(2,1)}, u32[]{:S(2)}, u32[]{:S(2)}) collective-permute-start(bf16[2,2,1024,256]{3,2,1,0:T(8,128)(2,1)} %get-tuple-element.104), channel_id=1, source_target_pairs={{0,1},{1,0},{2,3},{3,2},{4,5},{5,4},{6,7},{7,6},{8,9},{9,8},{10,11... | collective-permute-start | bytes 6291464 | tf_op jit(solution)/shard_map/ppermute | solution.py:310
  594.5 44.7 %collective-permute-start.8 = (bf16[2,1024,256]{2,1,0:T(8,128)(2,1)S(1)}, bf16[2,1024,256]{2,1,0:T(8,128)(2,1)S(1)}, u32[]{:S(2)}, u32[]{:S(2)}) collective-permute-start(bf16[2,1024,256]{2,1,0:T(8,128)(2,1)S(1)} %get-tuple-element.170), channel_id=1, source_target_pairs={{0,2},{1,3},{2,0},{3,1},{4,6},{5,7},{6,4},{7,5},{8,10},{9,11},{10,... | collective-permute-start | bytes 3145736 | tf_op jit(solution)/shard_map/ppermute | solution.py:310
  666.4 39.2 %collective-permute-start.41 = (bf16[2,1024,256]{2,1,0:T(8,128)(2,1)S(1)}, bf16[2,1024,256]{2,1,0:T(8,128)(2,1)S(1)}, u32[]{:S(2)}, u32[]{:S(2)}) collective-permute-start(bf16[2,1024,256]{2,1,0:T(8,128)(2,1)S(1)} %pad_maximum_fusion.5.refs_0_), channel_id=1, source_target_pairs={{0,2},{1,3},{2,0},{3,1},{4,6},{5,7},{6,4},{7,5},{8,10},{9,11},{10,... | collective-permute-start | bytes 3145736 | tf_op jit(solution)/shard_map/ppermute | solution.py:310
  705.7 41.6 %collective-permute-start.12 = (bf16[2,1024,256]{2,1,0:T(8,128)(2,1)}, bf16[2,1024,256]{2,1,0:T(8,128)(2,1)}, u32[]{:S(2)}, u32[]{:S(2)}) collective-permute-start(bf16[2,1024,256]{2,1,0:T(8,128)(2,1)} %pad_maximum_fusion.1.refs_0_), channel_id=1, source_target_pairs={{0,1},{1,0},{2,3},{3,2},{4,5},{5,4},{6,7},{7,6},{8,9},{9,8},{10,11... | collective-permute-start | bytes 3145736 | tf_op jit(solution)/shard_map/ppermute | solution.py:310
  706.2 66.6 %collective-permute-start.56 = (bf16[2,1024,256]{2,1,0:T(8,128)(2,1)S(1)}, bf16[2,1024,256]{2,1,0:T(8,128)(2,1)}, u32[]{:S(2)}, u32[]{:S(2)}) collective-permute-start(bf16[2,1024,256]{2,1,0:T(8,128)(2,1)S(1)} %pad_maximum_fusion.7.refs_0_), channel_id=1, source_target_pairs={{0,1},{1,0},{2,3},{3,2},{4,5},{5,4},{6,7},{7,6},{8,9},{9,8},{10,11... | collective-permute-start | bytes 3145736 | tf_op jit(solution)/shard_map/ppermute | solution.py:310
  720.7 52.1 %collective-permute-start.57 = (bf16[2,1024,256]{2,1,0:T(8,128)(2,1)}, bf16[2,1024,256]{2,1,0:T(8,128)(2,1)}, u32[]{:S(2)}, u32[]{:S(2)}) collective-permute-start(bf16[2,1024,256]{2,1,0:T(8,128)(2,1)} %collective-permute-done.55.refs_1_), channel_id=1, source_target_pairs={{0,1},{1,0},{2,3},{3,2},{4,5},{5,4},{6,7},{7,6},{8,9},{9,8},{10,11... | collective-permute-start | bytes 3145736 | tf_op jit(solution)/shard_map/ppermute | solution.py:310
  747.2 94.2 %collective-permute-start.76 = (bf16[2,2,1024,256]{3,2,1,0:T(8,128)(2,1)}, bf16[2,2,1024,256]{3,2,1,0:T(8,128)(2,1)}, u32[]{:S(2)}, u32[]{:S(2)}) collective-permute-start(bf16[2,2,1024,256]{3,2,1,0:T(8,128)(2,1)} %get-tuple-element.143), channel_id=1, source_target_pairs={{0,1},{1,0},{2,3},{3,2},{4,5},{5,4},{6,7},{7,6},{8,9},{9,8},{10,11... | collective-permute-start | bytes 6291464 | tf_op jit(solution)/shard_map/ppermute | solution.py:310
  747.2 97.9 %collective-permute-start.69 = (bf16[2,2,1024,256]{3,2,1,0:T(8,128)(2,1)}, bf16[2,2,1024,256]{3,2,1,0:T(8,128)(2,1)}, u32[]{:S(2)}, u32[]{:S(2)}) collective-permute-start(bf16[2,2,1024,256]{3,2,1,0:T(8,128)(2,1)} %get-tuple-element.141), channel_id=1, source_target_pairs={{0,1},{1,0},{2,3},{3,2},{4,5},{5,4},{6,7},{7,6},{8,9},{9,8},{10,11... | collective-permute-start | bytes 6291464 | tf_op jit(solution)/shard_map/ppermute | solution.py:310
  772.7 77.1 %collective-permute-start.62 = (bf16[2,2,1024,256]{3,2,1,0:T(8,128)(2,1)}, bf16[2,2,1024,256]{3,2,1,0:T(8,128)(2,1)}, u32[]{:S(2)}, u32[]{:S(2)}) collective-permute-start(bf16[2,2,1024,256]{3,2,1,0:T(8,128)(2,1)} %get-tuple-element.139), channel_id=1, source_target_pairs={{0,1},{1,0},{2,3},{3,2},{4,5},{5,4},{6,7},{7,6},{8,9},{9,8},{10,11... | collective-permute-start | bytes 6291464 | tf_op jit(solution)/shard_map/ppermute | solution.py:310
  798.2 56.7 %collective-permute-start.83 = (bf16[2,2,1024,256]{3,2,1,0:T(8,128)(2,1)}, bf16[2,2,1024,256]{3,2,1,0:T(8,128)(2,1)}, u32[]{:S(2)}, u32[]{:S(2)}) collective-permute-start(bf16[2,2,1024,256]{3,2,1,0:T(8,128)(2,1)} %get-tuple-element.145), channel_id=1, source_target_pairs={{0,1},{1,0},{2,3},{3,2},{4,5},{5,4},{6,7},{7,6},{8,9},{9,8},{10,11... | collective-permute-start | bytes 6291464 | tf_op jit(solution)/shard_map/ppermute | solution.py:310
  806.5 292.7 %collective-permute-start.61 = (bf16[8,512,1024]{2,1,0:T(8,128)(2,1)}, bf16[8,512,1024]{2,1,0:T(8,128)(2,1)}, u32[]{:S(2)}, u32[]{:S(2)}) collective-permute-start(bf16[8,512,1024]{2,1,0:T(8,128)(2,1)} %bitcast.269), channel_id=1, source_target_pairs={{0,8},{8,0},{1,9},{9,1},{2,10},{10,2},{3,11},{11,3},{4,12},{12,4},... | collective-permute-start | bytes 25165832 | tf_op jit(solution)/shard_map/ppermute | solution.py:352
  853.4 40.6 %collective-permute-start.63 = (bf16[2,1024,256]{2,1,0:T(8,128)(2,1)}, bf16[2,1024,256]{2,1,0:T(8,128)(2,1)}, u32[]{:S(2)}, u32[]{:S(2)}) collective-permute-start(bf16[2,1024,256]{2,1,0:T(8,128)(2,1)} %get-tuple-element.168), channel_id=1, source_target_pairs={{0,2},{1,3},{2,0},{3,1},{4,6},{5,7},{6,4},{7,5},{8,10},{9,11},{10,... | collective-permute-start | bytes 3145736 | tf_op jit(solution)/shard_map/ppermute | solution.py:310
  858.4 39.2 %collective-permute-start.84 = (bf16[2,1024,256]{2,1,0:T(8,128)(2,1)}, bf16[2,1024,256]{2,1,0:T(8,128)(2,1)}, u32[]{:S(2)}, u32[]{:S(2)}) collective-permute-start(bf16[2,1024,256]{2,1,0:T(8,128)(2,1)} %get-tuple-element.162), channel_id=1, source_target_pairs={{0,4},{1,5},{2,6},{3,7},{4,0},{5,1},{6,2},{7,3},{8,12},{9,13},{10,... | collective-permute-start | bytes 3145736 | tf_op jit(solution)/shard_map/ppermute | solution.py:310
  970.6 37.7 %collective-permute-start.67 = (bf16[2,1024,256]{2,1,0:T(8,128)(2,1)S(1)}, bf16[2,1024,256]{2,1,0:T(8,128)(2,1)}, u32[]{:S(2)}, u32[]{:S(2)}) collective-permute-start(bf16[2,1024,256]{2,1,0:T(8,128)(2,1)S(1)} %pad_maximum_fusion.8.refs_0_), channel_id=1, source_target_pairs={{0,1},{1,0},{2,3},{3,2},{4,5},{5,4},{6,7},{7,6},{8,9},{9,8},{10,11... | collective-permute-start | bytes 3145736 | tf_op jit(solution)/shard_map/ppermute | solution.py:310
  970.6 37.7 %collective-permute-start.66 = (bf16[2,1024,256]{2,1,0:T(8,128)(2,1)S(1)}, bf16[2,1024,256]{2,1,0:T(8,128)(2,1)S(1)}, u32[]{:S(2)}, u32[]{:S(2)}) collective-permute-start(bf16[2,1024,256]{2,1,0:T(8,128)(2,1)S(1)} %pad_maximum_fusion.8.refs_0_), channel_id=1, source_target_pairs={{0,2},{1,3},{2,0},{3,1},{4,6},{5,7},{6,4},{7,5},{8,10},{9,11},{10,... | collective-permute-start | bytes 3145736 | tf_op jit(solution)/shard_map/ppermute | solution.py:310
  1008.9 37.7 %collective-permute-start.89 = (bf16[2,1024,256]{2,1,0:T(8,128)(2,1)S(1)}, bf16[2,1024,256]{2,1,0:T(8,128)(2,1)}, u32[]{:S(2)}, u32[]{:S(2)}) collective-permute-start(bf16[2,1024,256]{2,1,0:T(8,128)(2,1)S(1)} %collective-permute-done.87.refs_13_), channel_id=1, source_target_pairs={{0,1},{1,0},{2,3},{3,2},{4,5},{5,4},{6,7},{7,6},{8,9},{9,8},{10,11... | collective-permute-start | bytes 3145736 | tf_op jit(solution)/shard_map/ppermute | solution.py:310
  1043.8 411.5 %collective-permute-start.58 = (f32[1024,1024]{1,0:T(8,128)}, f32[1024,1024]{1,0:T(8,128)}, u32[]{:S(2)}, u32[]{:S(2)}) collective-permute-start(f32[1024,1024]{1,0:T(8,128)} %shard_map.125), channel_id=1, source_target_pairs={{0,8},{8,0},{1,9},{9,1},{2,10},{10,2},{3,11},{11,3},{4,12},{12,4},... | collective-permute-start | bytes 12582920 | tf_op jit(solution)/shard_map/ppermute | solution.py:387
  1044.5 405.0 %collective-permute-start.59 = (f32[1024,1024]{1,0:T(8,128)}, f32[1024,1024]{1,0:T(8,128)}, u32[]{:S(2)}, u32[]{:S(2)}) collective-permute-start(f32[1024,1024]{1,0:T(8,128)} %shard_map.127), channel_id=1, source_target_pairs={{0,8},{8,0},{1,9},{9,1},{2,10},{10,2},{3,11},{11,3},{4,12},{12,4},... | collective-permute-start | bytes 12582920 | tf_op jit(solution)/shard_map/ppermute | solution.py:387
  1045.8 420.9 %collective-permute-start.90 = (f32[1024,1024]{1,0:T(8,128)}, f32[1024,1024]{1,0:T(8,128)}, u32[]{:S(2)}, u32[]{:S(2)}) collective-permute-start(f32[1024,1024]{1,0:T(8,128)} %shard_map.134), channel_id=1, source_target_pairs={{0,8},{8,0},{1,9},{9,1},{2,10},{10,2},{3,11},{11,3},{4,12},{12,4},... | collective-permute-start | bytes 12582920 | tf_op jit(solution)/shard_map/ppermute | solution.py:387
  1046.6 414.4 %collective-permute-start.91 = (f32[1024,1024]{1,0:T(8,128)}, f32[1024,1024]{1,0:T(8,128)}, u32[]{:S(2)}, u32[]{:S(2)}) collective-permute-start(f32[1024,1024]{1,0:T(8,128)} %shard_map.136), channel_id=1, source_target_pairs={{0,8},{8,0},{1,9},{9,1},{2,10},{10,2},{3,11},{11,3},{4,12},{12,4},... | collective-permute-start | bytes 12582920 | tf_op jit(solution)/shard_map/ppermute | solution.py:387
  1099.3 307.1 %collective-permute-start.60 = (f32[8]{0:T(128)S(1)}, f32[8]{0:T(128)S(1)}, u32[]{:S(2)}, u32[]{:S(2)}) collective-permute-start(f32[8]{0:T(128)S(1)} %copy-done.45), channel_id=1, source_target_pairs={{0,8},{8,0},{1,9},{9,1},{2,10},{10,2},{3,11},{11,3},{4,12},{12,4},... | collective-permute-start | bytes 104 | tf_op jit(solution)/shard_map/ppermute | solution.py:389
  (113 other events, 2258.5 us)
Sparse Core Ops, SparseCore 0:
  298.5 91.2 all-gather.4
  772.9 51.0 all-gather.2

commit v2 on v1

--- a/solution.py
+++ b/solution.py
@@ -159,64 +159,133 @@
     )(me, *operands, u_pre, w_up, w_down, x_in)
 
 
-def grad_kernel(sizes, half_ref, clip_ref, *refs):
-    n_lhs, n_rhs, per, has_init = sizes
-    if has_init:
-        scale_ref, init_ref, *refs = refs
-    lhs, rhs, out_ref = refs[:n_lhs], refs[n_lhs:-1], refs[-1]
+def grad_kernel(segs, n_lhs, n_rhs, init_layer, has_init, has_got, inv, half_ref, clip_ref, *refs):
+    refs = list(refs)
+    scale_ref = refs.pop(0) if has_init else None
+    lhs = [refs.pop(0) for _ in range(n_lhs)]
+    rhs = [refs.pop(0) for _ in range(n_rhs)]
+    init = refs.pop(0) if has_init else None
+    got = refs.pop(0) if has_got else None
+    out_ref, a_buf, b_buf, a_sem, b_sem, *extra = refs[-5 - 2 * (has_init + has_got) :]
+    init_buf, init_sem = extra[:2] if has_init else (None, None)
+    got_buf, got_sem = extra[-2:] if has_got else (None, None)
+    half = half_ref[0]
     step = pl.program_id(0)
+    n_steps = pl.num_programs(0)
+
+    def view(ref, kind, e):
+        layer, cols = kind
+        cols = pl.ds(pl.multiple_of(half * HALF, HALF), HALF) if cols else pl.ds(0, 1024)
+        if layer is not None:
+            return ref.at[layer, e // 4, e % 4, :, cols]
+        if len(ref.shape) == 4:
+            return ref.at[e // 4, e % 4, :, cols]
+        if len(ref.shape) == 3:
+            return ref.at[e, :, cols]
+        return ref.at[pl.ds(pl.multiple_of(e * 512, 512), 512), cols]
+
+    def fetch(at, slot):
+        for start, count, left, left_kind, left_first, right, right_kind, right_first in segs:
+
+            @pl.when(jnp.logical_and(at >= start, at < start + count))
+            def _():
+                e = at - start
+                pltpu.make_async_copy(view(lhs[left], left_kind, e + left_first), a_buf.at[slot], a_sem.at[slot]).start()
+                pltpu.make_async_copy(view(rhs[right], right_kind, e + right_first), b_buf.at[slot], b_sem.at[slot]).start()
+
+    slot = step % 2
 
     @pl.when(step == 0)
     def _():
-        out_ref[...] = scale_ref[0] * init_ref[...] if has_init else jnp.zeros_like(out_ref)
-
-    clip = clip_ref[step]
-    for k in range(max(n_lhs, n_rhs)):
-
-        @pl.when(step // per == k)
-        def _(k=k):
-            a = lhs[min(k, n_lhs - 1)]
-            b = rhs[min(k, n_rhs - 1)]
-            scaled = (b[...].astype(jnp.float32) * clip).astype(jnp.bfloat16)
-            for j in range(2):
-                cols = slice(j * 512, (j + 1) * 512)
-                out_ref[:, cols] += dot(a[...], scaled[:, cols], TN)
-
-
-def grad_operand(value, layer, per, columns):
-    def col(h):
-        return 0 if columns is None else h[0]
-
-    if isinstance(value, tuple):
-        return value, [
-            pl.BlockSpec((512, 1024), lambda s, h, k=k: (jnp.clip(s - per * k, 0, per - 1), col(h))) for k in range(len(value))
-        ]
-    lead = {5: lambda s: (layer, s // 4, s % 4), 4: lambda s: (s // 4, s % 4), 3: lambda s: (s,)}[value.ndim]
-    return (value,), [pl.BlockSpec((None,) * (value.ndim - 2) + (512, 1024), lambda s, h: (*lead(s), 0, col(h)))]
-
-
-def weight_grad(layer, half, clip, lhs, rhs, lhs_half, rhs_half, init=None, init_layer=0, scale=None):
-    parts = max(len(v) if isinstance(v, tuple) else 1 for v in (lhs, rhs))
-    n_ex = clip.shape[0]
-    per = n_ex // parts
-    lhs, lhs_specs = grad_operand(lhs, layer, per, lhs_half)
-    rhs, rhs_specs = grad_operand(rhs, layer, per, rhs_half)
-    lead, lead_specs = (), []
+        fetch(0, 0)
+        out_ref[...] = jnp.zeros_like(out_ref)
+
+    @pl.when(step + 1 < n_steps)
+    def _():
+        fetch(step + 1, 1 - slot)
+
+    @pl.when(step == 1)
+    def _():
+        if has_init:
+            pltpu.make_async_copy(init.at[init_layer], init_buf, init_sem).start()
+        if has_got:
+            pltpu.make_async_copy(got, got_buf, got_sem).start()
+
+    pltpu.make_async_copy(a_buf.at[slot], a_buf.at[slot], a_sem.at[slot]).wait()
+    pltpu.make_async_copy(b_buf.at[slot], b_buf.at[slot], b_sem.at[slot]).wait()
+    scaled = (b_buf[slot].astype(jnp.float32) * clip_ref[step]).astype(jnp.bfloat16)
+    for j in range(2):
+        cols = slice(j * 512, (j + 1) * 512)
+        out_ref[:, cols] += dot(a_buf[slot], scaled[:, cols], TN)
+
+    if has_init or has_got:
+
+        @pl.when(step == n_steps - 1)
+        def _():
+            total = out_ref[...]
+            if has_init:
+                pltpu.make_async_copy(init.at[init_layer], init_buf, init_sem).wait()
+                total = total + scale_ref[0] * init_buf[...]
+            if has_got:
+                pltpu.make_async_copy(got, got_buf, got_sem).wait()
+                total = total + got_buf[...]
+            out_ref[...] = total * inv if inv is not None else total
+
+
+def weight_grad(half, clip, segs, init=None, got=None, inv=None, result=None):
+    lhs, rhs, table, at = [], [], [], 0
+
+    def place(group, value):
+        for i, other in enumerate(group):
+            if other is value:
+                return i
+        group.append(value)
+        return len(group) - 1
+
+    for count, (a, a_layer, a_half, a_first), (b, b_layer, b_half, b_first) in segs:
+        left, right = place(lhs, a), place(rhs, b)
+        table.append((at, count, left, (a_layer, a_half), a_first, right, (b_layer, b_half), b_first))
+        at += count
+    any_spec = pl.BlockSpec(memory_space=pl.ANY)
+    smem_spec = pl.BlockSpec(memory_space=pltpu.SMEM)
+    operands, in_specs = [clip], [smem_spec]
+    scratch = [
+        pltpu.VMEM((2, 512, 1024), jnp.bfloat16),
+        pltpu.VMEM((2, 512, 1024), jnp.bfloat16),
+        pltpu.SemaphoreType.DMA((2,)),
+        pltpu.SemaphoreType.DMA((2,)),
+    ]
     if init is not None:
-        lead = (scale, init)
-        lead_specs = [pl.BlockSpec(memory_space=pltpu.SMEM), pl.BlockSpec((None, 1024, 1024), lambda s, h: (init_layer, 0, 0))]
+        operands.append(init[2])
+        in_specs.append(smem_spec)
+    operands += lhs + rhs
+    in_specs += [any_spec] * (len(lhs) + len(rhs))
+    for value in (init[0] if init is not None else None, got):
+        if value is not None:
+            operands.append(value)
+            in_specs.append(any_spec)
+            scratch += [pltpu.VMEM((1024, 1024), jnp.float32), pltpu.SemaphoreType.DMA]
+    aliases = {}
+    out_spec, out_shape = pl.BlockSpec((1024, 1024), lambda s, h: (0, 0)), (1024, 1024)
+    if result is not None:
+        out_layer, n_layers, buffer = result
+        out_spec, out_shape = pl.BlockSpec((None, 1024, 1024), lambda s, h: (out_layer, 0, 0)), (n_layers, 1024, 1024)
+        if buffer is not None:
+            aliases = {len(operands) + 1: 0}
+            operands.append(buffer)
+            in_specs.append(any_spec)
     return pl.pallas_call(
-        functools.partial(grad_kernel, (len(lhs), len(rhs), per, init is not None)),
+        functools.partial(
+            grad_kernel, table, len(lhs), len(rhs), init[1] if init is not None else 0, init is not None, got is not None, inv
+        ),
         grid_spec=pltpu.PrefetchScalarGridSpec(
-            num_scalar_prefetch=1,
-            grid=(n_ex,),
-            in_specs=[pl.BlockSpec(memory_space=pltpu.SMEM)] + lead_specs + lhs_specs + rhs_specs,
-            out_specs=pl.BlockSpec((1024, 1024), lambda s, h: (0, 0)),
+            num_scalar_prefetch=1, grid=(at,), in_specs=in_specs, out_specs=out_spec, scratch_shapes=scratch
         ),
-        out_shape=jax.ShapeDtypeStruct((1024, 1024), jnp.float32),
+        out_shape=jax.ShapeDtypeStruct(out_shape, jnp.float32),
+        input_output_aliases=aliases,
         compiler_params=pltpu.CompilerParams(dimension_semantics=("arbitrary",)),
-        cost_estimate=pl.CostEstimate(flops=2 * n_ex * 512 * 1024 * 1024, bytes_accessed=24 << 20, transcendentals=0),
-    )(half, clip, *lead, *lhs, *rhs)
+        cost_estimate=pl.CostEstimate(flops=2 * at * 512 * 1024 * 1024, bytes_accessed=24 << 20, transcendentals=0),
+    )(half, *operands)
 
 
 def hidden_kernel(u_ref, dz_ref, w2_ref, h_ref, dh_ref):
@@ -344,10 +413,9 @@
         top = n_layers - 1
         swap_dp = [(i, 1 - i) for i in range(dp_size)]
         ex_all = micro * per_micro
-        cot_slice = lax.dynamic_index_in_dim(d_out.reshape(ex_all, *d_out.shape[2:]), me, 0)
-        x_slice = lax.dynamic_slice(
-            x_in[top].reshape(ex_all, *d_out.shape[2:]), (me, 0, (1 - my_dp) * HALF), (1, d_out.shape[2], HALF)
-        )
+        ex_m, ex_e = me // per_micro, me % per_micro
+        cot_slice = lax.dynamic_slice(d_out, (ex_m, ex_e, 0, 0), (1, 1, *d_out.shape[2:]))[0]
+        x_slice = lax.dynamic_slice(x_in, (top, ex_m, ex_e, 0, (1 - my_dp) * HALF), (1, 1, 1, d_out.shape[2], HALF))[0, 0]
         cot_other = lax.ppermute(cot_slice, "dp", swap_dp)
         u_other = lax.ppermute(u_pre[top].reshape(ex_all, *u_pre.shape[3:]), "dp", swap_dp)
         x_other = lax.ppermute(x_slice, "dp", swap_dp)
@@ -376,28 +444,45 @@
         top = n_layers - 1
         grads = [(up, layer) for layer in reversed(range(top)) for up in (True, False)]
 
-        def grad(up, layer, half, *init):
+        def own_segs(up, layer):
             hids, dhids, full = saved[layer]
-            lhs, rhs = (x_in, dhids) if up else (hids, full)
-            return weight_grad(layer, half, clip, lhs, rhs, True if up else None, None if up else True, *init)
+            segs = []
+            for k, (m, e) in enumerate(chunks):
+                if up:
+                    segs.append((PER_CHUNK, (x_in, layer, True, m * per_micro + e), (dhids[k], None, False, 0)))
+                elif isinstance(full, tuple):
+                    segs.append((PER_CHUNK, (hids[k], None, False, 0), (full[k], None, True, 0)))
+                else:
+                    segs.append((PER_CHUNK, (hids[k], None, False, 0), (full, None, True, m * per_micro + e)))
+            return segs
+
+        def grad(half, clips, segs, *rest):
+            return weight_grad(half, clips, segs, *rest)
+
+        def noise_of(up, layer):
+            return (noise_up if up else noise_down, layer, noise_scale)
 
         got = []
         for up, layer in grads:
-            part = grad(up, layer, other_half)
+            part = grad(other_half, clip, own_segs(up, layer))
             got.append(lax.ppermute(part, "dp", swap_dp))
         result = [None, None]
-        clip_other = lax.ppermute(clip, "dp", swap_dp)
-        one = jnp.ones((1,), jnp.float32)
+        clip_all = jnp.concatenate([clip, lax.ppermute(clip, "dp", swap_dp)])
+        inv = 1.0 / examples
         for up in (True, False):
-            own = grad(up, top, own_half, noise_up if up else noise_down, top, noise_scale)[None]
-            lhs, rhs = (x_other, (dhid_other,)) if up else ((hid_other,), cot_other)
-            own = weight_grad(top, own_half, clip_other, lhs, rhs, None, None if up else True, own, 0, one)
-            result[up] = finish_grad(top, n_layers, examples, own, None, None)
+            rest = ((x_other, None, False, 0), (dhid_other, None, False, 0)) if up else ((hid_other, None, False, 0), (cot_other, None, True, 0))
+            segs = own_segs(up, top) + [(ex_all, *rest)]
+            result[up] = grad(own_half, clip_all, segs, noise_of(up, top), None, inv, (top, n_layers, None))
         for i, (up, layer) in enumerate(grads):
-            own = grad(up, layer, own_half, noise_up if up else noise_down, layer, noise_scale)
-            if i == len(grads) - 1:
-                own, d_in = lax.optimization_barrier((own, d_in))
-            result[up] = finish_grad(layer, n_layers, examples, own, got[i], result[up])
+            last = i == len(grads) - 1
+            if last:
+                own = grad(own_half, clip, own_segs(up, layer), noise_of(up, layer))
+            else:
+                result[up] = grad(
+                    own_half, clip, own_segs(up, layer), noise_of(up, layer), got[i], inv, (layer, n_layers, result[up])
+                )
+        own, d_in = lax.optimization_barrier((own, d_in))
+        result[up] = finish_grad(layer, n_layers, examples, own, got[-1], result[up])
         return result[1], result[0], d_in
 
     in_specs = (P(None, None, "dp", None, None), P(None, None, "dp", None, "tp"), P(None, None, "tp"), P(None, "tp", None), P(None, "dp", None, None), P(None, "dp", "tp"), P(None, "tp", "dp"), P(), P())

time: 1490 us -> 1500 us (level)
  waiting for transfers between devices: 704 us -> 783 us
  Pallas kernels: 586 us -> 542 us
  local copies, waits for them, and re-layouts: 34.6 us -> 17.2 us
  other arithmetic: 54.7 us -> 39.6 us
    ppermute x1, waiting for transfers between devices: 275 us -> 58.9 us  [local_pass(): clip_all = jnp.concatenate([clip, lax.ppermute(clip, 'dp', swap_dp)])]
    ppermute x4, waiting for transfers between devices: 0.01 us -> 184 us  [local_pass(): got.append(lax.ppermute(part, 'dp', swap_dp))]
    ppermute x84, waiting for transfers between devices: 402 us -> 499 us  [swap(): return lax.ppermute(value, 'tp', [(i, i ^ mask) for i in range(tp_size)])]
    pallas_call x6 -> x1, Pallas kernels: 32.4 us -> 5.76 us  [finish_grad(): pl.pallas_call(functools.partial(finish_kernel, 1.0 / examples, got is no...]
    pallas_call x12 -> x10, Pallas kernels: 210 us -> 193 us  [weight_grad(): pl.pallas_call(functools.partial(grad_kernel, table, len(lhs), len(rhs),...]
  transfers between devices with their start and end apart: 94 -> 94, of which waited for: 36 -> 37; matrix products, arithmetic and copies ran while one was open for 5% -> 3% of each run, Pallas kernels for 36% -> 33%
where the time goes in v2:
time: 1500 us; the launch traced here: 1490 us
  waiting for transfers between devices  783 us (52%)
  Pallas kernels  542 us (36%)
  starting transfers between devices  74 us (5%)
  other arithmetic  39.6 us (3%)
  blocking collectives  19.6 us (1%)
  local copies, waits for them, and re-layouts  17.2 us (1%)
  between operations  16.7 us (1%)
    ppermute x84, waiting for transfers between devices, swap(): return lax.ppermute(value, 'tp', [(i, i ^ mask) for i in range(tp_size)])  499 us
    pallas_call x12, Pallas kernels, backward_chunk(): pl.pallas_call(functools.partial(backward_kernel, layer, micro, first_ex,...  296 us
    pallas_call x10, Pallas kernels, weight_grad(): pl.pallas_call(functools.partial(grad_kernel, table, len(lhs), len(rhs),...  193 us
    ppermute x4, waiting for transfers between devices, local_pass(): got.append(lax.ppermute(part, 'dp', swap_dp))  184 us
    ppermute x84, starting transfers between devices, swap(): return lax.ppermute(value, 'tp', [(i, i ^ mask) for i in range(tp_size)])  64.5 us
    ppermute x1, waiting for transfers between devices, local_pass(): clip_all = jnp.concatenate([clip, lax.ppermute(clip, 'dp', swap_dp)])  58.9 us
    ppermute x1, waiting for transfers between devices, local_pass(): x_other = lax.ppermute(x_slice, 'dp', swap_dp)  41.4 us
    pallas_call x1, Pallas kernels, hidden_again(): pl.pallas_call(hidden_kernel, grid=(n_ex,), in_specs=[pl.BlockSpec((None,...  31.6 us
  transfers between devices with their start and end apart: 94, of which 37 were waited for; matrix products, arithmetic and copies ran while one was open for 3% of the time, Pallas kernels for 33%

profile of v2, /device:TPU:0, one launch (start us, length us, event | category | flops | bytes accessed | tf_op | source)
XLA Modules:
  0.0 1492.7 jit_solution(8397830730142860699)
XLA Ops:
  7.2 23.8 %shard_map.115 = (bf16[1024,1024]{1,0:T(8,128)(2,1)}, bf16[1024,1024]{1,0:T(8,128)(2,1)}, bf16[2,2,1024,256]{3,2,1,0:T(8,128)(2,1)}, bf16[2,2,1024,256]{3,2,1,0:...) custom-call(s32[1]{0:T(128)} %bitcast.2.me_ref, bf16[2,4,512,2048]{3,2,1,0:T(8,128)(2,1)} %refs_6_.21, ...), custom_call_target="tpu_custom_call" | custom-call | flops 12884901888 | bytes 25165824 | tf_op jit(solution)/shard_map/pallas_call | solution.py:136
  40.9 23.5 %collective-permute-done.17 = bf16[2,1024,256]{2,1,0:T(8,128)(2,1)S(1)} collective-permute-done((bf16[2,1024,256]{2,1,0:T(8,128)(2,1)S(1)}, bf16[2,1024,256]{2,1,0:T(8,128)(2,1)S(1)}, u32[]{:S(2)}, u32[]{:S(2)}) %collective-permute-start.17) | collective-permute-done | bytes 1048608 | tf_op jit(solution)/shard_map/ppermute | solution.py:379
  92.1 21.7 %collective-permute-done.20.refs_1_ = bf16[2,1024,256]{2,1,0:T(8,128)(2,1)S(1)} collective-permute-done((bf16[2,1024,256]{2,1,0:T(8,128)(2,1)S(1)}, bf16[2,1024,256]{2,1,0:T(8,128)(2,1)S(1)}, u32[]{:S(2)}, u32[]{:S(2)}) %collective-permute-start.20) | collective-permute-done | bytes 1048608 | tf_op jit(solution)/shard_map/ppermute | solution.py:379
  117.5 24.9 %shard_map.116 = (bf16[1024,1024]{1,0:T(8,128)(2,1)}, bf16[1024,1024]{1,0:T(8,128)(2,1)}, bf16[2,2,1024,256]{3,2,1,0:T(8,128)(2,1)}, bf16[2,2,1024,256]{3,2,1,0:...) custom-call(s32[1]{0:T(128)} %bitcast.2.me_ref, bf16[2,1024,256]{2,1,0:T(8,128)(2,1)} %copy-done.6, ...), custom_call_target="tpu_custom_call" | custom-call | flops 12884901888 | bytes 25165824 | tf_op jit(solution)/shard_map/pallas_call | solution.py:136
  149.9 24.3 %collective-permute-done.24 = bf16[2,1024,256]{2,1,0:T(8,128)(2,1)S(1)} collective-permute-done((bf16[2,1024,256]{2,1,0:T(8,128)(2,1)S(1)}, bf16[2,1024,256]{2,1,0:T(8,128)(2,1)S(1)}, u32[]{:S(2)}, u32[]{:S(2)}) %collective-permute-start.24) | collective-permute-done | bytes 1048608 | tf_op jit(solution)/shard_map/ppermute | solution.py:379
  201.1 21.8 %collective-permute-done.27.refs_1_ = bf16[2,1024,256]{2,1,0:T(8,128)(2,1)} collective-permute-done((bf16[2,1024,256]{2,1,0:T(8,128)(2,1)S(1)}, bf16[2,1024,256]{2,1,0:T(8,128)(2,1)}, u32[]{:S(2)}, u32[]{:S(2)}) %collective-permute-start.27) | collective-permute-done | bytes 1048608 | tf_op jit(solution)/shard_map/ppermute | solution.py:379
  229.0 25.0 %shard_map.117 = (bf16[1024,1024]{1,0:T(8,128)(2,1)}, bf16[1024,1024]{1,0:T(8,128)(2,1)}, bf16[2,2,1024,256]{3,2,1,0:T(8,128)(2,1)}, bf16[2,2,1024,256]{3,2,1,0:...) custom-call(s32[1]{0:T(128)} %bitcast.2.me_ref, bf16[2,1024,256]{2,1,0:T(8,128)(2,1)} %copy-done.2, ...), custom_call_target="tpu_custom_call" | custom-call | flops 12884901888 | bytes 25165824 | tf_op jit(solution)/shard_map/pallas_call | solution.py:136
  254.0 41.4 %collective-permute-done.15 = bf16[1,512,1024]{2,1,0:T(8,128)(2,1)} collective-permute-done((bf16[1,512,1024]{2,1,0:T(8,128)(2,1)}, bf16[1,512,1024]{2,1,0:T(8,128)(2,1)}, u32[]{:S(2)}, u32[]{:S(2)}) %collective-permute-start.15) | collective-permute-done | bytes 1048608 | tf_op jit(solution)/shard_map/ppermute | solution.py:421
  295.4 24.3 %shard_map.121 = (bf16[1024,1024]{1,0:T(8,128)(2,1)}, bf16[1024,1024]{1,0:T(8,128)(2,1)}, bf16[2,2,1024,256]{3,2,1,0:T(8,128)(2,1)}, bf16[2,2,1024,256]{3,2,1,0:...) custom-call(s32[1]{0:T(128)} %bitcast.2.me_ref, bf16[2,4,512,2048]{3,2,1,0:T(8,128)(2,1)} %refs_6_.21, ...), custom_call_target="tpu_custom_call" | custom-call | flops 12884901888 | bytes 25165824 | tf_op jit(solution)/shard_map/pallas_call | solution.py:136
  319.8 24.1 %shard_map.112 = (bf16[1024,1024]{1,0:T(8,128)(2,1)}, bf16[1024,1024]{1,0:T(8,128)(2,1)}, bf16[2,2,1024,256]{3,2,1,0:T(8,128)(2,1)}, bf16[2,2,1024,256]{3,2,1,0:...) custom-call(s32[1]{0:T(128)} %bitcast.2.me_ref, bf16[2,4,512,2048]{3,2,1,0:T(8,128)(2,1)} %refs_6_.21, ...), custom_call_target="tpu_custom_call" | custom-call | flops 12884901888 | bytes 25165824 | tf_op jit(solution)/shard_map/pallas_call | solution.py:136
  344.4 24.3 %shard_map.118 = (bf16[1024,1024]{1,0:T(8,128)(2,1)}, bf16[1024,1024]{1,0:T(8,128)(2,1)}, bf16[2,2,1024,256]{3,2,1,0:T(8,128)(2,1)}, bf16[2,2,1024,256]{3,2,1,0:...) custom-call(s32[1]{0:T(128)} %bitcast.2.me_ref, bf16[2,4,512,2048]{3,2,1,0:T(8,128)(2,1)} %refs_6_.21, ...), custom_call_target="tpu_custom_call" | custom-call | flops 12884901888 | bytes 25165824 | tf_op jit(solution)/shard_map/pallas_call | solution.py:136
  375.8 26.1 %collective-permute-done.45 = bf16[2,1024,256]{2,1,0:T(8,128)(2,1)S(1)} collective-permute-done((bf16[2,1024,256]{2,1,0:T(8,128)(2,1)S(1)}, bf16[2,1024,256]{2,1,0:T(8,128)(2,1)S(1)}, u32[]{:S(2)}, u32[]{:S(2)}) %collective-permute-start.45) | collective-permute-done | bytes 1048608 | tf_op jit(solution)/shard_map/ppermute | solution.py:379
  419.4 20.0 %collective-permute-done.31 = bf16[2,1024,256]{2,1,0:T(8,128)(2,1)S(1)} collective-permute-done((bf16[2,1024,256]{2,1,0:T(8,128)(2,1)S(1)}, bf16[2,1024,256]{2,1,0:T(8,128)(2,1)S(1)}, u32[]{:S(2)}, u32[]{:S(2)}) %collective-permute-start.31) | collective-permute-done | bytes 1048608 | tf_op jit(solution)/shard_map/ppermute | solution.py:379
  452.7 34.2 %collective-permute-done.3 = bf16[1024,256]{1,0:T(8,128)(2,1)S(1)} collective-permute-done((bf16[1024,256]{1,0:T(8,128)(2,1)S(1)}, bf16[1024,256]{1,0:T(8,128)(2,1)S(1)}, u32[]{:S(2)}, u32[]{:S(2)}) %collective-permute-start.3) | collective-permute-done | bytes 524320 | tf_op jit(solution)/shard_map/ppermute | solution.py:379
  534.1 25.1 %shard_map.122 = (bf16[1024,1024]{1,0:T(8,128)(2,1)}, bf16[1024,1024]{1,0:T(8,128)(2,1)}, bf16[2,2,1024,256]{3,2,1,0:T(8,128)(2,1)}, bf16[2,2,1024,256]{3,2,1,0:...) custom-call(s32[1]{0:T(128)} %bitcast.2.me_ref, bf16[2,1024,256]{2,1,0:T(8,128)(2,1)} %copy-done.4, ...), custom_call_target="tpu_custom_call" | custom-call | flops 12884901888 | bytes 25165824 | tf_op jit(solution)/shard_map/pallas_call | solution.py:136
  559.8 24.7 %shard_map.113 = (bf16[1024,1024]{1,0:T(8,128)(2,1)}, bf16[1024,1024]{1,0:T(8,128)(2,1)}, bf16[2,2,1024,256]{3,2,1,0:T(8,128)(2,1)}, bf16[2,2,1024,256]{3,2,1,0:...) custom-call(s32[1]{0:T(128)} %bitcast.2.me_ref, bf16[2,1024,256]{2,1,0:T(8,128)(2,1)} %pad_maximum_fusion.refs_0_, ...), custom_call_target="tpu_custom_call" | custom-call | flops 12884901888 | bytes 25165824 | tf_op jit(solution)/shard_map/pallas_call | solution.py:136
  585.6 24.9 %shard_map.119 = (bf16[1024,1024]{1,0:T(8,128)(2,1)}, bf16[1024,1024]{1,0:T(8,128)(2,1)}, bf16[2,2,1024,256]{3,2,1,0:T(8,128)(2,1)}, bf16[2,2,1024,256]{3,2,1,0:...) custom-call(s32[1]{0:T(128)} %bitcast.2.me_ref, bf16[2,1024,256]{2,1,0:T(8,128)(2,1)} %pad_maximum_fusion.4.refs_0_, ...), custom_call_target="tpu_custom_call" | custom-call | flops 12884901888 | bytes 25165824 | tf_op jit(solution)/shard_map/pallas_call | solution.py:136
  618.2 20.7 %collective-permute-done.52 = bf16[2,1024,256]{2,1,0:T(8,128)(2,1)S(1)} collective-permute-done((bf16[2,1024,256]{2,1,0:T(8,128)(2,1)S(1)}, bf16[2,1024,256]{2,1,0:T(8,128)(2,1)S(1)}, u32[]{:S(2)}, u32[]{:S(2)}) %collective-permute-start.52) | collective-permute-done | bytes 1048608 | tf_op jit(solution)/shard_map/ppermute | solution.py:379
  690.7 33.0 %collective-permute-done.10 = bf16[1024,256]{1,0:T(8,128)(2,1)S(1)} collective-permute-done((bf16[1024,256]{1,0:T(8,128)(2,1)S(1)}, bf16[1024,256]{1,0:T(8,128)(2,1)S(1)}, u32[]{:S(2)}, u32[]{:S(2)}) %collective-permute-start.10) | collective-permute-done | bytes 524320 | tf_op jit(solution)/shard_map/ppermute | solution.py:379
  769.7 24.9 %shard_map.123 = (bf16[1024,1024]{1,0:T(8,128)(2,1)}, bf16[1024,1024]{1,0:T(8,128)(2,1)}, bf16[2,2,1024,256]{3,2,1,0:T(8,128)(2,1)}, bf16[2,2,1024,256]{3,2,1,0:...) custom-call(s32[1]{0:T(128)} %bitcast.2.me_ref, bf16[2,1024,256]{2,1,0:T(8,128)(2,1)} %copy-done.5, ...), custom_call_target="tpu_custom_call" | custom-call | flops 12884901888 | bytes 25165824 | tf_op jit(solution)/shard_map/pallas_call | solution.py:136
  795.1 25.0 %shard_map.120 = (bf16[1024,1024]{1,0:T(8,128)(2,1)}, bf16[1024,1024]{1,0:T(8,128)(2,1)}, bf16[2,2,1024,256]{3,2,1,0:T(8,128)(2,1)}, bf16[2,2,1024,256]{3,2,1,0:...) custom-call(s32[1]{0:T(128)} %bitcast.2.me_ref, bf16[2,1024,256]{2,1,0:T(8,128)(2,1)} %pad_maximum_fusion.5.refs_0_, ...), custom_call_target="tpu_custom_call" | custom-call | flops 12884901888 | bytes 25165824 | tf_op jit(solution)/shard_map/pallas_call | solution.py:136
  820.7 25.3 %shard_map.114 = (bf16[1024,1024]{1,0:T(8,128)(2,1)}, bf16[1024,1024]{1,0:T(8,128)(2,1)}, bf16[2,2,1024,256]{3,2,1,0:T(8,128)(2,1)}, bf16[2,2,1024,256]{3,2,1,0:...) custom-call(s32[1]{0:T(128)} %bitcast.2.me_ref, bf16[2,1024,256]{2,1,0:T(8,128)(2,1)} %copy-done.3, ...), custom_call_target="tpu_custom_call" | custom-call | flops 12884901888 | bytes 25165824 | tf_op jit(solution)/shard_map/pallas_call | solution.py:136
  869.4 23.5 %collective-permute-done.84 = bf16[2,1024,256]{2,1,0:T(8,128)(2,1)S(1)} collective-permute-done((bf16[2,1024,256]{2,1,0:T(8,128)(2,1)S(1)}, bf16[2,1024,256]{2,1,0:T(8,128)(2,1)S(1)}, u32[]{:S(2)}, u32[]{:S(2)}) %collective-permute-start.84) | collective-permute-done | bytes 1048608 | tf_op jit(solution)/shard_map/ppermute | solution.py:379
  895.2 20.1 %collective-permute-done.70 = bf16[2,1024,256]{2,1,0:T(8,128)(2,1)S(1)} collective-permute-done((bf16[2,1024,256]{2,1,0:T(8,128)(2,1)S(1)}, bf16[2,1024,256]{2,1,0:T(8,128)(2,1)S(1)}, u32[]{:S(2)}, u32[]{:S(2)}) %collective-permute-start.70) | collective-permute-done | bytes 1048608 | tf_op jit(solution)/shard_map/ppermute | solution.py:379
  953.7 19.6 %psum.7 = f32[8]{0:T(128)S(1)} all-reduce(f32[8]{0:T(128)S(1)} %maximum_reduce_fusion), channel_id=1, replica_groups=mesh['dp'=2,'tp'=8] {'tp'}, use_global_device_ids=true, to_apply=%region_1.2 | all-reduce | flops 8 | bytes 64 | tf_op jit(solution)/shard_map/psum | solution.py:440
  978.8 58.9 %collective-permute-done.60 = f32[8]{0:T(128)S(1)} collective-permute-done((f32[8]{0:T(128)S(1)}, f32[8]{0:T(128)S(1)}, u32[]{:S(2)}, u32[]{:S(2)}) %collective-permute-start.60) | collective-permute-done | bytes 64 | tf_op jit(solution)/shard_map/ppermute | solution.py:470
  1150.3 31.6 %hidden_again.1 = (bf16[4096,1024]{1,0:T(8,128)(2,1)}, bf16[4096,1024]{1,0:T(8,128)(2,1)}) custom-call(bf16[8,512,1024]{2,1,0:T(8,128)(2,1)} %collective-permute-done.61.u_ref, bf16[8,512,2048]{2,1,0:T(8,128)(2,1)} %all-gather.5.cloned.1.call-done.dz_ref.refs_7_, bf16[3,1024,2048]{2,1,0:T(8,128)(2,1)} %w2_ref.1), custom_call_target="tpu_custom_call" | custom-call | flops 17179869184 | bytes 50331648 | tf_op jit(solution)/shard_map/hidden_again/pallas_call | solution.py:300
  1182.0 28.6 %shard_map.132.refs_11_ = f32[3,1024,1024]{2,1,0:T(8,128)} custom-call(s32[1]{0:T(128)} %bitcast.half_ref, f32[16]{0:T(128)} %pad_maximum_fusion.12.clip_ref, f32[1]{0:T(128)} %bitcast.62.refs_0_, bf16[1024,1024]{1,0:T(8,128)(2,1)} %get-tuple-element.155.refs_1_, bf16[1024,1024]{1,0:T(8,128)(2,1)} %get-tuple-element.156.refs_2_, ...), custom_call_target="tpu_custom_call" | custom-call | flops 17179869184 | bytes 25165824 | tf_op jit(solution)/shard_map/pallas_call | solution.py:277
  1229.4 28.5 %shard_map.126.refs_8_ = f32[3,1024,1024]{2,1,0:T(8,128)} custom-call(s32[1]{0:T(128)} %bitcast.half_ref, f32[16]{0:T(128)} %pad_maximum_fusion.12.clip_ref, f32[1]{0:T(128)} %bitcast.62.refs_0_, bf16[3,2,4,512,2048]{4,3,2,1,0:T(8,128)(2,1)} %refs_1_.13, bf16[8,512,1024]{2,1,0:T(8,128)(2,1)} %all-gather.3.cloned.1.call-done.refs_2_, ...), custom_call_target="tpu_custom_call" | custom-call | flops 17179869184 | bytes 25165824 | tf_op jit(solution)/shard_map/pallas_call | solution.py:277
  1257.9 113.5 %collective-permute-done.59.refs_7_ = f32[1024,1024]{1,0:T(8,128)} collective-permute-done((f32[1024,1024]{1,0:T(8,128)}, f32[1024,1024]{1,0:T(8,128)}, u32[]{:S(2)}, u32[]{:S(2)}) %collective-permute-start.59) | collective-permute-done | bytes 4194336 | tf_op jit(solution)/shard_map/ppermute | solution.py:468
  1371.4 19.0 %shard_map.127.refs_8_ = f32[3,1024,1024]{2,1,0:T(8,128)} custom-call(s32[1]{0:T(128)} %bitcast.half_ref, f32[8]{0:T(128)} %copy-done.36, f32[1]{0:T(128)} %bitcast.62.refs_0_, bf16[3,2,4,512,2048]{4,3,2,1,0:T(8,128)(2,1)} %refs_1_.13, bf16[1024,1024]{1,0:T(8,128)(2,1)} %get-tuple-element.119.refs_1_.refs_2_, ...), custom_call_target="tpu_custom_call", output_to_operand_aliasing={{}: (10, {})} | custom-call | flops 8589934592 | bytes 25165824 | tf_op jit(solution)/shard_map/pallas_call | solution.py:277
  1390.4 70.4 %collective-permute-done.58.refs_7_ = f32[1024,1024]{1,0:T(8,128)} collective-permute-done((f32[1024,1024]{1,0:T(8,128)}, f32[1024,1024]{1,0:T(8,128)}, u32[]{:S(2)}, u32[]{:S(2)}) %collective-permute-start.58) | collective-permute-done | bytes 4194336 | tf_op jit(solution)/shard_map/ppermute | solution.py:468
  (322 shorter events, 499.4 us)
Async XLA Ops:
  7.2 1143.2 %all-gather.5.cloned.1.call-start = ((), (), s32[]{:S(2)}) async-start(), calls=%async_computation.1 | async-start | bytes 18874368 | tf_op jit(solution)/shard_map/all_gather | solution.py:436
  224.7 70.7 %collective-permute-start.14 = (bf16[1,512,2048]{2,1,0:T(8,128)(2,1)S(1)}, bf16[1,512,2048]{2,1,0:T(8,128)(2,1)}, u32[]{:S(2)}, u32[]{:S(2)}) collective-permute-start(bf16[1,512,2048]{2,1,0:T(8,128)(2,1)S(1)} %dynamic-slice_bitcast_fusion), channel_id=1, source_target_pairs={{0,8},{8,0},{1,9},{9,1},{2,10},{10,2},{3,11},{11,3},{4,12},{12,4},... | collective-permute-start | bytes 6291464 | tf_op jit(solution)/shard_map/ppermute | solution.py:419
  228.0 67.4 %collective-permute-start.15 = (bf16[1,512,1024]{2,1,0:T(8,128)(2,1)}, bf16[1,512,1024]{2,1,0:T(8,128)(2,1)}, u32[]{:S(2)}, u32[]{:S(2)}) collective-permute-start(bf16[1,512,1024]{2,1,0:T(8,128)(2,1)} %dynamic-slice_bitcast_fusion.1), channel_id=1, source_target_pairs={{0,8},{8,0},{1,9},{9,1},{2,10},{10,2},{3,11},{11,3},{4,12},{12,4},... | collective-permute-start | bytes 3145736 | tf_op jit(solution)/shard_map/ppermute | solution.py:421
  295.4 934.0 %all-gather.3.cloned.1.call-start = ((), (), s32[]{:S(2)}) async-start(), calls=%async_computation | async-start | bytes 9437184 | tf_op jit(solution)/shard_map/all_gather | solution.py:437
  319.8 49.1 %collective-permute-start.44 = (bf16[2,2,1024,256]{3,2,1,0:T(8,128)(2,1)}, bf16[2,2,1024,256]{3,2,1,0:T(8,128)(2,1)}, u32[]{:S(2)}, u32[]{:S(2)}) collective-permute-start(bf16[2,2,1024,256]{3,2,1,0:T(8,128)(2,1)} %get-tuple-element.109), channel_id=1, source_target_pairs={{0,1},{1,0},{2,3},{3,2},{4,5},{5,4},{6,7},{7,6},{8,9},{9,8},{10,11... | collective-permute-start | bytes 6291464 | tf_op jit(solution)/shard_map/ppermute | solution.py:379
  374.4 44.3 %collective-permute-start.1 = (bf16[2,1024,256]{2,1,0:T(8,128)(2,1)S(1)}, bf16[2,1024,256]{2,1,0:T(8,128)(2,1)S(1)}, u32[]{:S(2)}, u32[]{:S(2)}) collective-permute-start(bf16[2,1024,256]{2,1,0:T(8,128)(2,1)S(1)} %get-tuple-element.172), channel_id=1, source_target_pairs={{0,2},{1,3},{2,0},{3,1},{4,6},{5,7},{6,4},{7,5},{8,10},{9,11},{10,... | collective-permute-start | bytes 3145736 | tf_op jit(solution)/shard_map/ppermute | solution.py:379
  449.6 49.2 %collective-permute-start.48 = (bf16[2,1024,256]{2,1,0:T(8,128)(2,1)S(1)}, bf16[2,1024,256]{2,1,0:T(8,128)(2,1)S(1)}, u32[]{:S(2)}, u32[]{:S(2)}) collective-permute-start(bf16[2,1024,256]{2,1,0:T(8,128)(2,1)S(1)} %pad_maximum_fusion.6.refs_0_), channel_id=1, source_target_pairs={{0,4},{1,5},{2,6},{3,7},{4,0},{5,1},{6,2},{7,3},{8,12},{9,13},{10,... | collective-permute-start | bytes 3145736 | tf_op jit(solution)/shard_map/ppermute | solution.py:379
  452.3 43.9 %collective-permute-start.33 = (bf16[1024,256]{1,0:T(8,128)(2,1)S(1)}, bf16[1024,256]{1,0:T(8,128)(2,1)S(1)}, u32[]{:S(2)}, u32[]{:S(2)}) collective-permute-start(bf16[1024,256]{1,0:T(8,128)(2,1)S(1)} %fusion.42), channel_id=1, source_target_pairs={{0,4},{1,5},{2,6},{3,7},{4,0},{5,1},{6,2},{7,3},{8,12},{9,13},{10,... | collective-permute-start | bytes 1572872 | tf_op jit(solution)/shard_map/ppermute | solution.py:379
  499.4 60.4 %collective-permute-start.5 = (bf16[2,1024,256]{2,1,0:T(8,128)(2,1)}, bf16[2,1024,256]{2,1,0:T(8,128)(2,1)}, u32[]{:S(2)}, u32[]{:S(2)}) collective-permute-start(bf16[2,1024,256]{2,1,0:T(8,128)(2,1)} %pad_maximum_fusion.refs_0_), channel_id=1, source_target_pairs={{0,1},{1,0},{2,3},{3,2},{4,5},{5,4},{6,7},{7,6},{8,9},{9,8},{10,11... | collective-permute-start | bytes 3145736 | tf_op jit(solution)/shard_map/ppermute | solution.py:379
  514.4 70.2 %collective-permute-start.35 = (bf16[2,1024,256]{2,1,0:T(8,128)(2,1)}, bf16[2,1024,256]{2,1,0:T(8,128)(2,1)}, u32[]{:S(2)}, u32[]{:S(2)}) collective-permute-start(bf16[2,1024,256]{2,1,0:T(8,128)(2,1)} %pad_maximum_fusion.4.refs_0_), channel_id=1, source_target_pairs={{0,1},{1,0},{2,3},{3,2},{4,5},{5,4},{6,7},{7,6},{8,9},{9,8},{10,11... | collective-permute-start | bytes 3145736 | tf_op jit(solution)/shard_map/ppermute | solution.py:379
  532.2 52.4 %collective-permute-start.36 = (bf16[2,1024,256]{2,1,0:T(8,128)(2,1)}, bf16[2,1024,256]{2,1,0:T(8,128)(2,1)S(1)}, u32[]{:S(2)}, u32[]{:S(2)}) collective-permute-start(bf16[2,1024,256]{2,1,0:T(8,128)(2,1)} %collective-permute-done.34.refs_1_), channel_id=1, source_target_pairs={{0,1},{1,0},{2,3},{3,2},{4,5},{5,4},{6,7},{7,6},{8,9},{9,8},{10,11... | collective-permute-start | bytes 3145736 | tf_op jit(solution)/shard_map/ppermute | solution.py:379
  559.2 51.7 %collective-permute-start.51 = (bf16[2,2,1024,256]{3,2,1,0:T(8,128)(2,1)}, bf16[2,2,1024,256]{3,2,1,0:T(8,128)(2,1)}, u32[]{:S(2)}, u32[]{:S(2)}) collective-permute-start(bf16[2,2,1024,256]{3,2,1,0:T(8,128)(2,1)} %get-tuple-element.112), channel_id=1, source_target_pairs={{0,1},{1,0},{2,3},{3,2},{4,5},{5,4},{6,7},{7,6},{8,9},{9,8},{10,11... | collective-permute-start | bytes 6291464 | tf_op jit(solution)/shard_map/ppermute | solution.py:379
  686.4 49.4 %collective-permute-start.55 = (bf16[2,1024,256]{2,1,0:T(8,128)(2,1)S(1)}, bf16[2,1024,256]{2,1,0:T(8,128)(2,1)S(1)}, u32[]{:S(2)}, u32[]{:S(2)}) collective-permute-start(bf16[2,1024,256]{2,1,0:T(8,128)(2,1)S(1)} %pad_maximum_fusion.7.refs_0_), channel_id=1, source_target_pairs={{0,4},{1,5},{2,6},{3,7},{4,0},{5,1},{6,2},{7,3},{8,12},{9,13},{10,... | collective-permute-start | bytes 3145736 | tf_op jit(solution)/shard_map/ppermute | solution.py:379
  689.1 43.7 %collective-permute-start.40 = (bf16[1024,256]{1,0:T(8,128)(2,1)S(1)}, bf16[1024,256]{1,0:T(8,128)(2,1)S(1)}, u32[]{:S(2)}, u32[]{:S(2)}) collective-permute-start(bf16[1024,256]{1,0:T(8,128)(2,1)S(1)} %fusion.38), channel_id=1, source_target_pairs={{0,4},{1,5},{2,6},{3,7},{4,0},{5,1},{6,2},{7,3},{8,12},{9,13},{10,... | collective-permute-start | bytes 1572872 | tf_op jit(solution)/shard_map/ppermute | solution.py:379
  736.3 84.4 %collective-permute-start.12 = (bf16[2,1024,256]{2,1,0:T(8,128)(2,1)S(1)}, bf16[2,1024,256]{2,1,0:T(8,128)(2,1)}, u32[]{:S(2)}, u32[]{:S(2)}) collective-permute-start(bf16[2,1024,256]{2,1,0:T(8,128)(2,1)S(1)} %pad_maximum_fusion.1.refs_0_), channel_id=1, source_target_pairs={{0,1},{1,0},{2,3},{3,2},{4,5},{5,4},{6,7},{7,6},{8,9},{9,8},{10,11... | collective-permute-start | bytes 3145736 | tf_op jit(solution)/shard_map/ppermute | solution.py:379
  750.0 45.1 %collective-permute-start.42 = (bf16[2,1024,256]{2,1,0:T(8,128)(2,1)}, bf16[2,1024,256]{2,1,0:T(8,128)(2,1)}, u32[]{:S(2)}, u32[]{:S(2)}) collective-permute-start(bf16[2,1024,256]{2,1,0:T(8,128)(2,1)} %pad_maximum_fusion.5.refs_0_), channel_id=1, source_target_pairs={{0,1},{1,0},{2,3},{3,2},{4,5},{5,4},{6,7},{7,6},{8,9},{9,8},{10,11... | collective-permute-start | bytes 3145736 | tf_op jit(solution)/shard_map/ppermute | solution.py:379
  767.7 53.0 %collective-permute-start.13 = (bf16[2,1024,256]{2,1,0:T(8,128)(2,1)}, bf16[2,1024,256]{2,1,0:T(8,128)(2,1)}, u32[]{:S(2)}, u32[]{:S(2)}) collective-permute-start(bf16[2,1024,256]{2,1,0:T(8,128)(2,1)} %collective-permute-done.11.refs_1_), channel_id=1, source_target_pairs={{0,1},{1,0},{2,3},{3,2},{4,5},{5,4},{6,7},{7,6},{8,9},{9,8},{10,11... | collective-permute-start | bytes 3145736 | tf_op jit(solution)/shard_map/ppermute | solution.py:379
  794.6 61.5 %collective-permute-start.83 = (bf16[2,2,1024,256]{3,2,1,0:T(8,128)(2,1)}, bf16[2,2,1024,256]{3,2,1,0:T(8,128)(2,1)}, u32[]{:S(2)}, u32[]{:S(2)}) collective-permute-start(bf16[2,2,1024,256]{3,2,1,0:T(8,128)(2,1)} %get-tuple-element.145), channel_id=1, source_target_pairs={{0,1},{1,0},{2,3},{3,2},{4,5},{5,4},{6,7},{7,6},{8,9},{9,8},{10,11... | collective-permute-start | bytes 6291464 | tf_op jit(solution)/shard_map/ppermute | solution.py:379
  820.1 39.8 %collective-permute-start.76 = (bf16[2,2,1024,256]{3,2,1,0:T(8,128)(2,1)}, bf16[2,2,1024,256]{3,2,1,0:T(8,128)(2,1)}, u32[]{:S(2)}, u32[]{:S(2)}) collective-permute-start(bf16[2,2,1024,256]{3,2,1,0:T(8,128)(2,1)} %get-tuple-element.143), channel_id=1, source_target_pairs={{0,1},{1,0},{2,3},{3,2},{4,5},{5,4},{6,7},{7,6},{8,9},{9,8},{10,11... | collective-permute-start | bytes 6291464 | tf_op jit(solution)/shard_map/ppermute | solution.py:379
  820.2 43.5 %collective-permute-start.69 = (bf16[2,2,1024,256]{3,2,1,0:T(8,128)(2,1)}, bf16[2,2,1024,256]{3,2,1,0:T(8,128)(2,1)}, u32[]{:S(2)}, u32[]{:S(2)}) collective-permute-start(bf16[2,2,1024,256]{3,2,1,0:T(8,128)(2,1)} %get-tuple-element.141), channel_id=1, source_target_pairs={{0,1},{1,0},{2,3},{3,2},{4,5},{5,4},{6,7},{7,6},{8,9},{9,8},{10,11... | collective-permute-start | bytes 6291464 | tf_op jit(solution)/shard_map/ppermute | solution.py:379
  854.4 295.9 %collective-permute-start.61 = (bf16[8,512,1024]{2,1,0:T(8,128)(2,1)}, bf16[8,512,1024]{2,1,0:T(8,128)(2,1)}, u32[]{:S(2)}, u32[]{:S(2)}) collective-permute-start(bf16[8,512,1024]{2,1,0:T(8,128)(2,1)} %bitcast.266), channel_id=1, source_target_pairs={{0,8},{8,0},{1,9},{9,1},{2,10},{10,2},{3,11},{11,3},{4,12},{12,4},... | collective-permute-start | bytes 25165832 | tf_op jit(solution)/shard_map/ppermute | solution.py:420
  865.9 49.4 %collective-permute-start.70 = (bf16[2,1024,256]{2,1,0:T(8,128)(2,1)S(1)}, bf16[2,1024,256]{2,1,0:T(8,128)(2,1)S(1)}, u32[]{:S(2)}, u32[]{:S(2)}) collective-permute-start(bf16[2,1024,256]{2,1,0:T(8,128)(2,1)S(1)} %get-tuple-element.166), channel_id=1, source_target_pairs={{0,4},{1,5},{2,6},{3,7},{4,0},{5,1},{6,2},{7,3},{8,12},{9,13},{10,... | collective-permute-start | bytes 3145736 | tf_op jit(solution)/shard_map/ppermute | solution.py:379
  869.1 58.3 %collective-permute-start.63 = (bf16[2,1024,256]{2,1,0:T(8,128)(2,1)S(1)}, bf16[2,1024,256]{2,1,0:T(8,128)(2,1)S(1)}, u32[]{:S(2)}, u32[]{:S(2)}) collective-permute-start(bf16[2,1024,256]{2,1,0:T(8,128)(2,1)S(1)} %get-tuple-element.168), channel_id=1, source_target_pairs={{0,2},{1,3},{2,0},{3,1},{4,6},{5,7},{6,4},{7,5},{8,10},{9,11},{10,... | collective-permute-start | bytes 3145736 | tf_op jit(solution)/shard_map/ppermute | solution.py:379
  929.6 43.7 %collective-permute-start.79 = (bf16[1024,256]{1,0:T(8,128)(2,1)S(1)}, bf16[1024,256]{1,0:T(8,128)(2,1)}, u32[]{:S(2)}, u32[]{:S(2)}) collective-permute-start(bf16[1024,256]{1,0:T(8,128)(2,1)S(1)} %fusion.18), channel_id=1, source_target_pairs={{0,4},{1,5},{2,6},{3,7},{4,0},{5,1},{6,2},{7,3},{8,12},{9,13},{10,... | collective-permute-start | bytes 1572872 | tf_op jit(solution)/shard_map/ppermute | solution.py:379
  949.0 90.4 %collective-permute-start.87 = (bf16[2,1024,256]{2,1,0:T(8,128)(2,1)S(1)}, bf16[2,1024,256]{2,1,0:T(8,128)(2,1)}, u32[]{:S(2)}, u32[]{:S(2)}) collective-permute-start(bf16[2,1024,256]{2,1,0:T(8,128)(2,1)S(1)} %pad_maximum_fusion.11.refs_12_), channel_id=1, source_target_pairs={{0,4},{1,5},{2,6},{3,7},{4,0},{5,1},{6,2},{7,3},{8,12},{9,13},{10,... | collective-permute-start | bytes 3145736 | tf_op jit(solution)/shard_map/ppermute | solution.py:379
  952.5 86.9 %collective-permute-start.65 = (bf16[1024,256]{1,0:T(8,128)(2,1)S(1)}, bf16[1024,256]{1,0:T(8,128)(2,1)S(1)}, u32[]{:S(2)}, u32[]{:S(2)}) collective-permute-start(bf16[1024,256]{1,0:T(8,128)(2,1)S(1)} %fusion.26), channel_id=1, source_target_pairs={{0,4},{1,5},{2,6},{3,7},{4,0},{5,1},{6,2},{7,3},{8,12},{9,13},{10,... | collective-permute-start | bytes 1572872 | tf_op jit(solution)/shard_map/ppermute | solution.py:379
  973.3 64.4 %collective-permute-start.60 = (f32[8]{0:T(128)S(1)}, f32[8]{0:T(128)S(1)}, u32[]{:S(2)}, u32[]{:S(2)}) collective-permute-start(f32[8]{0:T(128)S(1)} %multiply_minimum_fusion.clip_ref), channel_id=1, source_target_pairs={{0,8},{8,0},{1,9},{9,1},{2,10},{10,2},{3,11},{11,3},{4,12},{12,4},... | collective-permute-start | bytes 104 | tf_op jit(solution)/shard_map/ppermute | solution.py:470
  976.1 82.2 %collective-permute-start.88 = (bf16[2,1024,256]{2,1,0:T(8,128)(2,1)S(1)}, bf16[2,1024,256]{2,1,0:T(8,128)(2,1)}, u32[]{:S(2)}, u32[]{:S(2)}) collective-permute-start(bf16[2,1024,256]{2,1,0:T(8,128)(2,1)S(1)} %pad_maximum_fusion.11.refs_12_), channel_id=1, source_target_pairs={{0,1},{1,0},{2,3},{3,2},{4,5},{5,4},{6,7},{7,6},{8,9},{9,8},{10,11... | collective-permute-start | bytes 3145736 | tf_op jit(solution)/shard_map/ppermute | solution.py:379
  1097.8 112.7 %collective-permute-start.91 = (f32[1024,1024]{1,0:T(8,128)}, f32[1024,1024]{1,0:T(8,128)}, u32[]{:S(2)}, u32[]{:S(2)}) collective-permute-start(f32[1024,1024]{1,0:T(8,128)} %shard_map.131), channel_id=1, source_target_pairs={{0,8},{8,0},{1,9},{9,1},{2,10},{10,2},{3,11},{11,3},{4,12},{12,4},... | collective-permute-start | bytes 12582920 | tf_op jit(solution)/shard_map/ppermute | solution.py:468
  1132.2 347.4 %collective-permute-start.90 = (f32[1024,1024]{1,0:T(8,128)}, f32[1024,1024]{1,0:T(8,128)}, u32[]{:S(2)}, u32[]{:S(2)}) collective-permute-start(f32[1024,1024]{1,0:T(8,128)} %shard_map.130), channel_id=1, source_target_pairs={{0,8},{8,0},{1,9},{9,1},{2,10},{10,2},{3,11},{11,3},{4,12},{12,4},... | collective-permute-start | bytes 12582920 | tf_op jit(solution)/shard_map/ppermute | solution.py:468
  1132.5 238.8 %collective-permute-start.59 = (f32[1024,1024]{1,0:T(8,128)}, f32[1024,1024]{1,0:T(8,128)}, u32[]{:S(2)}, u32[]{:S(2)}) collective-permute-start(f32[1024,1024]{1,0:T(8,128)} %shard_map.125), channel_id=1, source_target_pairs={{0,8},{8,0},{1,9},{9,1},{2,10},{10,2},{3,11},{11,3},{4,12},{12,4},... | collective-permute-start | bytes 12582920 | tf_op jit(solution)/shard_map/ppermute | solution.py:468
  1134.2 326.6 %collective-permute-start.58 = (f32[1024,1024]{1,0:T(8,128)}, f32[1024,1024]{1,0:T(8,128)}, u32[]{:S(2)}, u32[]{:S(2)}) collective-permute-start(f32[1024,1024]{1,0:T(8,128)} %shard_map.124), channel_id=1, source_target_pairs={{0,8},{8,0},{1,9},{9,1},{2,10},{10,2},{3,11},{11,3},{4,12},{12,4},... | collective-permute-start | bytes 12582920 | tf_op jit(solution)/shard_map/ppermute | solution.py:468
  (104 other events, 2400.4 us)
Sparse Core Ops, SparseCore 0:
  295.5 91.8 all-gather.4
  820.8 60.2 all-gather.2

commit v3 on v2

--- a/solution.py
+++ b/solution.py
@@ -43,17 +43,25 @@
         dh_ref[:, cols] = (slope * d_act).astype(jnp.bfloat16)
 
 
-def backward_kernel(layer, micro, first_ex, x_first, from_slots, me_ref, *refs):
-    *refs, w1, w2, x_buf, w1_sem, w2_sem, x_sem = refs
-    if from_slots:
-        own, first, core_own, core_first, norm_in, u_ref, w1_hbm, w2_hbm, x_hbm = refs[:9]
-        h_ref, dh_ref, keep_ref, send_ref, norm_ref, dz_ref = refs[9:]
-    else:
-        dz_in, u_ref, w1_hbm, w2_hbm, x_hbm, h_ref, dh_ref, keep_ref, send_ref, norm_ref, piece_ref = refs
+def gram_product(left, right):
+    prod = dot(left[...], left[:256, :], NT) * dot(right[...], right[:256, :], NT)
+    corner = dot(left[256:, :], left[256:, :], NT) * dot(right[256:, :], right[256:, :], NT)
+    total = prod[:256] + 2.0 * prod[256:] + corner
+    return jnp.sum(total.reshape(32, 8, 256), axis=0)
+
+
+def backward_kernel(layer, micro, first_ex, x_first, from_slots, do_back, me_ref, *refs):
+    refs = list(refs)
+    slot_refs = [refs.pop(0) for _ in range(4 if from_slots else 1)]
+    u_ref, w2_hbm, last_hbm, h_ref, dh_ref, dz_ref = refs[:6]
     me = me_ref[0]
     step = pl.program_id(0)
     slots = [(rc, r1, r2) for rc in (1, 0) for r1 in range(2) for r2 in range(2)]
     hid = u_ref.shape[-1]
+    if do_back:
+        keep_ref, send_ref, w2, w2_sem, w1, w1_sem = refs[6:]
+    else:
+        norm_ref, w2, w2_sem, x_buf, x_sem = refs[6:]
 
     def rows_of(rc, r1, r2):
         return pl.ds(pl.multiple_of(piece_of(me, r1, r2, rc, x_first) * PIECE, PIECE), PIECE)
@@ -63,27 +71,30 @@
         return pltpu.make_async_copy(w2_hbm.at[layer, rows, :], w2.at[rows, :], w2_sem.at[i])
 
     def w1_copy(i):
-        return pltpu.make_async_copy(w1_hbm.at[layer, rows_of(*slots[i]), :], w1.at[i], w1_sem.at[i])
+        return pltpu.make_async_copy(last_hbm.at[layer, rows_of(*slots[i]), :], w1.at[i], w1_sem.at[i])
 
     def x_copy():
-        return pltpu.make_async_copy(x_hbm.at[layer, micro, first_ex + step], x_buf, x_sem)
+        return pltpu.make_async_copy(last_hbm.at[layer, micro, first_ex + step], x_buf, x_sem)
 
     @pl.when(step == 0)
     def _():
         for i in range(2):
             w2_copy(i).start()
-        for i in range(8):
-            w1_copy(i).start()
-
-    x_copy().start()
+        if do_back:
+            for i in range(8):
+                w1_copy(i).start()
+
+    if not do_back:
+        x_copy().start()
     if from_slots:
+        own, first, core_own, core_first = slot_refs
         for rc, r1, slot in ((0, 0, own), (0, 1, first), (1, 0, core_own), (1, 1, core_first)):
             for r2 in range(2):
                 dz_ref[:, rows_of(rc, r1, r2)] = slot[r2]
         cot = dz_ref
     else:
-        cot = dz_in
-        piece_ref[...] = dz_in[:, pl.ds(pl.multiple_of(me * PIECE, PIECE), PIECE)]
+        cot = slot_refs[0]
+        dz_ref[...] = cot[:, pl.ds(pl.multiple_of(me * PIECE, PIECE), PIECE)]
 
     def wait_weights(j):
         if j % 2 == 0:
@@ -93,70 +104,114 @@
                 w2_copy(j // 2).wait()
 
     hidden_of(u_ref, cot, w2, h_ref, dh_ref, wait_weights)
-
-    @pl.when(step == 0)
-    def _():
-        for i in range(8):
-            w1_copy(i).wait()
-
-    for i, (rc, r1, r2) in enumerate(slots):
-        out = send_ref if rc else keep_ref
-        out[r1, r2] = dot(dh_ref[...], w1[i], NT).astype(jnp.bfloat16)
-
-    def gram_product(left, right):
-        prod = dot(left[...], left[:256, :], NT) * dot(right[...], right[:256, :], NT)
-        corner = dot(left[256:, :], left[256:, :], NT) * dot(right[256:, :], right[256:, :], NT)
-        total = prod[:256] + 2.0 * prod[256:] + corner
-        return jnp.sum(total.reshape(32, 8, 256), axis=0)
-
-    norm = gram_product(h_ref, cot)
-    x_copy().wait()
-    norm += gram_product(dh_ref, x_buf)
-    norm_ref[...] = norm_in[...] + norm if from_slots else norm
-
-
-def backward_chunk(layer, micro, first_ex, x_first, me, dz_inputs, norm_in, x_in, u_pre, w_up, w_down):
+    if do_back:
+
+        @pl.when(step == 0)
+        def _():
+            for i in range(8):
+                w1_copy(i).wait()
+
+        for i, (rc, r1, r2) in enumerate(slots):
+            out = send_ref if rc else keep_ref
+            out[r1, r2] = dot(dh_ref[...], w1[i], NT).astype(jnp.bfloat16)
+    else:
+        norm = gram_product(h_ref, cot)
+        x_copy().wait()
+        norm_ref[...] = norm + gram_product(dh_ref, x_buf)
+
+
+NORM_SPEC = pl.BlockSpec((None, 8, 256), lambda e, *_: (e, 0, 0))
+NORM_SHAPE = jax.ShapeDtypeStruct((PER_CHUNK, 8, 256), jnp.float32)
+PART_SPEC = pl.BlockSpec((2, 2, 512, PIECE), lambda e, *_: (0, 0, e, 0))
+PART_SHAPE = jax.ShapeDtypeStruct((2, 2, PER_CHUNK * 512, PIECE), jnp.bfloat16)
+ANY_SPEC = pl.BlockSpec(memory_space=pl.ANY)
+
+
+def backward_chunk(layer, micro, first_ex, x_first, me, dz_inputs, do_back, x_in, u_pre, w_up, w_down):
     rows = PER_CHUNK * 512
     hid, model = u_pre.shape[-1], w_up.shape[1]
     from_slots = isinstance(dz_inputs, tuple)
-    norm_spec = pl.BlockSpec((None, 8, 256), lambda e, m: (e, 0, 0))
-    piece_spec = pl.BlockSpec((512, PIECE), lambda e, m: (e, 0))
     if from_slots:
-        in_specs = [pl.BlockSpec((2, 512, PIECE), lambda e, m: (0, e, 0))] * 4 + [norm_spec]
-        operands = (*dz_inputs, norm_in)
+        in_specs = [pl.BlockSpec((2, 512, PIECE), lambda e, m: (0, e, 0))] * 4
     else:
         in_specs = [pl.BlockSpec((None, None, 512, model), lambda e, m: (micro, first_ex + e, 0, 0))]
-        operands = (dz_inputs,)
-    part_spec = pl.BlockSpec((2, 2, 512, PIECE), lambda e, m: (0, 0, e, 0))
-    part_shape = jax.ShapeDtypeStruct((2, 2, rows, PIECE), jnp.bfloat16)
+        dz_inputs = (dz_inputs,)
     act_spec = pl.BlockSpec((512, hid), lambda e, m: (e, 0))
     act_shape = jax.ShapeDtypeStruct((rows, hid), jnp.bfloat16)
-    last_cols = model if from_slots else PIECE
-    any_spec = pl.BlockSpec(memory_space=pl.ANY)
-    return pl.pallas_call(
-        functools.partial(backward_kernel, layer, micro, first_ex, x_first, from_slots),
+    dz_cols = model if from_slots else PIECE
+    if do_back:
+        last_specs, last_shapes = [PART_SPEC] * 2, [PART_SHAPE] * 2
+        scratch = [pltpu.VMEM((8, PIECE, hid), jnp.bfloat16), pltpu.SemaphoreType.DMA((8,))]
+    else:
+        last_specs, last_shapes = [NORM_SPEC], [NORM_SHAPE]
+        scratch = [pltpu.VMEM((512, model), jnp.bfloat16), pltpu.SemaphoreType.DMA]
+    return pl.pallas_call(
+        functools.partial(backward_kernel, layer, micro, first_ex, x_first, from_slots, do_back),
         grid_spec=pltpu.PrefetchScalarGridSpec(
             num_scalar_prefetch=1,
             grid=(PER_CHUNK,),
             in_specs=in_specs
             + [pl.BlockSpec((None, None, None, 512, hid), lambda e, m: (layer, micro, first_ex + e, 0, 0))]
-            + [any_spec] * 3,
-            out_specs=[act_spec, act_spec, part_spec, part_spec, norm_spec]
-            + [pl.BlockSpec((512, last_cols), lambda e, m: (e, 0))],
-            scratch_shapes=[
-                pltpu.VMEM((8, PIECE, hid), jnp.bfloat16),
-                pltpu.VMEM((hid, model), jnp.bfloat16),
-                pltpu.VMEM((512, model), jnp.bfloat16),
-                pltpu.SemaphoreType.DMA((8,)),
-                pltpu.SemaphoreType.DMA((2,)),
-                pltpu.SemaphoreType.DMA,
+            + [ANY_SPEC] * 2,
+            out_specs=[act_spec, act_spec, pl.BlockSpec((512, dz_cols), lambda e, m: (e, 0))] + last_specs,
+            scratch_shapes=[pltpu.VMEM((hid, model), jnp.bfloat16), pltpu.SemaphoreType.DMA((2,))] + scratch,
+        ),
+        out_shape=[act_shape, act_shape, jax.ShapeDtypeStruct((rows, dz_cols), jnp.bfloat16)] + last_shapes,
+        compiler_params=pltpu.CompilerParams(dimension_semantics=("arbitrary",)),
+        cost_estimate=pl.CostEstimate(flops=4 * rows * hid * model, bytes_accessed=24 << 20, transcendentals=rows * hid),
+    )(me, *dz_inputs, u_pre, w_down, w_up if do_back else x_in)
+
+
+def norm_kernel(h_ref, dh_ref, dz_ref, x_ref, out_ref):
+    out_ref[...] = gram_product(h_ref, dz_ref) + gram_product(dh_ref, x_ref)
+
+
+def norm_chunk(layer, micro, first_ex, hidden, d_hid, cot, x_in):
+    hid, model = hidden.shape[1], x_in.shape[-1]
+    act_spec = pl.BlockSpec((512, hid), lambda e: (e, 0))
+    if cot.ndim == 4:
+        cot_spec = pl.BlockSpec((None, None, 512, model), lambda e: (micro, first_ex + e, 0, 0))
+    else:
+        cot_spec = pl.BlockSpec((512, model), lambda e: (e, 0))
+    x_spec = pl.BlockSpec((None, None, None, 512, model), lambda e: (layer, micro, first_ex + e, 0, 0))
+    return pl.pallas_call(
+        norm_kernel,
+        grid=(PER_CHUNK,),
+        in_specs=[act_spec, act_spec, cot_spec, x_spec],
+        out_specs=NORM_SPEC,
+        out_shape=NORM_SHAPE,
+        compiler_params=pltpu.CompilerParams(dimension_semantics=("arbitrary",)),
+        cost_estimate=pl.CostEstimate(flops=3 * PER_CHUNK * 512 * 512 * (hid + model), bytes_accessed=12 << 20, transcendentals=0),
+    )(hidden, d_hid, cot, x_in)
+
+
+def back_kernel(x_first, me_ref, dh_ref, w1_ref, keep_ref, send_ref):
+    for rc, out in ((1, send_ref), (0, keep_ref)):
+        for r1 in range(2):
+            for r2 in range(2):
+                start = pl.multiple_of(piece_of(me_ref[0], r1, r2, rc, x_first) * PIECE, PIECE)
+                out[r1, r2] = dot(dh_ref[...], w1_ref[pl.ds(start, PIECE), :], NT).astype(jnp.bfloat16)
+
+
+def back_chunk(layer, x_first, me, d_hid, w_up):
+    rows, hid = d_hid.shape
+    model = w_up.shape[1]
+    return pl.pallas_call(
+        functools.partial(back_kernel, x_first),
+        grid_spec=pltpu.PrefetchScalarGridSpec(
+            num_scalar_prefetch=1,
+            grid=(PER_CHUNK,),
+            in_specs=[
+                pl.BlockSpec((512, hid), lambda e, m: (e, 0)),
+                pl.BlockSpec((None, model, hid), lambda e, m: (layer, 0, 0)),
             ],
+            out_specs=[PART_SPEC] * 2,
         ),
-        out_shape=[act_shape, act_shape, part_shape, part_shape]
-        + [jax.ShapeDtypeStruct((PER_CHUNK, 8, 256), jnp.float32), jax.ShapeDtypeStruct((rows, last_cols), jnp.bfloat16)],
-        compiler_params=pltpu.CompilerParams(dimension_semantics=("arbitrary",)),
-        cost_estimate=pl.CostEstimate(flops=6 * rows * hid * model, bytes_accessed=24 << 20, transcendentals=rows * hid),
-    )(me, *operands, u_pre, w_up, w_down, x_in)
+        out_shape=[PART_SHAPE] * 2,
+        compiler_params=pltpu.CompilerParams(dimension_semantics=("arbitrary",)),
+        cost_estimate=pl.CostEstimate(flops=2 * rows * hid * model, bytes_accessed=10 << 20, transcendentals=0),
+        name="back_chunk",
+    )(me, d_hid, w_up)
 
 
 def grad_kernel(segs, n_lhs, n_rhs, init_layer, has_init, has_got, inv, half_ref, clip_ref, *refs):
@@ -288,29 +343,32 @@
     )(half, *operands)
 
 
-def hidden_kernel(u_ref, dz_ref, w2_ref, h_ref, dh_ref):
+def hidden_kernel(from_ref, u_ref, dz_ref, w2_ref, h_ref, dh_ref):
     hidden_of(u_ref, dz_ref, w2_ref, h_ref, dh_ref)
 
 
-def hidden_again(layer, u_other, cot_other, w_down):
+def hidden_again(layer, from_micro, u_other, cot_other, w_down):
     n_ex, _, model = cot_other.shape
     hid = u_other.shape[-1]
-    act_spec = pl.BlockSpec((512, hid), lambda e: (e, 0))
+    act_spec = pl.BlockSpec((512, hid), lambda e, m: (e, 0))
     act_shape = jax.ShapeDtypeStruct((n_ex * 512, hid), jnp.bfloat16)
     return pl.pallas_call(
         hidden_kernel,
-        grid=(n_ex,),
-        in_specs=[
-            pl.BlockSpec((None, 512, hid), lambda e: (e, 0, 0)),
-            pl.BlockSpec((None, 512, model), lambda e: (e, 0, 0)),
-            pl.BlockSpec((None, hid, model), lambda e: (layer, 0, 0)),
-        ],
-        out_specs=[act_spec, act_spec],
+        grid_spec=pltpu.PrefetchScalarGridSpec(
+            num_scalar_prefetch=1,
+            grid=(n_ex,),
+            in_specs=[
+                pl.BlockSpec((None, None, 512, hid), lambda e, m: (m[0], e, 0, 0)),
+                pl.BlockSpec((None, 512, model), lambda e, m: (e, 0, 0)),
+                pl.BlockSpec((None, hid, model), lambda e, m: (layer, 0, 0)),
+            ],
+            out_specs=[act_spec, act_spec],
+        ),
         out_shape=[act_shape, act_shape],
         compiler_params=pltpu.CompilerParams(dimension_semantics=("arbitrary",)),
-        cost_estimate=pl.CostEstimate(flops=2 * n_ex * 512 * hid * model, bytes_accessed=48 << 20, transcendentals=n_ex * 512 * hid),
+        cost_estimate=pl.CostEstimate(flops=2 * n_ex * 512 * hid * model, bytes_accessed=24 << 20, transcendentals=n_ex * 512 * hid),
         name="hidden_again",
-    )(u_other, cot_other, w_down)
+    )(from_micro, u_other, cot_other, w_down)
 
 
 def finish_kernel(inv, has_got, own_ref, *refs):
@@ -408,37 +466,51 @@
         orders = [k % 2 == 0 for k in range(len(chunks))]
         cots = [d_out] * len(chunks)
         pieces = [None] * len(chunks)
-        norms = [None] * len(chunks)
+        norms = [[] for _ in chunks]
         saved = [None] * n_layers
         top = n_layers - 1
         swap_dp = [(i, 1 - i) for i in range(dp_size)]
+        my_core = me % 2
         ex_all = micro * per_micro
-        ex_m, ex_e = me // per_micro, me % per_micro
-        cot_slice = lax.dynamic_slice(d_out, (ex_m, ex_e, 0, 0), (1, 1, *d_out.shape[2:]))[0]
-        x_slice = lax.dynamic_slice(x_in, (top, ex_m, ex_e, 0, (1 - my_dp) * HALF), (1, 1, 1, d_out.shape[2], HALF))[0, 0]
-        cot_other = lax.ppermute(cot_slice, "dp", swap_dp)
-        u_other = lax.ppermute(u_pre[top].reshape(ex_all, *u_pre.shape[3:]), "dp", swap_dp)
-        x_other = lax.ppermute(x_slice, "dp", swap_dp)
+        u_other = lax.ppermute(u_pre[top], "dp", swap_dp)
+        cot_other = lax.ppermute(lax.dynamic_index_in_dim(d_out, my_core, 0, keepdims=False), "dp", swap_dp)
+        x_sizes = (1, 1, *x_in.shape[2:4], HALF)
+        x_other = lax.dynamic_slice(x_in, (top, my_core, 0, 0, (1 - my_dp) * HALF), x_sizes)[0, 0]
+        x_other = lax.ppermute(x_other, "dp", swap_dp)
+        cot_other = (cot_other, swap(cot_other, CORE))
         for layer in reversed(range(n_layers)):
-            top = layer == n_layers - 1
+            on_top = layer == top
             hids, dhids, full = [], [], []
             for k, (m, e) in enumerate(chunks):
-                hidden, d_hid, keep, send, norms[k], cot = backward_chunk(
-                    layer, m, e, orders[k], me_arr, cots[k], norms[k], x_in, u_pre, w_up, w_down
+                hidden, d_hid, cot, *rest = backward_chunk(
+                    layer, m, e, orders[k], me_arr, cots[k], layer > 0, x_in, u_pre, w_up, w_down
                 )
-                if (layer, k) == (0, 1):
-                    cot_other, x_other, norms[k] = lax.optimization_barrier((cot_other, x_other, norms[k]))
-                pieces[k], cots[k] = sum_over_tp(keep, send, cot if top else pieces[k], orders[k])
+                if layer > 0:
+                    norms[k].append(norm_chunk(layer, m, e, hidden, d_hid, d_out if on_top else cot, x_in))
+                    pieces[k], cots[k] = sum_over_tp(*rest, cot if on_top else pieces[k], orders[k])
+                else:
+                    norms[k].append(rest[0])
                 hids.append(hidden)
                 dhids.append(d_hid)
                 full.append(cot)
-            saved[layer] = (tuple(hids), tuple(dhids), d_out if top else tuple(full))
-        cot_other = lax.all_gather(cot_other, "tp", axis=0, tiled=True)
-        x_other = lax.all_gather(x_other, "tp", axis=0, tiled=True)
-        hid_other, dhid_other = hidden_again(n_layers - 1, u_other, cot_other, w_down)
+            saved[layer] = (tuple(hids), tuple(dhids), d_out if on_top else tuple(full))
+        norm_part = sum(jnp.concatenate([norms[k][i] for k in range(len(chunks))]) for i in range(n_layers))
+        norm_vec = lax.psum(jnp.sum(norm_part, axis=(1, 2)), "tp")
+        clip = jnp.minimum(1.0, clip_norm[0] / jnp.sqrt(norm_vec))
+        clip_other = lax.ppermute(clip, "dp", swap_dp)
+        for k in range(len(chunks)):
+            keep, send = back_chunk(0, orders[k], me_arr, dhids[k], w_up)
+            _, cots[k] = sum_over_tp(keep, send, pieces[k], orders[k])
+        hid_other, dhid_other = [], []
+        for i in range(2):
+            h_i, dh_i = hidden_again(top, (my_core ^ i).reshape(1), u_other, cot_other[i], w_down)
+            hid_other.append(h_i)
+            dhid_other.append(dh_i)
+        x_other, clip_other, *hid_other = lax.optimization_barrier((x_other, clip_other, *hid_other))
+        x_other = (x_other, swap(x_other, CORE))
+        clip_other = lax.dynamic_slice(jnp.concatenate([clip_other, clip_other]), (my_core * per_micro,), (ex_all,))
+        clip_all = jnp.concatenate([clip, clip_other])
         d_in = join_slots(me_arr, orders, cots, d_out.shape)
-        norm_vec = lax.psum(jnp.sum(jnp.concatenate(norms), axis=(1, 2)), "tp")
-        clip = jnp.minimum(1.0, clip_norm[0] / jnp.sqrt(norm_vec))
         noise_scale = (noise_mult[0] * clip_norm[0]).reshape(1)
         own_half, other_half = my_dp.reshape(1), (1 - my_dp).reshape(1)
         top = n_layers - 1
@@ -467,11 +539,13 @@
             part = grad(other_half, clip, own_segs(up, layer))
             got.append(lax.ppermute(part, "dp", swap_dp))
         result = [None, None]
-        clip_all = jnp.concatenate([clip, lax.ppermute(clip, "dp", swap_dp)])
         inv = 1.0 / examples
         for up in (True, False):
-            rest = ((x_other, None, False, 0), (dhid_other, None, False, 0)) if up else ((hid_other, None, False, 0), (cot_other, None, True, 0))
-            segs = own_segs(up, top) + [(ex_all, *rest)]
+            if up:
+                rest = [(per_micro, (x_other[r], None, False, 0), (dhid_other[r], None, False, 0)) for r in range(2)]
+            else:
+                rest = [(per_micro, (hid_other[r], None, False, 0), (cot_other[r], None, True, 0)) for r in range(2)]
+            segs = own_segs(up, top) + rest
             result[up] = grad(own_half, clip_all, segs, noise_of(up, top), None, inv, (top, n_layers, None))
         for i, (up, layer) in enumerate(grads):
             last = i == len(grads) - 1

time: 1500 us -> 1230 us (0.82)
  waiting for transfers between devices: 783 us -> 478 us
  Pallas kernels: 542 us -> 575 us
  other arithmetic: 39.6 us -> 70.7 us
    ppermute x84 -> x86, waiting for transfers between devices: 499 us -> 231 us  [swap(): return lax.ppermute(value, 'tp', [(i, i ^ mask) for i in range(tp_size)])]
    pallas_call x1 -> x14, Pallas kernels: 31.6 us -> 142 us  [the longest x8 71.1 us: norm_chunk(): pl.pallas_call(norm_kernel, grid=(PER_CHUNK,), in_specs=[act_spec, act_sp...]
    pallas_call x12, Pallas kernels: 296 us -> 218 us  [backward_chunk(): pl.pallas_call(functools.partial(backward_kernel, layer, micro, first_ex,...]
    ppermute x4, waiting for transfers between devices: 184 us -> 118 us  [local_pass(): got.append(lax.ppermute(part, 'dp', swap_dp))]
    ppermute x4, waiting for transfers between devices: 100 us -> 128 us  [the longest x1 87.8 us: local_pass(): clip_other = lax.ppermute(clip, 'dp', swap_dp)]
    convert_element_type x24, other arithmetic: 25.8 us -> 44.7 us  [add(): return (a.astype(jnp.float32) + b.astype(jnp.float32)).astype(jnp.bfloat16)]
    squeeze x2 -> x3, local copies, waits for them, and re-layouts: 3.99 us -> 20.8 us  [the longest x1 8.44 us: local_pass(): lax.dynamic_index_in_dim(d_out, my_core, 0, keepdims=False)]
    ppermute x84 -> x86, starting transfers between devices: 64.5 us -> 50.7 us  [swap(): return lax.ppermute(value, 'tp', [(i, i ^ mask) for i in range(tp_size)])]
  transfers between devices with their start and end apart: 94 -> 94, of which waited for: 37 -> 30; matrix products, arithmetic and copies ran while one was open for 3% -> 7% of each run, Pallas kernels for 33% -> 44%
where the time goes in v3:
time: 1230 us; the launch traced here: 1220 us
  Pallas kernels  575 us (47%)
  waiting for transfers between devices  478 us (39%)
  other arithmetic  70.7 us (6%)
  starting transfers between devices  60.7 us (5%)
  local copies, waits for them, and re-layouts  22.2 us (2%)
  blocking collectives  13.2 us (1%)
    ppermute x86, waiting for transfers between devices, swap(): return lax.ppermute(value, 'tp', [(i, i ^ mask) for i in range(tp_size)])  231 us
    pallas_call x12, Pallas kernels, backward_chunk(): pl.pallas_call(functools.partial(backward_kernel, layer, micro, first_ex,...  218 us
    pallas_call x10, Pallas kernels, weight_grad(): pl.pallas_call(functools.partial(grad_kernel, table, len(lhs), len(rhs),...  194 us
    ppermute x4, waiting for transfers between devices, local_pass(): got.append(lax.ppermute(part, 'dp', swap_dp))  118 us
    ppermute x1, waiting for transfers between devices, local_pass(): clip_other = lax.ppermute(clip, 'dp', swap_dp)  87.8 us
    pallas_call x8, Pallas kernels, norm_chunk(): pl.pallas_call(norm_kernel, grid=(PER_CHUNK,), in_specs=[act_spec, act_sp...  71.1 us
    ppermute x86, starting transfers between devices, swap(): return lax.ppermute(value, 'tp', [(i, i ^ mask) for i in range(tp_size)])  50.7 us
    convert_element_type x24, other arithmetic, add(): return (a.astype(jnp.float32) + b.astype(jnp.float32)).astype(jnp.bfloat16)  44.7 us
  transfers between devices with their start and end apart: 94, of which 30 were waited for; matrix products, arithmetic and copies ran while one was open for 7% of the time, Pallas kernels for 44%

profile of v3, /device:TPU:0, one launch (start us, length us, event | category | flops | bytes accessed | tf_op | source)
XLA Modules:
  0.0 1223.2 jit_solution(3321191544540248722)
XLA Ops:
  0.6 17.9 %shard_map.112 = (bf16[1024,1024]{1,0:T(8,128)(2,1)}, bf16[1024,1024]{1,0:T(8,128)(2,1)}, bf16[1024,256]{1,0:T(8,128)(2,1)}, bf16[2,2,1024,256]{3,2,1,0:T(8,128)(2,1)}, bf16[2,2,1024,256]{3,2,1,0:T(8,128)(2,1)}) custom-call(s32[1]{0:T(128)} %bitcast.2.me_ref, bf16[2,4,512,2048]{3,2,1,0:T(8,128)(2,1)} %refs_7_.1, bf16[3,2,4,512,1024]{4,3,2,1,0:T(8,128)(2,1)} %refs_4_.15, ...), custom_call_target="tpu_custom_call" | custom-call | flops 8589934592 | bytes 25165824 | tf_op jit(solution)/shard_map/pallas_call | solution.py:148
  19.3 17.9 %shard_map.114 = (bf16[1024,1024]{1,0:T(8,128)(2,1)}, bf16[1024,1024]{1,0:T(8,128)(2,1)}, bf16[1024,256]{1,0:T(8,128)(2,1)}, bf16[2,2,1024,256]{3,2,1,0:T(8,128)(2,1)}, bf16[2,2,1024,256]{3,2,1,0:T(8,128)(2,1)}) custom-call(s32[1]{0:T(128)} %bitcast.2.me_ref, bf16[2,4,512,2048]{3,2,1,0:T(8,128)(2,1)} %refs_7_.1, bf16[3,2,4,512,1024]{4,3,2,1,0:T(8,128)(2,1)} %refs_4_.15, ...), custom_call_target="tpu_custom_call" | custom-call | flops 8589934592 | bytes 25165824 | tf_op jit(solution)/shard_map/pallas_call | solution.py:148
  37.3 18.4 %shard_map.118 = (bf16[1024,1024]{1,0:T(8,128)(2,1)}, bf16[1024,1024]{1,0:T(8,128)(2,1)}, bf16[1024,256]{1,0:T(8,128)(2,1)}, bf16[2,2,1024,256]{3,2,1,0:T(8,128)(2,1)}, bf16[2,2,1024,256]{3,2,1,0:T(8,128)(2,1)}) custom-call(s32[1]{0:T(128)} %bitcast.2.me_ref, bf16[2,4,512,2048]{3,2,1,0:T(8,128)(2,1)} %refs_7_.1, bf16[3,2,4,512,1024]{4,3,2,1,0:T(8,128)(2,1)} %refs_4_.15, ...), custom_call_target="tpu_custom_call" | custom-call | flops 8589934592 | bytes 25165824 | tf_op jit(solution)/shard_map/pallas_call | solution.py:148
  56.2 18.2 %shard_map.116 = (bf16[1024,1024]{1,0:T(8,128)(2,1)}, bf16[1024,1024]{1,0:T(8,128)(2,1)}, bf16[1024,256]{1,0:T(8,128)(2,1)}, bf16[2,2,1024,256]{3,2,1,0:T(8,128)(2,1)}, bf16[2,2,1024,256]{3,2,1,0:T(8,128)(2,1)}) custom-call(s32[1]{0:T(128)} %bitcast.2.me_ref, bf16[2,4,512,2048]{3,2,1,0:T(8,128)(2,1)} %refs_7_.1, bf16[3,2,4,512,1024]{4,3,2,1,0:T(8,128)(2,1)} %refs_4_.15, ...), custom_call_target="tpu_custom_call" | custom-call | flops 8589934592 | bytes 25165824 | tf_op jit(solution)/shard_map/pallas_call | solution.py:148
  86.3 16.7 %collective-permute-done.1 = bf16[2,1024,256]{2,1,0:T(8,128)(2,1)S(1)} collective-permute-done((bf16[2,1024,256]{2,1,0:T(8,128)(2,1)S(1)}, bf16[2,1024,256]{2,1,0:T(8,128)(2,1)S(1)}, u32[]{:S(2)}, u32[]{:S(2)}) %collective-permute-start.1) | collective-permute-done | bytes 1048608 | tf_op jit(solution)/shard_map/ppermute | solution.py:437
  108.2 32.3 %collective-permute-done.2 = bf16[1024,256]{1,0:T(8,128)(2,1)S(1)} collective-permute-done((bf16[1024,256]{1,0:T(8,128)(2,1)S(1)}, bf16[1024,256]{1,0:T(8,128)(2,1)S(1)}, u32[]{:S(2)}, u32[]{:S(2)}) %collective-permute-start.2) | collective-permute-done | bytes 524320 | tf_op jit(solution)/shard_map/ppermute | solution.py:437
  170.1 29.8 %collective-permute-done.24 = bf16[1024,256]{1,0:T(8,128)(2,1)S(1)} collective-permute-done((bf16[1024,256]{1,0:T(8,128)(2,1)S(1)}, bf16[1024,256]{1,0:T(8,128)(2,1)S(1)}, u32[]{:S(2)}, u32[]{:S(2)}) %collective-permute-start.24) | collective-permute-done | bytes 524320 | tf_op jit(solution)/shard_map/ppermute | solution.py:437
  202.4 31.7 %collective-permute-done.17 = bf16[1024,256]{1,0:T(8,128)(2,1)S(1)} collective-permute-done((bf16[1024,256]{1,0:T(8,128)(2,1)S(1)}, bf16[1024,256]{1,0:T(8,128)(2,1)S(1)}, u32[]{:S(2)}, u32[]{:S(2)}) %collective-permute-start.17) | collective-permute-done | bytes 524320 | tf_op jit(solution)/shard_map/ppermute | solution.py:437
  237.5 18.6 %shard_map.120 = (bf16[1024,1024]{1,0:T(8,128)(2,1)}, bf16[1024,1024]{1,0:T(8,128)(2,1)}, bf16[1024,2048]{1,0:T(8,128)(2,1)}, bf16[2,2,1024,256]{3,2,1,0:T(8,128)(2,1)}, bf16[2,2,1024,256]{3,2,1,0:T(8,128)(2,1)}) custom-call(s32[1]{0:T(128)} %bitcast.2.me_ref, bf16[2,1024,256]{2,1,0:T(8,128)(2,1)} %copy-done.14, ...), custom_call_target="tpu_custom_call" | custom-call | flops 8589934592 | bytes 25165824 | tf_op jit(solution)/shard_map/pallas_call | solution.py:148
  262.6 18.8 %shard_map.122 = (bf16[1024,1024]{1,0:T(8,128)(2,1)}, bf16[1024,1024]{1,0:T(8,128)(2,1)}, bf16[1024,2048]{1,0:T(8,128)(2,1)}, bf16[2,2,1024,256]{3,2,1,0:T(8,128)(2,1)}, bf16[2,2,1024,256]{3,2,1,0:T(8,128)(2,1)}) custom-call(s32[1]{0:T(128)} %bitcast.2.me_ref, bf16[2,1024,256]{2,1,0:T(8,128)(2,1)} %pad_maximum_fusion.1.refs_0_, ...), custom_call_target="tpu_custom_call" | custom-call | flops 8589934592 | bytes 25165824 | tf_op jit(solution)/shard_map/pallas_call | solution.py:148
  281.4 18.6 %shard_map.126 = (bf16[1024,1024]{1,0:T(8,128)(2,1)}, bf16[1024,1024]{1,0:T(8,128)(2,1)}, bf16[1024,2048]{1,0:T(8,128)(2,1)}, bf16[2,2,1024,256]{3,2,1,0:T(8,128)(2,1)}, bf16[2,2,1024,256]{3,2,1,0:T(8,128)(2,1)}) custom-call(s32[1]{0:T(128)} %bitcast.2.me_ref, bf16[2,1024,256]{2,1,0:T(8,128)(2,1)} %copy-done.13, ...), custom_call_target="tpu_custom_call" | custom-call | flops 8589934592 | bytes 25165824 | tf_op jit(solution)/shard_map/pallas_call | solution.py:148
  300.6 19.0 %shard_map.124 = (bf16[1024,1024]{1,0:T(8,128)(2,1)}, bf16[1024,1024]{1,0:T(8,128)(2,1)}, bf16[1024,2048]{1,0:T(8,128)(2,1)}, bf16[2,2,1024,256]{3,2,1,0:T(8,128)(2,1)}, bf16[2,2,1024,256]{3,2,1,0:T(8,128)(2,1)}) custom-call(s32[1]{0:T(128)} %bitcast.2.me_ref, bf16[2,1024,256]{2,1,0:T(8,128)(2,1)} %pad_maximum_fusion.2.refs_0_, ...), custom_call_target="tpu_custom_call" | custom-call | flops 8589934592 | bytes 25165824 | tf_op jit(solution)/shard_map/pallas_call | solution.py:148
  374.2 19.5 %collective-permute-done.36 = bf16[2,1024,256]{2,1,0:T(8,128)(2,1)} collective-permute-done((bf16[2,1024,256]{2,1,0:T(8,128)(2,1)}, bf16[2,1024,256]{2,1,0:T(8,128)(2,1)}, u32[]{:S(2)}, u32[]{:S(2)}) %collective-permute-start.36) | collective-permute-done | bytes 1048608 | tf_op jit(solution)/shard_map/ppermute | solution.py:437
  494.5 17.6 %shard_map.131 = (bf16[1024,1024]{1,0:T(8,128)(2,1)}, bf16[1024,1024]{1,0:T(8,128)(2,1)}, bf16[1024,2048]{1,0:T(8,128)(2,1)}, f32[2,8,256]{2,1,0:T(8,128)}) custom-call(s32[1]{0:T(128)} %bitcast.2.me_ref, bf16[2,1024,256]{2,1,0:T(8,128)(2,1)} %pad_maximum_fusion.7.refs_0_, bf16[2,1024,256]{2,1,0:T(8,128)(2,1)} %collective-permute-done.53.refs_1_, ...), custom_call_target="tpu_custom_call" | custom-call | flops 8589934592 | bytes 25165824 | tf_op jit(solution)/shard_map/pallas_call | solution.py:148
  522.1 17.9 %shard_map.129 = (bf16[1024,1024]{1,0:T(8,128)(2,1)}, bf16[1024,1024]{1,0:T(8,128)(2,1)}, bf16[1024,2048]{1,0:T(8,128)(2,1)}, f32[2,8,256]{2,1,0:T(8,128)}) custom-call(s32[1]{0:T(128)} %bitcast.2.me_ref, bf16[2,1024,256]{2,1,0:T(8,128)(2,1)} %copy-done.8, bf16[2,1024,256]{2,1,0:T(8,128)(2,1)} %collective-permute-done.39.refs_1_, ...), custom_call_target="tpu_custom_call" | custom-call | flops 8589934592 | bytes 25165824 | tf_op jit(solution)/shard_map/pallas_call | solution.py:148
  540.7 17.5 %shard_map.130 = (bf16[1024,1024]{1,0:T(8,128)(2,1)}, bf16[1024,1024]{1,0:T(8,128)(2,1)}, bf16[1024,2048]{1,0:T(8,128)(2,1)}, f32[2,8,256]{2,1,0:T(8,128)}) custom-call(s32[1]{0:T(128)} %bitcast.2.me_ref, bf16[2,1024,256]{2,1,0:T(8,128)(2,1)} %pad_maximum_fusion.6.refs_0_, bf16[2,1024,256]{2,1,0:T(8,128)(2,1)} %collective-permute-done.46.refs_1_, ...), custom_call_target="tpu_custom_call" | custom-call | flops 8589934592 | bytes 25165824 | tf_op jit(solution)/shard_map/pallas_call | solution.py:148
  576.3 17.5 %shard_map.128 = (bf16[1024,1024]{1,0:T(8,128)(2,1)}, bf16[1024,1024]{1,0:T(8,128)(2,1)}, bf16[1024,2048]{1,0:T(8,128)(2,1)}, f32[2,8,256]{2,1,0:T(8,128)}) custom-call(s32[1]{0:T(128)} %bitcast.2.me_ref, bf16[2,1024,256]{2,1,0:T(8,128)(2,1)} %copy-done.9, bf16[2,1024,256]{2,1,0:T(8,128)(2,1)} %copy-done.39, ...), custom_call_target="tpu_custom_call" | custom-call | flops 8589934592 | bytes 25165824 | tf_op jit(solution)/shard_map/pallas_call | solution.py:148
  659.4 32.1 %collective-permute-done.60.u_ref = bf16[2,4,512,1024]{3,2,1,0:T(8,128)(2,1)} collective-permute-done((bf16[2,4,512,1024]{3,2,1,0:T(8,128)(2,1)}, bf16[2,4,512,1024]{3,2,1,0:T(8,128)(2,1)}, u32[]{:S(2)}, u32[]{:S(2)}) %collective-permute-start.60) | collective-permute-done | bytes 8388640 | tf_op jit(solution)/shard_map/ppermute | solution.py:475
  753.4 18.0 %hidden_again.2 = (bf16[2048,1024]{1,0:T(8,128)(2,1)}, bf16[2048,1024]{1,0:T(8,128)(2,1)}) custom-call(s32[1]{0:T(128)} %bitcast.63.from_ref, bf16[2,4,512,1024]{3,2,1,0:T(8,128)(2,1)} %collective-permute-done.60.u_ref, bf16[4,512,2048]{2,1,0:T(8,128)(2,1)} %collective-permute-done.61.dz_ref.refs_8_, bf16[3,1024,2048]{2,1,0:T(8,128)(2,1)} %w2_ref.3), custom_call_target="tpu_custom_call" | custom-call | flops 8589934592 | bytes 25165824 | tf_op jit(solution)/shard_map/hidden_again/pallas_call | solution.py:355
  783.0 87.8 %collective-permute-done.59 = f32[8]{0:T(128)S(1)} collective-permute-done((f32[8]{0:T(128)S(1)}, f32[8]{0:T(128)S(1)}, u32[]{:S(2)}, u32[]{:S(2)}) %collective-permute-start.59) | collective-permute-done | bytes 64 | tf_op jit(solution)/shard_map/ppermute | solution.py:500
  897.0 15.9 %shard_map.138 = f32[1024,1024]{1,0:T(8,128)} custom-call(s32[1]{0:T(128)} %bitcast.61.half_ref, f32[8]{0:T(128)} %multiply_minimum_fusion.clip_ref, bf16[1024,1024]{1,0:T(8,128)(2,1)} %get-tuple-element.131.refs_1_.refs_0_, bf16[1024,1024]{1,0:T(8,128)(2,1)} %get-tuple-element.132.refs_2_.refs_1_, bf16[1024,1024]{1,0:T(8,128)(2,1)} %get-tuple-element.133.refs_3_.refs_2_, ...), custom_call_target="tpu_custom_call" | custom-call | flops 8589934592 | bytes 25165824 | tf_op jit(solution)/shard_map/pallas_call | solution.py:332
  912.9 17.9 %hidden_again.3 = (bf16[2048,1024]{1,0:T(8,128)(2,1)}, bf16[2048,1024]{1,0:T(8,128)(2,1)}) custom-call(s32[1]{0:T(128)} %bitcast.66.from_ref, bf16[2,4,512,1024]{3,2,1,0:T(8,128)(2,1)} %collective-permute-done.60.u_ref, bf16[4,512,2048]{2,1,0:T(8,128)(2,1)} %collective-permute-done.62.dz_ref.refs_9_, bf16[3,1024,2048]{2,1,0:T(8,128)(2,1)} %w2_ref.3), custom_call_target="tpu_custom_call" | custom-call | flops 8589934592 | bytes 25165824 | tf_op jit(solution)/shard_map/hidden_again/pallas_call | solution.py:355
  933.6 15.6 %shard_map.132 = f32[1024,1024]{1,0:T(8,128)} custom-call(s32[1]{0:T(128)} %bitcast.61.half_ref, f32[8]{0:T(128)} %multiply_minimum_fusion.clip_ref, bf16[3,2,4,512,2048]{4,3,2,1,0:T(8,128)(2,1)} %refs_1_.13, bf16[1024,1024]{1,0:T(8,128)(2,1)} %get-tuple-element.121.refs_1_.refs_2_.dh_ref, bf16[1024,1024]{1,0:T(8,128)(2,1)} %get-tuple-element.122.refs_2_.refs_3_.dh_ref, ...), custom_call_target="tpu_custom_call" | custom-call | flops 8589934592 | bytes 25165824 | tf_op jit(solution)/shard_map/pallas_call | solution.py:332
  949.3 16.9 %shard_map.137.own_ref = f32[1024,1024]{1,0:T(8,128)} custom-call(s32[1]{0:T(128)} %bitcast.half_ref, f32[8]{0:T(128)} %multiply_minimum_fusion.clip_ref, f32[1]{0:T(128)} %bitcast.60.refs_0_, bf16[1024,1024]{1,0:T(8,128)(2,1)} %get-tuple-element.131.refs_1_.refs_0_, bf16[1024,1024]{1,0:T(8,128)(2,1)} %get-tuple-element.132.refs_2_.refs_1_, ...), custom_call_target="tpu_custom_call" | custom-call | flops 8589934592 | bytes 25165824 | tf_op jit(solution)/shard_map/pallas_call | solution.py:332
  969.0 28.6 %shard_map.140.refs_11_ = f32[3,1024,1024]{2,1,0:T(8,128)} custom-call(s32[1]{0:T(128)} %bitcast.half_ref, f32[16]{0:T(128)} %pad_maximum_fusion.13.clip_ref, f32[1]{0:T(128)} %bitcast.60.refs_0_, bf16[1024,1024]{1,0:T(8,128)(2,1)} %get-tuple-element.77.h_ref.refs_1_, bf16[1024,1024]{1,0:T(8,128)(2,1)} %get-tuple-element.79.h_ref.refs_2_, ...), custom_call_target="tpu_custom_call" | custom-call | flops 17179869184 | bytes 25165824 | tf_op jit(solution)/shard_map/pallas_call | solution.py:332
  997.7 19.0 %shard_map.141.refs_1_ = f32[3,1024,1024]{2,1,0:T(8,128)} custom-call(s32[1]{0:T(128)} %bitcast.half_ref, f32[8]{0:T(128)} %multiply_minimum_fusion.clip_ref, f32[1]{0:T(128)} %bitcast.60.refs_0_, bf16[1024,1024]{1,0:T(8,128)(2,1)} %get-tuple-element.88.h_ref.refs_0_.refs_1_, ...), custom_call_target="tpu_custom_call", output_to_operand_aliasing={{}: (13, {})} | custom-call | flops 8589934592 | bytes 25165824 | tf_op jit(solution)/shard_map/pallas_call | solution.py:332
  1016.7 15.7 %join_d_in.1 = bf16[2,4,512,2048]{3,2,1,0:T(8,128)(2,1)} custom-call(s32[1]{0:T(128)} %bitcast.2.me_ref, bf16[2,1024,256]{2,1,0:T(8,128)(2,1)} %pad_maximum_fusion.8.refs_0_, bf16[2,1024,256]{2,1,0:T(8,128)(2,1)} %copy-done.40, bf16[2,1024,256]{2,1,0:T(8,128)(2,1)} %collective-permute-done.69.refs_2_, bf16[2,1024,256]{2,1,0:T(8,128)(2,1)} %collective-permute-done.70.refs_3_, ...), custom_call_target="tpu_custom_call" | custom-call | flops 33554432 | bytes 33554432 | tf_op jit(solution)/shard_map/join_d_in/pallas_call | solution.py:417
  1038.1 28.6 %shard_map.134.refs_8_ = f32[3,1024,1024]{2,1,0:T(8,128)} custom-call(s32[1]{0:T(128)} %bitcast.half_ref, f32[16]{0:T(128)} %pad_maximum_fusion.13.clip_ref, f32[1]{0:T(128)} %bitcast.60.refs_0_, bf16[3,2,4,512,2048]{4,3,2,1,0:T(8,128)(2,1)} %refs_1_.13, bf16[4,512,1024]{2,1,0:T(8,128)(2,1)} %collective-permute-done.58.refs_2_, ...), custom_call_target="tpu_custom_call" | custom-call | flops 17179869184 | bytes 25165824 | tf_op jit(solution)/shard_map/pallas_call | solution.py:332
  1066.7 47.8 %collective-permute-done.57.refs_7_ = f32[1024,1024]{1,0:T(8,128)} collective-permute-done((f32[1024,1024]{1,0:T(8,128)}, f32[1024,1024]{1,0:T(8,128)}, u32[]{:S(2)}, u32[]{:S(2)}) %collective-permute-start.57) | collective-permute-done | bytes 4194336 | tf_op jit(solution)/shard_map/ppermute | solution.py:540
  1114.5 18.7 %shard_map.135.refs_8_ = f32[3,1024,1024]{2,1,0:T(8,128)} custom-call(s32[1]{0:T(128)} %bitcast.half_ref, f32[8]{0:T(128)} %multiply_minimum_fusion.clip_ref, f32[1]{0:T(128)} %bitcast.60.refs_0_, bf16[3,2,4,512,2048]{4,3,2,1,0:T(8,128)(2,1)} %refs_1_.13, ...), custom_call_target="tpu_custom_call", output_to_operand_aliasing={{}: (10, {})} | custom-call | flops 8589934592 | bytes 25165824 | tf_op jit(solution)/shard_map/pallas_call | solution.py:332
  1133.3 70.6 %collective-permute-done.56.refs_7_ = f32[1024,1024]{1,0:T(8,128)} collective-permute-done((f32[1024,1024]{1,0:T(8,128)}, f32[1024,1024]{1,0:T(8,128)}, u32[]{:S(2)}, u32[]{:S(2)}) %collective-permute-start.56) | collective-permute-done | bytes 4194336 | tf_op jit(solution)/shard_map/ppermute | solution.py:540
  1203.9 19.0 %shard_map.136 = f32[3,1024,1024]{2,1,0:T(8,128)} custom-call(s32[1]{0:T(128)} %bitcast.half_ref, f32[8]{0:T(128)} %multiply_minimum_fusion.clip_ref, f32[1]{0:T(128)} %bitcast.60.refs_0_, bf16[3,2,4,512,2048]{4,3,2,1,0:T(8,128)(2,1)} %refs_1_.13, bf16[1024,1024]{1,0:T(8,128)(2,1)} %get-tuple-element.121.refs_1_.refs_2_.dh_ref, ...), custom_call_target="tpu_custom_call", output_to_operand_aliasing={{}: (10, {})} | custom-call | flops 8589934592 | bytes 25165824 | tf_op jit(solution)/shard_map/pallas_call | solution.py:332
  (379 shorter events, 419.5 us)
Async XLA Ops:
  18.5 55.9 %collective-permute-start = (bf16[2,2,1024,256]{3,2,1,0:T(8,128)(2,1)}, bf16[2,2,1024,256]{3,2,1,0:T(8,128)(2,1)}, u32[]{:S(2)}, u32[]{:S(2)}) collective-permute-start(bf16[2,2,1024,256]{3,2,1,0:T(8,128)(2,1)} %get-tuple-element.87), channel_id=1, source_target_pairs={{0,1},{1,0},{2,3},{3,2},{4,5},{5,4},{6,7},{7,6},{8,9},{9,8},{10,11... | collective-permute-start | bytes 6291464 | tf_op jit(solution)/shard_map/ppermute | solution.py:437
  85.7 56.6 %collective-permute-start.22 = (bf16[2,1024,256]{2,1,0:T(8,128)(2,1)S(1)}, bf16[2,1024,256]{2,1,0:T(8,128)(2,1)S(1)}, u32[]{:S(2)}, u32[]{:S(2)}) collective-permute-start(bf16[2,1024,256]{2,1,0:T(8,128)(2,1)S(1)} %get-tuple-element.174), channel_id=1, source_target_pairs={{0,4},{1,5},{2,6},{3,7},{4,0},{5,1},{6,2},{7,3},{8,12},{9,13},{10,... | collective-permute-start | bytes 3145736 | tf_op jit(solution)/shard_map/ppermute | solution.py:437
  105.5 52.6 %collective-permute-start.15 = (bf16[2,1024,256]{2,1,0:T(8,128)(2,1)S(1)}, bf16[2,1024,256]{2,1,0:T(8,128)(2,1)S(1)}, u32[]{:S(2)}, u32[]{:S(2)}) collective-permute-start(bf16[2,1024,256]{2,1,0:T(8,128)(2,1)S(1)} %get-tuple-element.172), channel_id=1, source_target_pairs={{0,2},{1,3},{2,0},{3,1},{4,6},{5,7},{6,4},{7,5},{8,10},{9,11},{10,... | collective-permute-start | bytes 3145736 | tf_op jit(solution)/shard_map/ppermute | solution.py:437
  153.6 46.9 %collective-permute-start.4 = (bf16[2,1024,256]{2,1,0:T(8,128)(2,1)S(1)}, bf16[2,1024,256]{2,1,0:T(8,128)(2,1)}, u32[]{:S(2)}, u32[]{:S(2)}) collective-permute-start(bf16[2,1024,256]{2,1,0:T(8,128)(2,1)S(1)} %pad_maximum_fusion.refs_0_), channel_id=1, source_target_pairs={{0,2},{1,3},{2,0},{3,1},{4,6},{5,7},{6,4},{7,5},{8,10},{9,11},{10,... | collective-permute-start | bytes 3145736 | tf_op jit(solution)/shard_map/ppermute | solution.py:437
  158.6 76.6 %collective-permute-start.5 = (bf16[2,1024,256]{2,1,0:T(8,128)(2,1)S(1)}, bf16[2,1024,256]{2,1,0:T(8,128)(2,1)S(1)}, u32[]{:S(2)}, u32[]{:S(2)}) collective-permute-start(bf16[2,1024,256]{2,1,0:T(8,128)(2,1)S(1)} %pad_maximum_fusion.refs_0_), channel_id=1, source_target_pairs={{0,1},{1,0},{2,3},{3,2},{4,5},{5,4},{6,7},{7,6},{8,9},{9,8},{10,11... | collective-permute-start | bytes 3145736 | tf_op jit(solution)/shard_map/ppermute | solution.py:437
  169.6 67.2 %collective-permute-start.11 = (bf16[2,1024,256]{2,1,0:T(8,128)(2,1)}, bf16[2,1024,256]{2,1,0:T(8,128)(2,1)}, u32[]{:S(2)}, u32[]{:S(2)}) collective-permute-start(bf16[2,1024,256]{2,1,0:T(8,128)(2,1)} %pad_maximum_fusion.1.refs_0_), channel_id=1, source_target_pairs={{0,4},{1,5},{2,6},{3,7},{4,0},{5,1},{6,2},{7,3},{8,12},{9,13},{10,... | collective-permute-start | bytes 3145736 | tf_op jit(solution)/shard_map/ppermute | solution.py:437
  237.0 44.4 %collective-permute-start.26 = (bf16[2,1024,256]{2,1,0:T(8,128)(2,1)S(1)}, bf16[2,1024,256]{2,1,0:T(8,128)(2,1)}, u32[]{:S(2)}, u32[]{:S(2)}) collective-permute-start(bf16[2,1024,256]{2,1,0:T(8,128)(2,1)S(1)} %pad_maximum_fusion.3.refs_0_), channel_id=1, source_target_pairs={{0,1},{1,0},{2,3},{3,2},{4,5},{5,4},{6,7},{7,6},{8,9},{9,8},{10,11... | collective-permute-start | bytes 3145736 | tf_op jit(solution)/shard_map/ppermute | solution.py:437
  256.1 44.4 %collective-permute-start.19 = (bf16[2,1024,256]{2,1,0:T(8,128)(2,1)}, bf16[2,1024,256]{2,1,0:T(8,128)(2,1)}, u32[]{:S(2)}, u32[]{:S(2)}) collective-permute-start(bf16[2,1024,256]{2,1,0:T(8,128)(2,1)} %pad_maximum_fusion.2.refs_0_), channel_id=1, source_target_pairs={{0,1},{1,0},{2,3},{3,2},{4,5},{5,4},{6,7},{7,6},{8,9},{9,8},{10,11... | collective-permute-start | bytes 3145736 | tf_op jit(solution)/shard_map/ppermute | solution.py:437
  262.1 75.4 %collective-permute-start.28 = (bf16[2,2,1024,256]{3,2,1,0:T(8,128)(2,1)}, bf16[2,2,1024,256]{3,2,1,0:T(8,128)(2,1)}, u32[]{:S(2)}, u32[]{:S(2)}) collective-permute-start(bf16[2,2,1024,256]{3,2,1,0:T(8,128)(2,1)} %get-tuple-element.110), channel_id=1, source_target_pairs={{0,1},{1,0},{2,3},{3,2},{4,5},{5,4},{6,7},{7,6},{8,9},{9,8},{10,11... | collective-permute-start | bytes 6291464 | tf_op jit(solution)/shard_map/ppermute | solution.py:437
  281.3 64.1 %collective-permute-start.35 = (bf16[2,2,1024,256]{3,2,1,0:T(8,128)(2,1)}, bf16[2,2,1024,256]{3,2,1,0:T(8,128)(2,1)}, u32[]{:S(2)}, u32[]{:S(2)}) collective-permute-start(bf16[2,2,1024,256]{3,2,1,0:T(8,128)(2,1)} %get-tuple-element.113), channel_id=1, source_target_pairs={{0,1},{1,0},{2,3},{3,2},{4,5},{5,4},{6,7},{7,6},{8,9},{9,8},{10,11... | collective-permute-start | bytes 6291464 | tf_op jit(solution)/shard_map/ppermute | solution.py:437
  328.1 184.0 %collective-permute-start.61 = (bf16[4,512,2048]{2,1,0:T(8,128)(2,1)}, bf16[4,512,2048]{2,1,0:T(8,128)(2,1)}, u32[]{:S(2)}, u32[]{:S(2)}) collective-permute-start(bf16[4,512,2048]{2,1,0:T(8,128)(2,1)} %dynamic-slice_bitcast_fusion), channel_id=1, source_target_pairs={{0,8},{8,0},{1,9},{9,1},{2,10},{10,2},{3,11},{11,3},{4,12},{12,4},... | collective-permute-start | bytes 25165832 | tf_op jit(solution)/shard_map/ppermute | solution.py:476
  349.0 44.7 %collective-permute-start.36 = (bf16[2,1024,256]{2,1,0:T(8,128)(2,1)}, bf16[2,1024,256]{2,1,0:T(8,128)(2,1)}, u32[]{:S(2)}, u32[]{:S(2)}) collective-permute-start(bf16[2,1024,256]{2,1,0:T(8,128)(2,1)} %get-tuple-element.162), channel_id=1, source_target_pairs={{0,4},{1,5},{2,6},{3,7},{4,0},{5,1},{6,2},{7,3},{8,12},{9,13},{10,... | collective-permute-start | bytes 3145736 | tf_op jit(solution)/shard_map/ppermute | solution.py:437
  436.7 45.9 %collective-permute-start.54 = (bf16[2,1024,256]{2,1,0:T(8,128)(2,1)}, bf16[2,1024,256]{2,1,0:T(8,128)(2,1)}, u32[]{:S(2)}, u32[]{:S(2)}) collective-permute-start(bf16[2,1024,256]{2,1,0:T(8,128)(2,1)} %pad_maximum_fusion.7.refs_0_), channel_id=1, source_target_pairs={{0,1},{1,0},{2,3},{3,2},{4,5},{5,4},{6,7},{7,6},{8,9},{9,8},{10,11... | collective-permute-start | bytes 3145736 | tf_op jit(solution)/shard_map/ppermute | solution.py:437
  437.8 44.8 %collective-permute-start.39 = (bf16[2,1024,256]{2,1,0:T(8,128)(2,1)S(1)}, bf16[2,1024,256]{2,1,0:T(8,128)(2,1)}, u32[]{:S(2)}, u32[]{:S(2)}) collective-permute-start(bf16[2,1024,256]{2,1,0:T(8,128)(2,1)S(1)} %pad_maximum_fusion.5.refs_0_), channel_id=1, source_target_pairs={{0,4},{1,5},{2,6},{3,7},{4,0},{5,1},{6,2},{7,3},{8,12},{9,13},{10,... | collective-permute-start | bytes 3145736 | tf_op jit(solution)/shard_map/ppermute | solution.py:437
  461.7 229.8 %collective-permute-start.60 = (bf16[2,4,512,1024]{3,2,1,0:T(8,128)(2,1)}, bf16[2,4,512,1024]{3,2,1,0:T(8,128)(2,1)}, u32[]{:S(2)}, u32[]{:S(2)}) collective-permute-start(bf16[2,4,512,1024]{3,2,1,0:T(8,128)(2,1)} %slice_bitcast_fusion), channel_id=1, source_target_pairs={{0,8},{8,0},{1,9},{9,1},{2,10},{10,2},{3,11},{11,3},{4,12},{12,4},... | collective-permute-start | bytes 25165832 | tf_op jit(solution)/shard_map/ppermute | solution.py:475
  521.6 370.1 %collective-permute-start.62 = (bf16[4,512,2048]{2,1,0:T(8,128)(2,1)}, bf16[4,512,2048]{2,1,0:T(8,128)(2,1)}, u32[]{:S(2)}, u32[]{:S(2)}) collective-permute-start(bf16[4,512,2048]{2,1,0:T(8,128)(2,1)} %collective-permute-done.61.dz_ref.refs_8_), channel_id=1, source_target_pairs={{0,1},{1,0},{2,3},{3,2},{4,5},{5,4},{6,7},{7,6},{8,9},{9,8},{10,11... | collective-permute-start | bytes 25165832 | tf_op jit(solution)/shard_map/ppermute | solution.py:437
  540.6 61.8 %collective-permute-start.85 = (bf16[2,2,1024,256]{3,2,1,0:T(8,128)(2,1)}, bf16[2,2,1024,256]{3,2,1,0:T(8,128)(2,1)}, u32[]{:S(2)}, u32[]{:S(2)}) collective-permute-start(bf16[2,2,1024,256]{3,2,1,0:T(8,128)(2,1)} %get-tuple-element.146), channel_id=1, source_target_pairs={{0,1},{1,0},{2,3},{3,2},{4,5},{5,4},{6,7},{7,6},{8,9},{9,8},{10,11... | collective-permute-start | bytes 6291464 | tf_op jit(solution)/shard_map/ppermute | solution.py:437
  575.8 70.4 %collective-permute-start.78 = (bf16[2,2,1024,256]{3,2,1,0:T(8,128)(2,1)}, bf16[2,2,1024,256]{3,2,1,0:T(8,128)(2,1)}, u32[]{:S(2)}, u32[]{:S(2)}) collective-permute-start(bf16[2,2,1024,256]{3,2,1,0:T(8,128)(2,1)} %get-tuple-element.144), channel_id=1, source_target_pairs={{0,1},{1,0},{2,3},{3,2},{4,5},{5,4},{6,7},{7,6},{8,9},{9,8},{10,11... | collective-permute-start | bytes 6291464 | tf_op jit(solution)/shard_map/ppermute | solution.py:437
  576.2 75.3 %collective-permute-start.71 = (bf16[2,2,1024,256]{3,2,1,0:T(8,128)(2,1)}, bf16[2,2,1024,256]{3,2,1,0:T(8,128)(2,1)}, u32[]{:S(2)}, u32[]{:S(2)}) collective-permute-start(bf16[2,2,1024,256]{3,2,1,0:T(8,128)(2,1)} %get-tuple-element.142), channel_id=1, source_target_pairs={{0,1},{1,0},{2,3},{3,2},{4,5},{5,4},{6,7},{7,6},{8,9},{9,8},{10,11... | collective-permute-start | bytes 6291464 | tf_op jit(solution)/shard_map/ppermute | solution.py:437
  602.5 53.4 %collective-permute-start.64 = (bf16[2,2,1024,256]{3,2,1,0:T(8,128)(2,1)}, bf16[2,2,1024,256]{3,2,1,0:T(8,128)(2,1)}, u32[]{:S(2)}, u32[]{:S(2)}) collective-permute-start(bf16[2,2,1024,256]{3,2,1,0:T(8,128)(2,1)} %get-tuple-element.140), channel_id=1, source_target_pairs={{0,1},{1,0},{2,3},{3,2},{4,5},{5,4},{6,7},{7,6},{8,9},{9,8},{10,11... | collective-permute-start | bytes 6291464 | tf_op jit(solution)/shard_map/ppermute | solution.py:437
  646.1 45.9 %collective-permute-start.86 = (bf16[2,1024,256]{2,1,0:T(8,128)(2,1)S(1)}, bf16[2,1024,256]{2,1,0:T(8,128)(2,1)}, u32[]{:S(2)}, u32[]{:S(2)}) collective-permute-start(bf16[2,1024,256]{2,1,0:T(8,128)(2,1)S(1)} %get-tuple-element.152), channel_id=1, source_target_pairs={{0,4},{1,5},{2,6},{3,7},{4,0},{5,1},{6,2},{7,3},{8,12},{9,13},{10,... | collective-permute-start | bytes 3145736 | tf_op jit(solution)/shard_map/ppermute | solution.py:437
  651.5 129.9 %collective-permute-start.58 = (bf16[4,512,1024]{2,1,0:T(8,128)(2,1)}, bf16[4,512,1024]{2,1,0:T(8,128)(2,1)}, u32[]{:S(2)}, u32[]{:S(2)}) collective-permute-start(bf16[4,512,1024]{2,1,0:T(8,128)(2,1)} %dynamic-slice_bitcast_fusion.1), channel_id=1, source_target_pairs={{0,8},{8,0},{1,9},{9,1},{2,10},{10,2},{3,11},{11,3},{4,12},{12,4},... | collective-permute-start | bytes 12582920 | tf_op jit(solution)/shard_map/ppermute | solution.py:479
  655.9 52.7 %collective-permute-start.79 = (bf16[2,1024,256]{2,1,0:T(8,128)(2,1)}, bf16[2,1024,256]{2,1,0:T(8,128)(2,1)}, u32[]{:S(2)}, u32[]{:S(2)}) collective-permute-start(bf16[2,1024,256]{2,1,0:T(8,128)(2,1)} %get-tuple-element.154), channel_id=1, source_target_pairs={{0,2},{1,3},{2,0},{3,1},{4,6},{5,7},{6,4},{7,5},{8,10},{9,11},{10,... | collective-permute-start | bytes 3145736 | tf_op jit(solution)/shard_map/ppermute | solution.py:437
  708.6 183.4 %collective-permute-start.93 = (f32[1024,1024]{1,0:T(8,128)}, f32[1024,1024]{1,0:T(8,128)}, u32[]{:S(2)}, u32[]{:S(2)}) collective-permute-start(f32[1024,1024]{1,0:T(8,128)} %shard_map.139), channel_id=1, source_target_pairs={{0,8},{8,0},{1,9},{9,1},{2,10},{10,2},{3,11},{11,3},{4,12},{12,4},... | collective-permute-start | bytes 12582920 | tf_op jit(solution)/shard_map/ppermute | solution.py:540
  752.1 119.2 %collective-permute-start.74 = (bf16[1024,256]{1,0:T(8,128)(2,1)S(1)}, bf16[1024,256]{1,0:T(8,128)(2,1)}, u32[]{:S(2)}, u32[]{:S(2)}) collective-permute-start(bf16[1024,256]{1,0:T(8,128)(2,1)S(1)} %fusion.22), channel_id=1, source_target_pairs={{0,2},{1,3},{2,0},{3,1},{4,6},{5,7},{6,4},{7,5},{8,10},{9,11},{10,... | collective-permute-start | bytes 1572872 | tf_op jit(solution)/shard_map/ppermute | solution.py:437
  752.6 118.7 %collective-permute-start.67 = (bf16[1024,256]{1,0:T(8,128)(2,1)S(1)}, bf16[1024,256]{1,0:T(8,128)(2,1)}, u32[]{:S(2)}, u32[]{:S(2)}) collective-permute-start(bf16[1024,256]{1,0:T(8,128)(2,1)S(1)} %fusion.26), channel_id=1, source_target_pairs={{0,4},{1,5},{2,6},{3,7},{4,0},{5,1},{6,2},{7,3},{8,12},{9,13},{10,... | collective-permute-start | bytes 1572872 | tf_op jit(solution)/shard_map/ppermute | solution.py:437
  781.4 89.4 %collective-permute-start.59 = (f32[8]{0:T(128)S(1)}, f32[8]{0:T(128)S(1)}, u32[]{:S(2)}, u32[]{:S(2)}) collective-permute-start(f32[8]{0:T(128)S(1)} %copy-done.58), channel_id=1, source_target_pairs={{0,8},{8,0},{1,9},{9,1},{2,10},{10,2},{3,11},{11,3},{4,12},{12,4},... | collective-permute-start | bytes 104 | tf_op jit(solution)/shard_map/ppermute | solution.py:500
  930.9 101.5 %collective-permute-start.92 = (f32[1024,1024]{1,0:T(8,128)}, f32[1024,1024]{1,0:T(8,128)}, u32[]{:S(2)}, u32[]{:S(2)}) collective-permute-start(f32[1024,1024]{1,0:T(8,128)} %shard_map.138), channel_id=1, source_target_pairs={{0,8},{8,0},{1,9},{9,1},{2,10},{10,2},{3,11},{11,3},{4,12},{12,4},... | collective-permute-start | bytes 12582920 | tf_op jit(solution)/shard_map/ppermute | solution.py:540
  932.6 105.5 %collective-permute-start.63 = (bf16[4,512,1024]{2,1,0:T(8,128)(2,1)}, bf16[4,512,1024]{2,1,0:T(8,128)(2,1)}, u32[]{:S(2)}, u32[]{:S(2)}) collective-permute-start(bf16[4,512,1024]{2,1,0:T(8,128)(2,1)} %collective-permute-done.58.refs_2_), channel_id=1, source_target_pairs={{0,1},{1,0},{2,3},{3,2},{4,5},{5,4},{6,7},{7,6},{8,9},{9,8},{10,11... | collective-permute-start | bytes 12582920 | tf_op jit(solution)/shard_map/ppermute | solution.py:437
  966.2 148.3 %collective-permute-start.57 = (f32[1024,1024]{1,0:T(8,128)}, f32[1024,1024]{1,0:T(8,128)}, u32[]{:S(2)}, u32[]{:S(2)}) collective-permute-start(f32[1024,1024]{1,0:T(8,128)} %shard_map.133), channel_id=1, source_target_pairs={{0,8},{8,0},{1,9},{9,1},{2,10},{10,2},{3,11},{11,3},{4,12},{12,4},... | collective-permute-start | bytes 12582920 | tf_op jit(solution)/shard_map/ppermute | solution.py:540
  967.3 236.6 %collective-permute-start.56 = (f32[1024,1024]{1,0:T(8,128)}, f32[1024,1024]{1,0:T(8,128)}, u32[]{:S(2)}, u32[]{:S(2)}) collective-permute-start(f32[1024,1024]{1,0:T(8,128)} %shard_map.132), channel_id=1, source_target_pairs={{0,8},{8,0},{1,9},{9,1},{2,10},{10,2},{3,11},{11,3},{4,12},{12,4},... | collective-permute-start | bytes 12582920 | tf_op jit(solution)/shard_map/ppermute | solution.py:540
  969.0 47.6 %collective-permute-start.70 = (bf16[2,1024,256]{2,1,0:T(8,128)(2,1)S(1)}, bf16[2,1024,256]{2,1,0:T(8,128)(2,1)}, u32[]{:S(2)}, u32[]{:S(2)}) collective-permute-start(bf16[2,1024,256]{2,1,0:T(8,128)(2,1)S(1)} %collective-permute-done.68.refs_1_), channel_id=1, source_target_pairs={{0,1},{1,0},{2,3},{3,2},{4,5},{5,4},{6,7},{7,6},{8,9},{9,8},{10,11... | collective-permute-start | bytes 3145736 | tf_op jit(solution)/shard_map/ppermute | solution.py:437
  (126 other events, 3095.6 us)

commit v4 on v3

--- a/solution.py
+++ b/solution.py
@@ -12,6 +12,9 @@
 PIECE = 256
 HALF = 1024
 PER_CHUNK = 2
+ROWS = 512
+WIDE = 1024
+BLOCK = 256
 TANH_SCALE = math.sqrt(2.0 / math.pi)
 TANH_CUBE = 0.044715
 
@@ -29,7 +32,7 @@
 
 
 def hidden_of(u_ref, cot, w2, h_ref, dh_ref, before=lambda j: None):
-    width = 256
+    width = BLOCK
     for j in range(u_ref.shape[-1] // width):
         before(j)
         cols = slice(j * width, (j + 1) * width)
@@ -44,10 +47,10 @@
 
 
 def gram_product(left, right):
-    prod = dot(left[...], left[:256, :], NT) * dot(right[...], right[:256, :], NT)
-    corner = dot(left[256:, :], left[256:, :], NT) * dot(right[256:, :], right[256:, :], NT)
-    total = prod[:256] + 2.0 * prod[256:] + corner
-    return jnp.sum(total.reshape(32, 8, 256), axis=0)
+    prod = dot(left[...], left[:BLOCK, :], NT) * dot(right[...], right[:BLOCK, :], NT)
+    corner = dot(left[BLOCK:, :], left[BLOCK:, :], NT) * dot(right[BLOCK:, :], right[BLOCK:, :], NT)
+    total = prod[:BLOCK] + 2.0 * prod[BLOCK:] + corner
+    return jnp.sum(total.reshape(32, 8, BLOCK), axis=0)
 
 
 def backward_kernel(layer, micro, first_ex, x_first, from_slots, do_back, me_ref, *refs):
@@ -80,9 +83,6 @@
     def _():
         for i in range(2):
             w2_copy(i).start()
-        if do_back:
-            for i in range(8):
-                w1_copy(i).start()
 
     if not do_back:
         x_copy().start()
@@ -102,6 +102,9 @@
             @pl.when(step == 0)
             def _():
                 w2_copy(j // 2).wait()
+                if do_back and j == 0:
+                    for i in range(8):
+                        w1_copy(i).start()
 
     hidden_of(u_ref, cot, w2, h_ref, dh_ref, wait_weights)
     if do_back:
@@ -120,23 +123,23 @@
         norm_ref[...] = norm + gram_product(dh_ref, x_buf)
 
 
-NORM_SPEC = pl.BlockSpec((None, 8, 256), lambda e, *_: (e, 0, 0))
-NORM_SHAPE = jax.ShapeDtypeStruct((PER_CHUNK, 8, 256), jnp.float32)
-PART_SPEC = pl.BlockSpec((2, 2, 512, PIECE), lambda e, *_: (0, 0, e, 0))
-PART_SHAPE = jax.ShapeDtypeStruct((2, 2, PER_CHUNK * 512, PIECE), jnp.bfloat16)
+NORM_SPEC = pl.BlockSpec((None, 8, BLOCK), lambda e, *_: (e, 0, 0))
+NORM_SHAPE = jax.ShapeDtypeStruct((PER_CHUNK, 8, BLOCK), jnp.float32)
+PART_SPEC = pl.BlockSpec((2, 2, ROWS, PIECE), lambda e, *_: (0, 0, e, 0))
+PART_SHAPE = jax.ShapeDtypeStruct((2, 2, PER_CHUNK * ROWS, PIECE), jnp.bfloat16)
 ANY_SPEC = pl.BlockSpec(memory_space=pl.ANY)
 
 
 def backward_chunk(layer, micro, first_ex, x_first, me, dz_inputs, do_back, x_in, u_pre, w_up, w_down):
-    rows = PER_CHUNK * 512
+    rows = PER_CHUNK * ROWS
     hid, model = u_pre.shape[-1], w_up.shape[1]
     from_slots = isinstance(dz_inputs, tuple)
     if from_slots:
-        in_specs = [pl.BlockSpec((2, 512, PIECE), lambda e, m: (0, e, 0))] * 4
+        in_specs = [pl.BlockSpec((2, ROWS, PIECE), lambda e, m: (0, e, 0))] * 4
     else:
-        in_specs = [pl.BlockSpec((None, None, 512, model), lambda e, m: (micro, first_ex + e, 0, 0))]
+        in_specs = [pl.BlockSpec((None, None, ROWS, model), lambda e, m: (micro, first_ex + e, 0, 0))]
         dz_inputs = (dz_inputs,)
-    act_spec = pl.BlockSpec((512, hid), lambda e, m: (e, 0))
+    act_spec = pl.BlockSpec((ROWS, hid), lambda e, m: (e, 0))
     act_shape = jax.ShapeDtypeStruct((rows, hid), jnp.bfloat16)
     dz_cols = model if from_slots else PIECE
     if do_back:
@@ -144,16 +147,16 @@
         scratch = [pltpu.VMEM((8, PIECE, hid), jnp.bfloat16), pltpu.SemaphoreType.DMA((8,))]
     else:
         last_specs, last_shapes = [NORM_SPEC], [NORM_SHAPE]
-        scratch = [pltpu.VMEM((512, model), jnp.bfloat16), pltpu.SemaphoreType.DMA]
+        scratch = [pltpu.VMEM((ROWS, model), jnp.bfloat16), pltpu.SemaphoreType.DMA]
     return pl.pallas_call(
         functools.partial(backward_kernel, layer, micro, first_ex, x_first, from_slots, do_back),
         grid_spec=pltpu.PrefetchScalarGridSpec(
             num_scalar_prefetch=1,
             grid=(PER_CHUNK,),
             in_specs=in_specs
-            + [pl.BlockSpec((None, None, None, 512, hid), lambda e, m: (layer, micro, first_ex + e, 0, 0))]
+            + [pl.BlockSpec((None, None, None, ROWS, hid), lambda e, m: (layer, micro, first_ex + e, 0, 0))]
             + [ANY_SPEC] * 2,
-            out_specs=[act_spec, act_spec, pl.BlockSpec((512, dz_cols), lambda e, m: (e, 0))] + last_specs,
+            out_specs=[act_spec, act_spec, pl.BlockSpec((ROWS, dz_cols), lambda e, m: (e, 0))] + last_specs,
             scratch_shapes=[pltpu.VMEM((hid, model), jnp.bfloat16), pltpu.SemaphoreType.DMA((2,))] + scratch,
         ),
         out_shape=[act_shape, act_shape, jax.ShapeDtypeStruct((rows, dz_cols), jnp.bfloat16)] + last_shapes,
@@ -168,12 +171,12 @@
 
 def norm_chunk(layer, micro, first_ex, hidden, d_hid, cot, x_in):
     hid, model = hidden.shape[1], x_in.shape[-1]
-    act_spec = pl.BlockSpec((512, hid), lambda e: (e, 0))
+    act_spec = pl.BlockSpec((ROWS, hid), lambda e: (e, 0))
     if cot.ndim == 4:
-        cot_spec = pl.BlockSpec((None, None, 512, model), lambda e: (micro, first_ex + e, 0, 0))
+        cot_spec = pl.BlockSpec((None, None, ROWS, model), lambda e: (micro, first_ex + e, 0, 0))
     else:
-        cot_spec = pl.BlockSpec((512, model), lambda e: (e, 0))
-    x_spec = pl.BlockSpec((None, None, None, 512, model), lambda e: (layer, micro, first_ex + e, 0, 0))
+        cot_spec = pl.BlockSpec((ROWS, model), lambda e: (e, 0))
+    x_spec = pl.BlockSpec((None, None, None, ROWS, model), lambda e: (layer, micro, first_ex + e, 0, 0))
     return pl.pallas_call(
         norm_kernel,
         grid=(PER_CHUNK,),
@@ -181,7 +184,7 @@
         out_specs=NORM_SPEC,
         out_shape=NORM_SHAPE,
         compiler_params=pltpu.CompilerParams(dimension_semantics=("arbitrary",)),
-        cost_estimate=pl.CostEstimate(flops=3 * PER_CHUNK * 512 * 512 * (hid + model), bytes_accessed=12 << 20, transcendentals=0),
+        cost_estimate=pl.CostEstimate(flops=3 * PER_CHUNK * ROWS * ROWS * (hid + model), bytes_accessed=12 << 20, transcendentals=0),
     )(hidden, d_hid, cot, x_in)
 
 
@@ -202,7 +205,7 @@
             num_scalar_prefetch=1,
             grid=(PER_CHUNK,),
             in_specs=[
-                pl.BlockSpec((512, hid), lambda e, m: (e, 0)),
+                pl.BlockSpec((ROWS, hid), lambda e, m: (e, 0)),
                 pl.BlockSpec((None, model, hid), lambda e, m: (layer, 0, 0)),
             ],
             out_specs=[PART_SPEC] * 2,
@@ -230,14 +233,14 @@
 
     def view(ref, kind, e):
         layer, cols = kind
-        cols = pl.ds(pl.multiple_of(half * HALF, HALF), HALF) if cols else pl.ds(0, 1024)
+        cols = pl.ds(pl.multiple_of(half * HALF, HALF), HALF) if cols else pl.ds(0, WIDE)
         if layer is not None:
             return ref.at[layer, e // 4, e % 4, :, cols]
         if len(ref.shape) == 4:
             return ref.at[e // 4, e % 4, :, cols]
         if len(ref.shape) == 3:
             return ref.at[e, :, cols]
-        return ref.at[pl.ds(pl.multiple_of(e * 512, 512), 512), cols]
+        return ref.at[pl.ds(pl.multiple_of(e * ROWS, ROWS), ROWS), cols]
 
     def fetch(at, slot):
         for start, count, left, left_kind, left_first, right, right_kind, right_first in segs:
@@ -270,7 +273,7 @@
     pltpu.make_async_copy(b_buf.at[slot], b_buf.at[slot], b_sem.at[slot]).wait()
     scaled = (b_buf[slot].astype(jnp.float32) * clip_ref[step]).astype(jnp.bfloat16)
     for j in range(2):
-        cols = slice(j * 512, (j + 1) * 512)
+        cols = slice(j * ROWS, (j + 1) * ROWS)
         out_ref[:, cols] += dot(a_buf[slot], scaled[:, cols], TN)
 
     if has_init or has_got:
@@ -305,8 +308,8 @@
     smem_spec = pl.BlockSpec(memory_space=pltpu.SMEM)
     operands, in_specs = [clip], [smem_spec]
     scratch = [
-        pltpu.VMEM((2, 512, 1024), jnp.bfloat16),
-        pltpu.VMEM((2, 512, 1024), jnp.bfloat16),
+        pltpu.VMEM((2, ROWS, WIDE), jnp.bfloat16),
+        pltpu.VMEM((2, ROWS, WIDE), jnp.bfloat16),
         pltpu.SemaphoreType.DMA((2,)),
         pltpu.SemaphoreType.DMA((2,)),
     ]
@@ -319,12 +322,12 @@
         if value is not None:
             operands.append(value)
             in_specs.append(any_spec)
-            scratch += [pltpu.VMEM((1024, 1024), jnp.float32), pltpu.SemaphoreType.DMA]
+            scratch += [pltpu.VMEM((WIDE, WIDE), jnp.float32), pltpu.SemaphoreType.DMA]
     aliases = {}
-    out_spec, out_shape = pl.BlockSpec((1024, 1024), lambda s, h: (0, 0)), (1024, 1024)
+    out_spec, out_shape = pl.BlockSpec((WIDE, WIDE), lambda s, h: (0, 0)), (WIDE, WIDE)
     if result is not None:
         out_layer, n_layers, buffer = result
-        out_spec, out_shape = pl.BlockSpec((None, 1024, 1024), lambda s, h: (out_layer, 0, 0)), (n_layers, 1024, 1024)
+        out_spec, out_shape = pl.BlockSpec((None, WIDE, WIDE), lambda s, h: (out_layer, 0, 0)), (n_layers, WIDE, WIDE)
         if buffer is not None:
             aliases = {len(operands) + 1: 0}
             operands.append(buffer)
@@ -339,7 +342,7 @@
         out_shape=jax.ShapeDtypeStruct(out_shape, jnp.float32),
         input_output_aliases=aliases,
         compiler_params=pltpu.CompilerParams(dimension_semantics=("arbitrary",)),
-        cost_estimate=pl.CostEstimate(flops=2 * at * 512 * 1024 * 1024, bytes_accessed=24 << 20, transcendentals=0),
+        cost_estimate=pl.CostEstimate(flops=2 * at * ROWS * WIDE * WIDE, bytes_accessed=24 << 20, transcendentals=0),
     )(half, *operands)
 
 
@@ -350,23 +353,23 @@
 def hidden_again(layer, from_micro, u_other, cot_other, w_down):
     n_ex, _, model = cot_other.shape
     hid = u_other.shape[-1]
-    act_spec = pl.BlockSpec((512, hid), lambda e, m: (e, 0))
-    act_shape = jax.ShapeDtypeStruct((n_ex * 512, hid), jnp.bfloat16)
+    act_spec = pl.BlockSpec((ROWS, hid), lambda e, m: (e, 0))
+    act_shape = jax.ShapeDtypeStruct((n_ex * ROWS, hid), jnp.bfloat16)
     return pl.pallas_call(
         hidden_kernel,
         grid_spec=pltpu.PrefetchScalarGridSpec(
             num_scalar_prefetch=1,
             grid=(n_ex,),
             in_specs=[
-                pl.BlockSpec((None, None, 512, hid), lambda e, m: (m[0], e, 0, 0)),
-                pl.BlockSpec((None, 512, model), lambda e, m: (e, 0, 0)),
+                pl.BlockSpec((None, None, ROWS, hid), lambda e, m: (m[0], e, 0, 0)),
+                pl.BlockSpec((None, ROWS, model), lambda e, m: (e, 0, 0)),
                 pl.BlockSpec((None, hid, model), lambda e, m: (layer, 0, 0)),
             ],
             out_specs=[act_spec, act_spec],
         ),
         out_shape=[act_shape, act_shape],
         compiler_params=pltpu.CompilerParams(dimension_semantics=("arbitrary",)),
-        cost_estimate=pl.CostEstimate(flops=2 * n_ex * 512 * hid * model, bytes_accessed=24 << 20, transcendentals=n_ex * 512 * hid),
+        cost_estimate=pl.CostEstimate(flops=2 * n_ex * ROWS * hid * model, bytes_accessed=24 << 20, transcendentals=n_ex * ROWS * hid),
         name="hidden_again",
     )(from_micro, u_other, cot_other, w_down)
 
@@ -377,7 +380,7 @@
 
 
 def finish_grad(layer, n_layers, examples, own, got, buffer):
-    spec = pl.BlockSpec((256, 1024), lambda i: (i, 0))
+    spec = pl.BlockSpec((BLOCK, WIDE), lambda i: (i, 0))
     operands = (own,) if got is None else (own, got)
     in_specs, aliases = [spec] * len(operands), {}
     if buffer is not None:
@@ -388,8 +391,8 @@
         functools.partial(finish_kernel, 1.0 / examples, got is not None),
         grid=(4,),
         in_specs=in_specs,
-        out_specs=pl.BlockSpec((None, 256, 1024), lambda i: (layer, i, 0)),
-        out_shape=jax.ShapeDtypeStruct((n_layers, 1024, 1024), jnp.float32),
+        out_specs=pl.BlockSpec((None, BLOCK, WIDE), lambda i: (layer, i, 0)),
+        out_shape=jax.ShapeDtypeStruct((n_layers, WIDE, WIDE), jnp.float32),
         input_output_aliases=aliases,
         compiler_params=pltpu.CompilerParams(dimension_semantics=("arbitrary",)),
         cost_estimate=pl.CostEstimate(flops=12 << 20, bytes_accessed=12 << 20, transcendentals=0),
@@ -412,7 +415,7 @@
 
 def join_slots(me, orders, chunks, shape):
     def spec(k):
-        return pl.BlockSpec((2, 512, PIECE), lambda s, m: (0, jnp.clip(s - PER_CHUNK * k, 0, PER_CHUNK - 1), 0))
+        return pl.BlockSpec((2, ROWS, PIECE), lambda s, m: (0, jnp.clip(s - PER_CHUNK * k, 0, PER_CHUNK - 1), 0))
 
     return pl.pallas_call(
         functools.partial(join_kernel, orders),
@@ -420,7 +423,7 @@
             num_scalar_prefetch=1,
             grid=(len(orders) * PER_CHUNK,),
             in_specs=[spec(k) for k in range(len(orders)) for _ in range(4)],
-            out_specs=pl.BlockSpec((None, None, 512, shape[-1]), lambda s, m: (s // 4, s % 4, 0, 0)),
+            out_specs=pl.BlockSpec((None, None, ROWS, shape[-1]), lambda s, m: (s // 4, s % 4, 0, 0)),
         ),
         out_shape=jax.ShapeDtypeStruct(shape, jnp.bfloat16),
         compiler_params=pltpu.CompilerParams(dimension_semantics=("arbitrary",)),

time: 1230 us -> 1230 us (level)
  transfers between devices with their start and end apart: 94 -> 94, of which waited for: 30 -> 30; matrix products, arithmetic and copies ran while one was open for 7% -> 8% of each run, Pallas kernels for 44% -> 44%
where the time goes in v4:
time: 1230 us; the launch traced here: 1220 us
  Pallas kernels  566 us (46%)
  waiting for transfers between devices  480 us (39%)
  other arithmetic  70.7 us (6%)
  starting transfers between devices  60.7 us (5%)
  local copies, waits for them, and re-layouts  22.2 us (2%)
  blocking collectives  13.3 us (1%)
    ppermute x86, waiting for transfers between devices, swap(): return lax.ppermute(value, 'tp', [(i, i ^ mask) for i in range(tp_size)])  233 us
    pallas_call x12, Pallas kernels, backward_chunk(): pl.pallas_call(functools.partial(backward_kernel, layer, micro, first_ex,...  209 us
    pallas_call x10, Pallas kernels, weight_grad(): pl.pallas_call(functools.partial(grad_kernel, table, len(lhs), len(rhs),...  194 us
    ppermute x4, waiting for transfers between devices, local_pass(): got.append(lax.ppermute(part, 'dp', swap_dp))  118 us
    ppermute x1, waiting for transfers between devices, local_pass(): clip_other = lax.ppermute(clip, 'dp', swap_dp)  87.8 us
    pallas_call x8, Pallas kernels, norm_chunk(): pl.pallas_call(norm_kernel, grid=(PER_CHUNK,), in_specs=[act_spec, act_sp...  71.1 us
    ppermute x86, starting transfers between devices, swap(): return lax.ppermute(value, 'tp', [(i, i ^ mask) for i in range(tp_size)])  50.8 us
    convert_element_type x24, other arithmetic, add(): return (a.astype(jnp.float32) + b.astype(jnp.float32)).astype(jnp.bfloat16)  44.7 us
  transfers between devices with their start and end apart: 94, of which 30 were waited for; matrix products, arithmetic and copies ran while one was open for 8% of the time, Pallas kernels for 44%

profile of v4, /device:TPU:0, one launch (start us, length us, event | category | flops | bytes accessed | tf_op | source)
XLA Modules:
  0.0 1215.4 jit_solution(17038176900630974385)
XLA Ops:
  0.6 16.9 %shard_map.112 = (bf16[1024,1024]{1,0:T(8,128)(2,1)}, bf16[1024,1024]{1,0:T(8,128)(2,1)}, bf16[1024,256]{1,0:T(8,128)(2,1)}, bf16[2,2,1024,256]{3,2,1,0:T(8,128)(2,1)}, bf16[2,2,1024,256]{3,2,1,0:T(8,128)(2,1)}) custom-call(s32[1]{0:T(128)} %bitcast.2.me_ref, bf16[2,4,512,2048]{3,2,1,0:T(8,128)(2,1)} %refs_7_.1, bf16[3,2,4,512,1024]{4,3,2,1,0:T(8,128)(2,1)} %refs_4_.15, ...), custom_call_target="tpu_custom_call" | custom-call | flops 8589934592 | bytes 25165824 | tf_op jit(solution)/shard_map/pallas_call | solution.py:151
  18.3 17.0 %shard_map.114 = (bf16[1024,1024]{1,0:T(8,128)(2,1)}, bf16[1024,1024]{1,0:T(8,128)(2,1)}, bf16[1024,256]{1,0:T(8,128)(2,1)}, bf16[2,2,1024,256]{3,2,1,0:T(8,128)(2,1)}, bf16[2,2,1024,256]{3,2,1,0:T(8,128)(2,1)}) custom-call(s32[1]{0:T(128)} %bitcast.2.me_ref, bf16[2,4,512,2048]{3,2,1,0:T(8,128)(2,1)} %refs_7_.1, bf16[3,2,4,512,1024]{4,3,2,1,0:T(8,128)(2,1)} %refs_4_.15, ...), custom_call_target="tpu_custom_call" | custom-call | flops 8589934592 | bytes 25165824 | tf_op jit(solution)/shard_map/pallas_call | solution.py:151
  35.4 17.5 %shard_map.118 = (bf16[1024,1024]{1,0:T(8,128)(2,1)}, bf16[1024,1024]{1,0:T(8,128)(2,1)}, bf16[1024,256]{1,0:T(8,128)(2,1)}, bf16[2,2,1024,256]{3,2,1,0:T(8,128)(2,1)}, bf16[2,2,1024,256]{3,2,1,0:T(8,128)(2,1)}) custom-call(s32[1]{0:T(128)} %bitcast.2.me_ref, bf16[2,4,512,2048]{3,2,1,0:T(8,128)(2,1)} %refs_7_.1, bf16[3,2,4,512,1024]{4,3,2,1,0:T(8,128)(2,1)} %refs_4_.15, ...), custom_call_target="tpu_custom_call" | custom-call | flops 8589934592 | bytes 25165824 | tf_op jit(solution)/shard_map/pallas_call | solution.py:151
  53.4 17.2 %shard_map.116 = (bf16[1024,1024]{1,0:T(8,128)(2,1)}, bf16[1024,1024]{1,0:T(8,128)(2,1)}, bf16[1024,256]{1,0:T(8,128)(2,1)}, bf16[2,2,1024,256]{3,2,1,0:T(8,128)(2,1)}, bf16[2,2,1024,256]{3,2,1,0:T(8,128)(2,1)}) custom-call(s32[1]{0:T(128)} %bitcast.2.me_ref, bf16[2,4,512,2048]{3,2,1,0:T(8,128)(2,1)} %refs_7_.1, bf16[3,2,4,512,1024]{4,3,2,1,0:T(8,128)(2,1)} %refs_4_.15, ...), custom_call_target="tpu_custom_call" | custom-call | flops 8589934592 | bytes 25165824 | tf_op jit(solution)/shard_map/pallas_call | solution.py:151
  82.5 16.7 %collective-permute-done.1 = bf16[2,1024,256]{2,1,0:T(8,128)(2,1)S(1)} collective-permute-done((bf16[2,1024,256]{2,1,0:T(8,128)(2,1)S(1)}, bf16[2,1024,256]{2,1,0:T(8,128)(2,1)S(1)}, u32[]{:S(2)}, u32[]{:S(2)}) %collective-permute-start.1) | collective-permute-done | bytes 1048608 | tf_op jit(solution)/shard_map/ppermute | solution.py:440
  104.4 32.3 %collective-permute-done.2 = bf16[1024,256]{1,0:T(8,128)(2,1)S(1)} collective-permute-done((bf16[1024,256]{1,0:T(8,128)(2,1)S(1)}, bf16[1024,256]{1,0:T(8,128)(2,1)S(1)}, u32[]{:S(2)}, u32[]{:S(2)}) %collective-permute-start.2) | collective-permute-done | bytes 524320 | tf_op jit(solution)/shard_map/ppermute | solution.py:440
  166.3 29.8 %collective-permute-done.24 = bf16[1024,256]{1,0:T(8,128)(2,1)S(1)} collective-permute-done((bf16[1024,256]{1,0:T(8,128)(2,1)S(1)}, bf16[1024,256]{1,0:T(8,128)(2,1)S(1)}, u32[]{:S(2)}, u32[]{:S(2)}) %collective-permute-start.24) | collective-permute-done | bytes 524320 | tf_op jit(solution)/shard_map/ppermute | solution.py:440
  198.6 31.7 %collective-permute-done.17 = bf16[1024,256]{1,0:T(8,128)(2,1)S(1)} collective-permute-done((bf16[1024,256]{1,0:T(8,128)(2,1)S(1)}, bf16[1024,256]{1,0:T(8,128)(2,1)S(1)}, u32[]{:S(2)}, u32[]{:S(2)}) %collective-permute-start.17) | collective-permute-done | bytes 524320 | tf_op jit(solution)/shard_map/ppermute | solution.py:440
  233.7 17.2 %shard_map.120 = (bf16[1024,1024]{1,0:T(8,128)(2,1)}, bf16[1024,1024]{1,0:T(8,128)(2,1)}, bf16[1024,2048]{1,0:T(8,128)(2,1)}, bf16[2,2,1024,256]{3,2,1,0:T(8,128)(2,1)}, bf16[2,2,1024,256]{3,2,1,0:T(8,128)(2,1)}) custom-call(s32[1]{0:T(128)} %bitcast.2.me_ref, bf16[2,1024,256]{2,1,0:T(8,128)(2,1)} %copy-done.14, ...), custom_call_target="tpu_custom_call" | custom-call | flops 8589934592 | bytes 25165824 | tf_op jit(solution)/shard_map/pallas_call | solution.py:151
  258.8 17.4 %shard_map.122 = (bf16[1024,1024]{1,0:T(8,128)(2,1)}, bf16[1024,1024]{1,0:T(8,128)(2,1)}, bf16[1024,2048]{1,0:T(8,128)(2,1)}, bf16[2,2,1024,256]{3,2,1,0:T(8,128)(2,1)}, bf16[2,2,1024,256]{3,2,1,0:T(8,128)(2,1)}) custom-call(s32[1]{0:T(128)} %bitcast.2.me_ref, bf16[2,1024,256]{2,1,0:T(8,128)(2,1)} %pad_maximum_fusion.1.refs_0_, ...), custom_call_target="tpu_custom_call" | custom-call | flops 8589934592 | bytes 25165824 | tf_op jit(solution)/shard_map/pallas_call | solution.py:151
  276.3 17.2 %shard_map.126 = (bf16[1024,1024]{1,0:T(8,128)(2,1)}, bf16[1024,1024]{1,0:T(8,128)(2,1)}, bf16[1024,2048]{1,0:T(8,128)(2,1)}, bf16[2,2,1024,256]{3,2,1,0:T(8,128)(2,1)}, bf16[2,2,1024,256]{3,2,1,0:T(8,128)(2,1)}) custom-call(s32[1]{0:T(128)} %bitcast.2.me_ref, bf16[2,1024,256]{2,1,0:T(8,128)(2,1)} %copy-done.13, ...), custom_call_target="tpu_custom_call" | custom-call | flops 8589934592 | bytes 25165824 | tf_op jit(solution)/shard_map/pallas_call | solution.py:151
  294.1 17.7 %shard_map.124 = (bf16[1024,1024]{1,0:T(8,128)(2,1)}, bf16[1024,1024]{1,0:T(8,128)(2,1)}, bf16[1024,2048]{1,0:T(8,128)(2,1)}, bf16[2,2,1024,256]{3,2,1,0:T(8,128)(2,1)}, bf16[2,2,1024,256]{3,2,1,0:T(8,128)(2,1)}) custom-call(s32[1]{0:T(128)} %bitcast.2.me_ref, bf16[2,1024,256]{2,1,0:T(8,128)(2,1)} %pad_maximum_fusion.2.refs_0_, ...), custom_call_target="tpu_custom_call" | custom-call | flops 8589934592 | bytes 25165824 | tf_op jit(solution)/shard_map/pallas_call | solution.py:151
  366.4 19.5 %collective-permute-done.36 = bf16[2,1024,256]{2,1,0:T(8,128)(2,1)} collective-permute-done((bf16[2,1024,256]{2,1,0:T(8,128)(2,1)}, bf16[2,1024,256]{2,1,0:T(8,128)(2,1)}, u32[]{:S(2)}, u32[]{:S(2)}) %collective-permute-start.36) | collective-permute-done | bytes 1048608 | tf_op jit(solution)/shard_map/ppermute | solution.py:440
  486.6 17.6 %shard_map.131 = (bf16[1024,1024]{1,0:T(8,128)(2,1)}, bf16[1024,1024]{1,0:T(8,128)(2,1)}, bf16[1024,2048]{1,0:T(8,128)(2,1)}, f32[2,8,256]{2,1,0:T(8,128)}) custom-call(s32[1]{0:T(128)} %bitcast.2.me_ref, bf16[2,1024,256]{2,1,0:T(8,128)(2,1)} %pad_maximum_fusion.7.refs_0_, bf16[2,1024,256]{2,1,0:T(8,128)(2,1)} %collective-permute-done.53.refs_1_, ...), custom_call_target="tpu_custom_call" | custom-call | flops 8589934592 | bytes 25165824 | tf_op jit(solution)/shard_map/pallas_call | solution.py:151
  514.2 17.9 %shard_map.129 = (bf16[1024,1024]{1,0:T(8,128)(2,1)}, bf16[1024,1024]{1,0:T(8,128)(2,1)}, bf16[1024,2048]{1,0:T(8,128)(2,1)}, f32[2,8,256]{2,1,0:T(8,128)}) custom-call(s32[1]{0:T(128)} %bitcast.2.me_ref, bf16[2,1024,256]{2,1,0:T(8,128)(2,1)} %copy-done.8, bf16[2,1024,256]{2,1,0:T(8,128)(2,1)} %collective-permute-done.39.refs_1_, ...), custom_call_target="tpu_custom_call" | custom-call | flops 8589934592 | bytes 25165824 | tf_op jit(solution)/shard_map/pallas_call | solution.py:151
  532.8 17.5 %shard_map.130 = (bf16[1024,1024]{1,0:T(8,128)(2,1)}, bf16[1024,1024]{1,0:T(8,128)(2,1)}, bf16[1024,2048]{1,0:T(8,128)(2,1)}, f32[2,8,256]{2,1,0:T(8,128)}) custom-call(s32[1]{0:T(128)} %bitcast.2.me_ref, bf16[2,1024,256]{2,1,0:T(8,128)(2,1)} %pad_maximum_fusion.6.refs_0_, bf16[2,1024,256]{2,1,0:T(8,128)(2,1)} %collective-permute-done.46.refs_1_, ...), custom_call_target="tpu_custom_call" | custom-call | flops 8589934592 | bytes 25165824 | tf_op jit(solution)/shard_map/pallas_call | solution.py:151
  568.4 17.5 %shard_map.128 = (bf16[1024,1024]{1,0:T(8,128)(2,1)}, bf16[1024,1024]{1,0:T(8,128)(2,1)}, bf16[1024,2048]{1,0:T(8,128)(2,1)}, f32[2,8,256]{2,1,0:T(8,128)}) custom-call(s32[1]{0:T(128)} %bitcast.2.me_ref, bf16[2,1024,256]{2,1,0:T(8,128)(2,1)} %copy-done.9, bf16[2,1024,256]{2,1,0:T(8,128)(2,1)} %copy-done.39, ...), custom_call_target="tpu_custom_call" | custom-call | flops 8589934592 | bytes 25165824 | tf_op jit(solution)/shard_map/pallas_call | solution.py:151
  651.6 32.1 %collective-permute-done.60.u_ref = bf16[2,4,512,1024]{3,2,1,0:T(8,128)(2,1)} collective-permute-done((bf16[2,4,512,1024]{3,2,1,0:T(8,128)(2,1)}, bf16[2,4,512,1024]{3,2,1,0:T(8,128)(2,1)}, u32[]{:S(2)}, u32[]{:S(2)}) %collective-permute-start.60) | collective-permute-done | bytes 8388640 | tf_op jit(solution)/shard_map/ppermute | solution.py:478
  745.6 18.0 %hidden_again.2 = (bf16[2048,1024]{1,0:T(8,128)(2,1)}, bf16[2048,1024]{1,0:T(8,128)(2,1)}) custom-call(s32[1]{0:T(128)} %bitcast.63.from_ref, bf16[2,4,512,1024]{3,2,1,0:T(8,128)(2,1)} %collective-permute-done.60.u_ref, bf16[4,512,2048]{2,1,0:T(8,128)(2,1)} %collective-permute-done.61.dz_ref.refs_8_, bf16[3,1024,2048]{2,1,0:T(8,128)(2,1)} %w2_ref.3), custom_call_target="tpu_custom_call" | custom-call | flops 8589934592 | bytes 25165824 | tf_op jit(solution)/shard_map/hidden_again/pallas_call | solution.py:358
  775.2 87.8 %collective-permute-done.59 = f32[8]{0:T(128)S(1)} collective-permute-done((f32[8]{0:T(128)S(1)}, f32[8]{0:T(128)S(1)}, u32[]{:S(2)}, u32[]{:S(2)}) %collective-permute-start.59) | collective-permute-done | bytes 64 | tf_op jit(solution)/shard_map/ppermute | solution.py:503
  889.2 15.9 %shard_map.138 = f32[1024,1024]{1,0:T(8,128)} custom-call(s32[1]{0:T(128)} %bitcast.61.half_ref, f32[8]{0:T(128)} %multiply_minimum_fusion.clip_ref, bf16[1024,1024]{1,0:T(8,128)(2,1)} %get-tuple-element.131.refs_1_.refs_0_, bf16[1024,1024]{1,0:T(8,128)(2,1)} %get-tuple-element.132.refs_2_.refs_1_, bf16[1024,1024]{1,0:T(8,128)(2,1)} %get-tuple-element.133.refs_3_.refs_2_, ...), custom_call_target="tpu_custom_call" | custom-call | flops 8589934592 | bytes 25165824 | tf_op jit(solution)/shard_map/pallas_call | solution.py:335
  905.1 17.9 %hidden_again.3 = (bf16[2048,1024]{1,0:T(8,128)(2,1)}, bf16[2048,1024]{1,0:T(8,128)(2,1)}) custom-call(s32[1]{0:T(128)} %bitcast.66.from_ref, bf16[2,4,512,1024]{3,2,1,0:T(8,128)(2,1)} %collective-permute-done.60.u_ref, bf16[4,512,2048]{2,1,0:T(8,128)(2,1)} %collective-permute-done.62.dz_ref.refs_9_, bf16[3,1024,2048]{2,1,0:T(8,128)(2,1)} %w2_ref.3), custom_call_target="tpu_custom_call" | custom-call | flops 8589934592 | bytes 25165824 | tf_op jit(solution)/shard_map/hidden_again/pallas_call | solution.py:358
  925.8 15.6 %shard_map.132 = f32[1024,1024]{1,0:T(8,128)} custom-call(s32[1]{0:T(128)} %bitcast.61.half_ref, f32[8]{0:T(128)} %multiply_minimum_fusion.clip_ref, bf16[3,2,4,512,2048]{4,3,2,1,0:T(8,128)(2,1)} %refs_1_.13, bf16[1024,1024]{1,0:T(8,128)(2,1)} %get-tuple-element.121.refs_1_.refs_2_.dh_ref, bf16[1024,1024]{1,0:T(8,128)(2,1)} %get-tuple-element.122.refs_2_.refs_3_.dh_ref, ...), custom_call_target="tpu_custom_call" | custom-call | flops 8589934592 | bytes 25165824 | tf_op jit(solution)/shard_map/pallas_call | solution.py:335
  941.4 16.9 %shard_map.137.own_ref = f32[1024,1024]{1,0:T(8,128)} custom-call(s32[1]{0:T(128)} %bitcast.half_ref, f32[8]{0:T(128)} %multiply_minimum_fusion.clip_ref, f32[1]{0:T(128)} %bitcast.60.refs_0_, bf16[1024,1024]{1,0:T(8,128)(2,1)} %get-tuple-element.131.refs_1_.refs_0_, bf16[1024,1024]{1,0:T(8,128)(2,1)} %get-tuple-element.132.refs_2_.refs_1_, ...), custom_call_target="tpu_custom_call" | custom-call | flops 8589934592 | bytes 25165824 | tf_op jit(solution)/shard_map/pallas_call | solution.py:335
  961.2 28.6 %shard_map.140.refs_11_ = f32[3,1024,1024]{2,1,0:T(8,128)} custom-call(s32[1]{0:T(128)} %bitcast.half_ref, f32[16]{0:T(128)} %pad_maximum_fusion.13.clip_ref, f32[1]{0:T(128)} %bitcast.60.refs_0_, bf16[1024,1024]{1,0:T(8,128)(2,1)} %get-tuple-element.77.h_ref.refs_1_, bf16[1024,1024]{1,0:T(8,128)(2,1)} %get-tuple-element.79.h_ref.refs_2_, ...), custom_call_target="tpu_custom_call" | custom-call | flops 17179869184 | bytes 25165824 | tf_op jit(solution)/shard_map/pallas_call | solution.py:335
  989.8 19.0 %shard_map.141.refs_1_ = f32[3,1024,1024]{2,1,0:T(8,128)} custom-call(s32[1]{0:T(128)} %bitcast.half_ref, f32[8]{0:T(128)} %multiply_minimum_fusion.clip_ref, f32[1]{0:T(128)} %bitcast.60.refs_0_, bf16[1024,1024]{1,0:T(8,128)(2,1)} %get-tuple-element.88.h_ref.refs_0_.refs_1_, ...), custom_call_target="tpu_custom_call", output_to_operand_aliasing={{}: (13, {})} | custom-call | flops 8589934592 | bytes 25165824 | tf_op jit(solution)/shard_map/pallas_call | solution.py:335
  1008.8 15.7 %join_d_in.1 = bf16[2,4,512,2048]{3,2,1,0:T(8,128)(2,1)} custom-call(s32[1]{0:T(128)} %bitcast.2.me_ref, bf16[2,1024,256]{2,1,0:T(8,128)(2,1)} %pad_maximum_fusion.8.refs_0_, bf16[2,1024,256]{2,1,0:T(8,128)(2,1)} %copy-done.40, bf16[2,1024,256]{2,1,0:T(8,128)(2,1)} %collective-permute-done.69.refs_2_, bf16[2,1024,256]{2,1,0:T(8,128)(2,1)} %collective-permute-done.70.refs_3_, ...), custom_call_target="tpu_custom_call" | custom-call | flops 33554432 | bytes 33554432 | tf_op jit(solution)/shard_map/join_d_in/pallas_call | solution.py:420
  1030.3 28.6 %shard_map.134.refs_8_ = f32[3,1024,1024]{2,1,0:T(8,128)} custom-call(s32[1]{0:T(128)} %bitcast.half_ref, f32[16]{0:T(128)} %pad_maximum_fusion.13.clip_ref, f32[1]{0:T(128)} %bitcast.60.refs_0_, bf16[3,2,4,512,2048]{4,3,2,1,0:T(8,128)(2,1)} %refs_1_.13, bf16[4,512,1024]{2,1,0:T(8,128)(2,1)} %collective-permute-done.58.refs_2_, ...), custom_call_target="tpu_custom_call" | custom-call | flops 17179869184 | bytes 25165824 | tf_op jit(solution)/shard_map/pallas_call | solution.py:335
  1058.8 47.8 %collective-permute-done.57.refs_7_ = f32[1024,1024]{1,0:T(8,128)} collective-permute-done((f32[1024,1024]{1,0:T(8,128)}, f32[1024,1024]{1,0:T(8,128)}, u32[]{:S(2)}, u32[]{:S(2)}) %collective-permute-start.57) | collective-permute-done | bytes 4194336 | tf_op jit(solution)/shard_map/ppermute | solution.py:543
  1106.7 18.7 %shard_map.135.refs_8_ = f32[3,1024,1024]{2,1,0:T(8,128)} custom-call(s32[1]{0:T(128)} %bitcast.half_ref, f32[8]{0:T(128)} %multiply_minimum_fusion.clip_ref, f32[1]{0:T(128)} %bitcast.60.refs_0_, bf16[3,2,4,512,2048]{4,3,2,1,0:T(8,128)(2,1)} %refs_1_.13, ...), custom_call_target="tpu_custom_call", output_to_operand_aliasing={{}: (10, {})} | custom-call | flops 8589934592 | bytes 25165824 | tf_op jit(solution)/shard_map/pallas_call | solution.py:335
  1125.4 70.6 %collective-permute-done.56.refs_7_ = f32[1024,1024]{1,0:T(8,128)} collective-permute-done((f32[1024,1024]{1,0:T(8,128)}, f32[1024,1024]{1,0:T(8,128)}, u32[]{:S(2)}, u32[]{:S(2)}) %collective-permute-start.56) | collective-permute-done | bytes 4194336 | tf_op jit(solution)/shard_map/ppermute | solution.py:543
  1196.1 19.0 %shard_map.136 = f32[3,1024,1024]{2,1,0:T(8,128)} custom-call(s32[1]{0:T(128)} %bitcast.half_ref, f32[8]{0:T(128)} %multiply_minimum_fusion.clip_ref, f32[1]{0:T(128)} %bitcast.60.refs_0_, bf16[3,2,4,512,2048]{4,3,2,1,0:T(8,128)(2,1)} %refs_1_.13, bf16[1024,1024]{1,0:T(8,128)(2,1)} %get-tuple-element.121.refs_1_.refs_2_.dh_ref, ...), custom_call_target="tpu_custom_call", output_to_operand_aliasing={{}: (10, {})} | custom-call | flops 8589934592 | bytes 25165824 | tf_op jit(solution)/shard_map/pallas_call | solution.py:335
  (379 shorter events, 420.9 us)
Async XLA Ops:
  17.6 53.1 %collective-permute-start = (bf16[2,2,1024,256]{3,2,1,0:T(8,128)(2,1)}, bf16[2,2,1024,256]{3,2,1,0:T(8,128)(2,1)}, u32[]{:S(2)}, u32[]{:S(2)}) collective-permute-start(bf16[2,2,1024,256]{3,2,1,0:T(8,128)(2,1)} %get-tuple-element.87), channel_id=1, source_target_pairs={{0,1},{1,0},{2,3},{3,2},{4,5},{5,4},{6,7},{7,6},{8,9},{9,8},{10,11... | collective-permute-start | bytes 6291464 | tf_op jit(solution)/shard_map/ppermute | solution.py:440
  82.0 56.6 %collective-permute-start.22 = (bf16[2,1024,256]{2,1,0:T(8,128)(2,1)S(1)}, bf16[2,1024,256]{2,1,0:T(8,128)(2,1)S(1)}, u32[]{:S(2)}, u32[]{:S(2)}) collective-permute-start(bf16[2,1024,256]{2,1,0:T(8,128)(2,1)S(1)} %get-tuple-element.174), channel_id=1, source_target_pairs={{0,4},{1,5},{2,6},{3,7},{4,0},{5,1},{6,2},{7,3},{8,12},{9,13},{10,... | collective-permute-start | bytes 3145736 | tf_op jit(solution)/shard_map/ppermute | solution.py:440
  101.7 52.6 %collective-permute-start.15 = (bf16[2,1024,256]{2,1,0:T(8,128)(2,1)S(1)}, bf16[2,1024,256]{2,1,0:T(8,128)(2,1)S(1)}, u32[]{:S(2)}, u32[]{:S(2)}) collective-permute-start(bf16[2,1024,256]{2,1,0:T(8,128)(2,1)S(1)} %get-tuple-element.172), channel_id=1, source_target_pairs={{0,2},{1,3},{2,0},{3,1},{4,6},{5,7},{6,4},{7,5},{8,10},{9,11},{10,... | collective-permute-start | bytes 3145736 | tf_op jit(solution)/shard_map/ppermute | solution.py:440
  149.9 46.9 %collective-permute-start.4 = (bf16[2,1024,256]{2,1,0:T(8,128)(2,1)S(1)}, bf16[2,1024,256]{2,1,0:T(8,128)(2,1)}, u32[]{:S(2)}, u32[]{:S(2)}) collective-permute-start(bf16[2,1024,256]{2,1,0:T(8,128)(2,1)S(1)} %pad_maximum_fusion.refs_0_), channel_id=1, source_target_pairs={{0,2},{1,3},{2,0},{3,1},{4,6},{5,7},{6,4},{7,5},{8,10},{9,11},{10,... | collective-permute-start | bytes 3145736 | tf_op jit(solution)/shard_map/ppermute | solution.py:440
  154.8 76.6 %collective-permute-start.5 = (bf16[2,1024,256]{2,1,0:T(8,128)(2,1)S(1)}, bf16[2,1024,256]{2,1,0:T(8,128)(2,1)S(1)}, u32[]{:S(2)}, u32[]{:S(2)}) collective-permute-start(bf16[2,1024,256]{2,1,0:T(8,128)(2,1)S(1)} %pad_maximum_fusion.refs_0_), channel_id=1, source_target_pairs={{0,1},{1,0},{2,3},{3,2},{4,5},{5,4},{6,7},{7,6},{8,9},{9,8},{10,11... | collective-permute-start | bytes 3145736 | tf_op jit(solution)/shard_map/ppermute | solution.py:440
  165.8 67.1 %collective-permute-start.11 = (bf16[2,1024,256]{2,1,0:T(8,128)(2,1)}, bf16[2,1024,256]{2,1,0:T(8,128)(2,1)}, u32[]{:S(2)}, u32[]{:S(2)}) collective-permute-start(bf16[2,1024,256]{2,1,0:T(8,128)(2,1)} %pad_maximum_fusion.1.refs_0_), channel_id=1, source_target_pairs={{0,4},{1,5},{2,6},{3,7},{4,0},{5,1},{6,2},{7,3},{8,12},{9,13},{10,... | collective-permute-start | bytes 3145736 | tf_op jit(solution)/shard_map/ppermute | solution.py:440
  250.9 43.1 %collective-permute-start.19 = (bf16[2,1024,256]{2,1,0:T(8,128)(2,1)}, bf16[2,1024,256]{2,1,0:T(8,128)(2,1)}, u32[]{:S(2)}, u32[]{:S(2)}) collective-permute-start(bf16[2,1024,256]{2,1,0:T(8,128)(2,1)} %pad_maximum_fusion.2.refs_0_), channel_id=1, source_target_pairs={{0,1},{1,0},{2,3},{3,2},{4,5},{5,4},{6,7},{7,6},{8,9},{9,8},{10,11... | collective-permute-start | bytes 3145736 | tf_op jit(solution)/shard_map/ppermute | solution.py:440
  258.3 71.3 %collective-permute-start.28 = (bf16[2,2,1024,256]{3,2,1,0:T(8,128)(2,1)}, bf16[2,2,1024,256]{3,2,1,0:T(8,128)(2,1)}, u32[]{:S(2)}, u32[]{:S(2)}) collective-permute-start(bf16[2,2,1024,256]{3,2,1,0:T(8,128)(2,1)} %get-tuple-element.110), channel_id=1, source_target_pairs={{0,1},{1,0},{2,3},{3,2},{4,5},{5,4},{6,7},{7,6},{8,9},{9,8},{10,11... | collective-permute-start | bytes 6291464 | tf_op jit(solution)/shard_map/ppermute | solution.py:440
  276.3 61.4 %collective-permute-start.35 = (bf16[2,2,1024,256]{3,2,1,0:T(8,128)(2,1)}, bf16[2,2,1024,256]{3,2,1,0:T(8,128)(2,1)}, u32[]{:S(2)}, u32[]{:S(2)}) collective-permute-start(bf16[2,2,1024,256]{3,2,1,0:T(8,128)(2,1)} %get-tuple-element.113), channel_id=1, source_target_pairs={{0,1},{1,0},{2,3},{3,2},{4,5},{5,4},{6,7},{7,6},{8,9},{9,8},{10,11... | collective-permute-start | bytes 6291464 | tf_op jit(solution)/shard_map/ppermute | solution.py:440
  320.3 184.0 %collective-permute-start.61 = (bf16[4,512,2048]{2,1,0:T(8,128)(2,1)}, bf16[4,512,2048]{2,1,0:T(8,128)(2,1)}, u32[]{:S(2)}, u32[]{:S(2)}) collective-permute-start(bf16[4,512,2048]{2,1,0:T(8,128)(2,1)} %dynamic-slice_bitcast_fusion), channel_id=1, source_target_pairs={{0,8},{8,0},{1,9},{9,1},{2,10},{10,2},{3,11},{11,3},{4,12},{12,4},... | collective-permute-start | bytes 25165832 | tf_op jit(solution)/shard_map/ppermute | solution.py:479
  341.2 44.7 %collective-permute-start.36 = (bf16[2,1024,256]{2,1,0:T(8,128)(2,1)}, bf16[2,1024,256]{2,1,0:T(8,128)(2,1)}, u32[]{:S(2)}, u32[]{:S(2)}) collective-permute-start(bf16[2,1024,256]{2,1,0:T(8,128)(2,1)} %get-tuple-element.162), channel_id=1, source_target_pairs={{0,4},{1,5},{2,6},{3,7},{4,0},{5,1},{6,2},{7,3},{8,12},{9,13},{10,... | collective-permute-start | bytes 3145736 | tf_op jit(solution)/shard_map/ppermute | solution.py:440
  428.8 45.9 %collective-permute-start.54 = (bf16[2,1024,256]{2,1,0:T(8,128)(2,1)}, bf16[2,1024,256]{2,1,0:T(8,128)(2,1)}, u32[]{:S(2)}, u32[]{:S(2)}) collective-permute-start(bf16[2,1024,256]{2,1,0:T(8,128)(2,1)} %pad_maximum_fusion.7.refs_0_), channel_id=1, source_target_pairs={{0,1},{1,0},{2,3},{3,2},{4,5},{5,4},{6,7},{7,6},{8,9},{9,8},{10,11... | collective-permute-start | bytes 3145736 | tf_op jit(solution)/shard_map/ppermute | solution.py:440
  430.0 44.7 %collective-permute-start.39 = (bf16[2,1024,256]{2,1,0:T(8,128)(2,1)S(1)}, bf16[2,1024,256]{2,1,0:T(8,128)(2,1)}, u32[]{:S(2)}, u32[]{:S(2)}) collective-permute-start(bf16[2,1024,256]{2,1,0:T(8,128)(2,1)S(1)} %pad_maximum_fusion.5.refs_0_), channel_id=1, source_target_pairs={{0,4},{1,5},{2,6},{3,7},{4,0},{5,1},{6,2},{7,3},{8,12},{9,13},{10,... | collective-permute-start | bytes 3145736 | tf_op jit(solution)/shard_map/ppermute | solution.py:440
  442.7 43.7 %collective-permute-start.55 = (bf16[2,1024,256]{2,1,0:T(8,128)(2,1)}, bf16[2,1024,256]{2,1,0:T(8,128)(2,1)}, u32[]{:S(2)}, u32[]{:S(2)}) collective-permute-start(bf16[2,1024,256]{2,1,0:T(8,128)(2,1)} %collective-permute-done.53.refs_1_), channel_id=1, source_target_pairs={{0,1},{1,0},{2,3},{3,2},{4,5},{5,4},{6,7},{7,6},{8,9},{9,8},{10,11... | collective-permute-start | bytes 3145736 | tf_op jit(solution)/shard_map/ppermute | solution.py:440
  453.9 229.8 %collective-permute-start.60 = (bf16[2,4,512,1024]{3,2,1,0:T(8,128)(2,1)}, bf16[2,4,512,1024]{3,2,1,0:T(8,128)(2,1)}, u32[]{:S(2)}, u32[]{:S(2)}) collective-permute-start(bf16[2,4,512,1024]{3,2,1,0:T(8,128)(2,1)} %slice_bitcast_fusion), channel_id=1, source_target_pairs={{0,8},{8,0},{1,9},{9,1},{2,10},{10,2},{3,11},{11,3},{4,12},{12,4},... | collective-permute-start | bytes 25165832 | tf_op jit(solution)/shard_map/ppermute | solution.py:478
  513.8 370.1 %collective-permute-start.62 = (bf16[4,512,2048]{2,1,0:T(8,128)(2,1)}, bf16[4,512,2048]{2,1,0:T(8,128)(2,1)}, u32[]{:S(2)}, u32[]{:S(2)}) collective-permute-start(bf16[4,512,2048]{2,1,0:T(8,128)(2,1)} %collective-permute-done.61.dz_ref.refs_8_), channel_id=1, source_target_pairs={{0,1},{1,0},{2,3},{3,2},{4,5},{5,4},{6,7},{7,6},{8,9},{9,8},{10,11... | collective-permute-start | bytes 25165832 | tf_op jit(solution)/shard_map/ppermute | solution.py:440
  532.7 61.8 %collective-permute-start.85 = (bf16[2,2,1024,256]{3,2,1,0:T(8,128)(2,1)}, bf16[2,2,1024,256]{3,2,1,0:T(8,128)(2,1)}, u32[]{:S(2)}, u32[]{:S(2)}) collective-permute-start(bf16[2,2,1024,256]{3,2,1,0:T(8,128)(2,1)} %get-tuple-element.146), channel_id=1, source_target_pairs={{0,1},{1,0},{2,3},{3,2},{4,5},{5,4},{6,7},{7,6},{8,9},{9,8},{10,11... | collective-permute-start | bytes 6291464 | tf_op jit(solution)/shard_map/ppermute | solution.py:440
  567.9 70.4 %collective-permute-start.78 = (bf16[2,2,1024,256]{3,2,1,0:T(8,128)(2,1)}, bf16[2,2,1024,256]{3,2,1,0:T(8,128)(2,1)}, u32[]{:S(2)}, u32[]{:S(2)}) collective-permute-start(bf16[2,2,1024,256]{3,2,1,0:T(8,128)(2,1)} %get-tuple-element.144), channel_id=1, source_target_pairs={{0,1},{1,0},{2,3},{3,2},{4,5},{5,4},{6,7},{7,6},{8,9},{9,8},{10,11... | collective-permute-start | bytes 6291464 | tf_op jit(solution)/shard_map/ppermute | solution.py:440
  568.3 75.3 %collective-permute-start.71 = (bf16[2,2,1024,256]{3,2,1,0:T(8,128)(2,1)}, bf16[2,2,1024,256]{3,2,1,0:T(8,128)(2,1)}, u32[]{:S(2)}, u32[]{:S(2)}) collective-permute-start(bf16[2,2,1024,256]{3,2,1,0:T(8,128)(2,1)} %get-tuple-element.142), channel_id=1, source_target_pairs={{0,1},{1,0},{2,3},{3,2},{4,5},{5,4},{6,7},{7,6},{8,9},{9,8},{10,11... | collective-permute-start | bytes 6291464 | tf_op jit(solution)/shard_map/ppermute | solution.py:440
  594.6 53.4 %collective-permute-start.64 = (bf16[2,2,1024,256]{3,2,1,0:T(8,128)(2,1)}, bf16[2,2,1024,256]{3,2,1,0:T(8,128)(2,1)}, u32[]{:S(2)}, u32[]{:S(2)}) collective-permute-start(bf16[2,2,1024,256]{3,2,1,0:T(8,128)(2,1)} %get-tuple-element.140), channel_id=1, source_target_pairs={{0,1},{1,0},{2,3},{3,2},{4,5},{5,4},{6,7},{7,6},{8,9},{9,8},{10,11... | collective-permute-start | bytes 6291464 | tf_op jit(solution)/shard_map/ppermute | solution.py:440
  638.3 45.9 %collective-permute-start.86 = (bf16[2,1024,256]{2,1,0:T(8,128)(2,1)S(1)}, bf16[2,1024,256]{2,1,0:T(8,128)(2,1)}, u32[]{:S(2)}, u32[]{:S(2)}) collective-permute-start(bf16[2,1024,256]{2,1,0:T(8,128)(2,1)S(1)} %get-tuple-element.152), channel_id=1, source_target_pairs={{0,4},{1,5},{2,6},{3,7},{4,0},{5,1},{6,2},{7,3},{8,12},{9,13},{10,... | collective-permute-start | bytes 3145736 | tf_op jit(solution)/shard_map/ppermute | solution.py:440
  643.6 129.9 %collective-permute-start.58 = (bf16[4,512,1024]{2,1,0:T(8,128)(2,1)}, bf16[4,512,1024]{2,1,0:T(8,128)(2,1)}, u32[]{:S(2)}, u32[]{:S(2)}) collective-permute-start(bf16[4,512,1024]{2,1,0:T(8,128)(2,1)} %dynamic-slice_bitcast_fusion.1), channel_id=1, source_target_pairs={{0,8},{8,0},{1,9},{9,1},{2,10},{10,2},{3,11},{11,3},{4,12},{12,4},... | collective-permute-start | bytes 12582920 | tf_op jit(solution)/shard_map/ppermute | solution.py:482
  648.0 52.7 %collective-permute-start.79 = (bf16[2,1024,256]{2,1,0:T(8,128)(2,1)}, bf16[2,1024,256]{2,1,0:T(8,128)(2,1)}, u32[]{:S(2)}, u32[]{:S(2)}) collective-permute-start(bf16[2,1024,256]{2,1,0:T(8,128)(2,1)} %get-tuple-element.154), channel_id=1, source_target_pairs={{0,2},{1,3},{2,0},{3,1},{4,6},{5,7},{6,4},{7,5},{8,10},{9,11},{10,... | collective-permute-start | bytes 3145736 | tf_op jit(solution)/shard_map/ppermute | solution.py:440
  700.7 183.3 %collective-permute-start.93 = (f32[1024,1024]{1,0:T(8,128)}, f32[1024,1024]{1,0:T(8,128)}, u32[]{:S(2)}, u32[]{:S(2)}) collective-permute-start(f32[1024,1024]{1,0:T(8,128)} %shard_map.139), channel_id=1, source_target_pairs={{0,8},{8,0},{1,9},{9,1},{2,10},{10,2},{3,11},{11,3},{4,12},{12,4},... | collective-permute-start | bytes 12582920 | tf_op jit(solution)/shard_map/ppermute | solution.py:543
  744.2 119.3 %collective-permute-start.74 = (bf16[1024,256]{1,0:T(8,128)(2,1)S(1)}, bf16[1024,256]{1,0:T(8,128)(2,1)}, u32[]{:S(2)}, u32[]{:S(2)}) collective-permute-start(bf16[1024,256]{1,0:T(8,128)(2,1)S(1)} %fusion.22), channel_id=1, source_target_pairs={{0,2},{1,3},{2,0},{3,1},{4,6},{5,7},{6,4},{7,5},{8,10},{9,11},{10,... | collective-permute-start | bytes 1572872 | tf_op jit(solution)/shard_map/ppermute | solution.py:440
  744.7 118.8 %collective-permute-start.67 = (bf16[1024,256]{1,0:T(8,128)(2,1)S(1)}, bf16[1024,256]{1,0:T(8,128)(2,1)}, u32[]{:S(2)}, u32[]{:S(2)}) collective-permute-start(bf16[1024,256]{1,0:T(8,128)(2,1)S(1)} %fusion.26), channel_id=1, source_target_pairs={{0,4},{1,5},{2,6},{3,7},{4,0},{5,1},{6,2},{7,3},{8,12},{9,13},{10,... | collective-permute-start | bytes 1572872 | tf_op jit(solution)/shard_map/ppermute | solution.py:440
  773.6 89.4 %collective-permute-start.59 = (f32[8]{0:T(128)S(1)}, f32[8]{0:T(128)S(1)}, u32[]{:S(2)}, u32[]{:S(2)}) collective-permute-start(f32[8]{0:T(128)S(1)} %copy-done.58), channel_id=1, source_target_pairs={{0,8},{8,0},{1,9},{9,1},{2,10},{10,2},{3,11},{11,3},{4,12},{12,4},... | collective-permute-start | bytes 104 | tf_op jit(solution)/shard_map/ppermute | solution.py:503
  923.0 101.5 %collective-permute-start.92 = (f32[1024,1024]{1,0:T(8,128)}, f32[1024,1024]{1,0:T(8,128)}, u32[]{:S(2)}, u32[]{:S(2)}) collective-permute-start(f32[1024,1024]{1,0:T(8,128)} %shard_map.138), channel_id=1, source_target_pairs={{0,8},{8,0},{1,9},{9,1},{2,10},{10,2},{3,11},{11,3},{4,12},{12,4},... | collective-permute-start | bytes 12582920 | tf_op jit(solution)/shard_map/ppermute | solution.py:543
  924.7 105.6 %collective-permute-start.63 = (bf16[4,512,1024]{2,1,0:T(8,128)(2,1)}, bf16[4,512,1024]{2,1,0:T(8,128)(2,1)}, u32[]{:S(2)}, u32[]{:S(2)}) collective-permute-start(bf16[4,512,1024]{2,1,0:T(8,128)(2,1)} %collective-permute-done.58.refs_2_), channel_id=1, source_target_pairs={{0,1},{1,0},{2,3},{3,2},{4,5},{5,4},{6,7},{7,6},{8,9},{9,8},{10,11... | collective-permute-start | bytes 12582920 | tf_op jit(solution)/shard_map/ppermute | solution.py:440
  958.4 148.3 %collective-permute-start.57 = (f32[1024,1024]{1,0:T(8,128)}, f32[1024,1024]{1,0:T(8,128)}, u32[]{:S(2)}, u32[]{:S(2)}) collective-permute-start(f32[1024,1024]{1,0:T(8,128)} %shard_map.133), channel_id=1, source_target_pairs={{0,8},{8,0},{1,9},{9,1},{2,10},{10,2},{3,11},{11,3},{4,12},{12,4},... | collective-permute-start | bytes 12582920 | tf_op jit(solution)/shard_map/ppermute | solution.py:543
  959.5 236.6 %collective-permute-start.56 = (f32[1024,1024]{1,0:T(8,128)}, f32[1024,1024]{1,0:T(8,128)}, u32[]{:S(2)}, u32[]{:S(2)}) collective-permute-start(f32[1024,1024]{1,0:T(8,128)} %shard_map.132), channel_id=1, source_target_pairs={{0,8},{8,0},{1,9},{9,1},{2,10},{10,2},{3,11},{11,3},{4,12},{12,4},... | collective-permute-start | bytes 12582920 | tf_op jit(solution)/shard_map/ppermute | solution.py:543
  961.2 47.6 %collective-permute-start.70 = (bf16[2,1024,256]{2,1,0:T(8,128)(2,1)S(1)}, bf16[2,1024,256]{2,1,0:T(8,128)(2,1)}, u32[]{:S(2)}, u32[]{:S(2)}) collective-permute-start(bf16[2,1024,256]{2,1,0:T(8,128)(2,1)S(1)} %collective-permute-done.68.refs_1_), channel_id=1, source_target_pairs={{0,1},{1,0},{2,3},{3,2},{4,5},{5,4},{6,7},{7,6},{8,9},{9,8},{10,11... | collective-permute-start | bytes 3145736 | tf_op jit(solution)/shard_map/ppermute | solution.py:440
  (126 other events, 3084.4 us)
